TPU v7x, 256 devices: a 8x8x2 block of a 8x8x16 slice. The times are simulated.
256 devices in a mesh: ens: 2 (over z), gy: 128 (over x, y, core).
Axes of the slice: x: 8, y: 8, z: 2, core: 2. Of those that a mesh axis runs over, the one named last changes fastest.
The devices are a block of a 8x8x16 slice.
Arguments:
- forcing: float32 [4096, 16384], P(('ens', 'gy')), parts along dimension 0, may hold values from -6 to 6
- east: float32 [2048, 16384], P('gy'), may hold values from 0.5 to 2
- north: float32 [2048, 16384], P('gy'), may hold values from 0.5 to 2
- storage: float32 [2048, 16384], P('gy'), may hold values from 0.05 to 0.5
- coarse_inverse: float32 [64, 16, 16], replicated, as said below
- membership: int32 [32, 256], replicated, may hold values from 0 to 63, as said below
- land: int32 [32, 256], replicated, may hold values 0 or 1
Outputs:
- solution: float32 [4096, 16384], P(('ens', 'gy')), parts along dimension 0
- residual: float32 [4096, 16384], P(('ens', 'gy')), parts along dimension 0
There are 2 independent parts, one for each index of `ens`. A program takes and returns all parts, laid end to end along the dimension named above; an argument that names none is the same for every part. Nothing has to cross between parts.
Inputs may be any that keep to these rules, and one draw needn't show every extreme that they name: `coarse_inverse`: each inverse is symmetric positive definite. `membership`: every basin holds one tile or more.
All inputs are finite; a program needn't handle non-finite values.
Results may differ from a plain program's by a relative error of at most 0.0003.
Values sent between devices are 32-bit elements; how exact they have to be, the bound alone decides.
No kernel may reach another device: no remote copies, remote signals or barrier semaphores. Data moves between devices by JAX's collectives and lax.ppermute only.
A program may use at most 64 MiB of HBM per device.

v0:
```python
import functools

import jax
import jax.numpy as jnp
from jax import lax
from jax.sharding import Mesh
from jax.sharding import PartitionSpec as P

TILE = 64
ORDER = 4
ITERS = 2
GY = ("gy_0", "gy_1", "gy_2")
ENS_GY = ("ens", "gy_0", "gy_1", "gy_2")


HIGHEST = lax.Precision.HIGHEST


def shifted(block, axis, distance):
    devices = range(lax.axis_size(axis))
    route = [(i - distance, i) for i in devices if i - distance in devices]
    return lax.ppermute(block, axis, route)


def padded_2(shard, sides, width):
    for axis, dim in sides:
        devices, length = (lax.axis_size(axis), shard.shape[dim])
        up = [(i, (i + 1) % devices) for i in range(devices - 1)]
        down = [(j, i) for i, j in up]
        last = lax.slice_in_dim(shard, length - width, length, axis=dim)
        leading = lax.slice_in_dim(shard, 0, width, axis=dim)
        before = lax.ppermute(last, axis, up)
        after = lax.ppermute(leading, axis, down)
        shard = jnp.concatenate([before, shard, after], axis=dim)
    return shard


def by_axis(shard, axes):
    return functools.reduce(lax.psum, axes, shard)


def body(forcing, east, north, storage, coarse_inverse, membership, land):
    rows, width = forcing.shape
    index = lax.axis_index(GY)
    start = index * rows
    basins = coarse_inverse.shape[0]
    coarse = coarse_inverse.shape[1]
    tile = TILE
    order = ORDER
    tiles_x = width // tile
    tile_rows = membership.shape[0]
    total_rows = tile_rows * tile
    row_ids = start + jnp.arange(rows + 1, dtype=jnp.int32)
    tile_of_row = jnp.minimum(row_ids // tile, tile_rows - 1)
    picker = (tile_of_row[:, None] == jnp.arange(tile_rows, dtype=jnp.int32)[None, :]).astype(
        jnp.float32
    )
    land_rows = jnp.dot(picker, land.astype(jnp.float32), precision=HIGHEST)
    inside = (row_ids < total_rows).astype(jnp.float32)
    wet_rows = jnp.repeat((1.0 - land_rows) * inside[:, None], tile, axis=1)
    wet = wet_rows[:rows]
    above = wet_rows[1:]
    east_face = east * wet * jnp.roll(wet, -1, axis=1)
    north_face = north * wet * above
    lower = shifted(north_face[rows - 1 :], GY, 1)
    south_face = jnp.concatenate([lower, north_face[:-1]], axis=0)
    west_face = jnp.roll(east_face, 1, axis=1)
    center = 1.0 - wet + wet * storage + east_face + west_face + north_face + south_face
    jacobi = 1.0 / center
    degree = jnp.arange(order).astype(jnp.float32)
    local_rows = (start % tile + jnp.arange(rows, dtype=jnp.int32)).astype(jnp.float32)
    row_modes = jnp.cos(jnp.pi * degree[:, None] * (local_rows[None, :] + 0.5) / tile)
    local_cols = (jnp.arange(width, dtype=jnp.int32) % tile).astype(jnp.float32)
    col_modes = jnp.cos(jnp.pi * degree[:, None] * (local_cols[None, :] + 0.5) / tile)
    my_basins = lax.dynamic_slice_in_dim(membership, start // tile, 1, 0)[0]
    owned = (my_basins[:, None] == jnp.arange(basins, dtype=jnp.int32)[None, :]).astype(jnp.float32)

    def operate(field):
        padded = padded_2(field, ((GY, 0),), 1)
        return (
            center * field
            - east_face * jnp.roll(field, -1, axis=1)
            - west_face * jnp.roll(field, 1, axis=1)
            - north_face * padded[2:]
            - south_face * padded[:-2]
        )

    def moments(field):
        lifted = jnp.dot(row_modes, wet * field, precision=HIGHEST)
        product = (lifted[:, None, :] * col_modes[None, :, :]).reshape(coarse, tiles_x, tile)
        per_tile = jnp.sum(product, axis=2)
        return jnp.dot(per_tile, owned, precision=HIGHEST).T

    def spread(coef):
        per_tile = jnp.dot(owned, coef, precision=HIGHEST)
        per_col = jnp.repeat(per_tile.T, tile, axis=1).reshape(order, order, width)
        lifted = jnp.sum(per_col * col_modes[None, :, :], axis=1)
        return wet * jnp.dot(row_modes.T, lifted, precision=HIGHEST)

    def reduce_coarse(partial_value, dots):
        return (by_axis(partial_value, GY), by_axis(dots, GY))

    def expand(held_g):
        held_c = jnp.einsum("nij,nj->ni", coarse_inverse, held_g, precision=HIGHEST)
        return (held_c, jnp.sum(held_g * held_c))

    solution = jnp.zeros_like(forcing)
    residual = forcing
    smoothed = jacobi * residual
    held_g, dots = reduce_coarse(moments(residual), jnp.stack([jnp.sum(residual * smoothed)]))
    full_c, coarse_dot = expand(held_g)
    precond = smoothed + spread(full_c)
    energy = dots[0] + coarse_dot
    direction = precond
    image = operate(precond)
    held_s, dots = reduce_coarse(moments(image), jnp.stack([jnp.sum(image * precond)]))
    alpha = energy / dots[0]
    along = image
    for step in range(ITERS):
        solution = solution + alpha * direction
        residual = residual - alpha * along
        if step + 1 < ITERS:
            held_g = held_g - alpha * held_s
            smoothed = jacobi * residual
            full_c, coarse_dot = expand(held_g)
            precond = smoothed + spread(full_c)
            image = operate(precond)
            held_w, dots = reduce_coarse(
                moments(image), jnp.stack([jnp.sum(residual * smoothed), jnp.sum(image * precond)])
            )
            energy_next = dots[0] + coarse_dot
            beta = energy_next / energy
            alpha = energy_next / (dots[1] - beta * energy_next / alpha)
            direction = precond + beta * direction
            along = image + beta * along
            held_s = held_w + beta * held_s
            energy = energy_next
    return (solution, residual)


def solution(mesh):
    finer = Mesh(mesh.devices.reshape(mesh.shape["ens"], 8, 8, 2), ("ens", "gy_0", "gy_1", "gy_2"))
    return jax.shard_map(
        body,
        mesh=finer,
        in_specs=(P(ENS_GY, None), P(GY, None), P(GY, None), P(GY, None), P(), P(), P()),
        out_specs=(P(ENS_GY, None), P(ENS_GY, None)),
        check_vma=False,
    )
```

profile of v0, /device:TPU:513, one launch (start us, length us, event | category | flops | bytes accessed | tf_op | source)
XLA Modules:
  0.0 215.0 jit_solution(15899413752547063470)
XLA Ops:
  6.5 2.4 %maximum_multiply_fusion = (f32[16,16384]{1,0:T(8,128)S(1)}, f32[16,16384]{1,0:T(8,128)S(1)}) fusion(f32[16,1]{1,0:T(8,128)S(1)} %slice.124, f32[16,16383]{1,0:T(8,128)} %slice.123, f32[16,16384]{1,0:T(8,128)} %param.8, f32[16,16384]{1,0:T(8,128)S(1)} %slice.95, f32[16,16384]{1,0:T(8,128)} %slice.101, f32[16,16384]{1,0:T(8,128)} %param.9), kind=kLoop, calls=%fused_computation.18 | loop fusion | flops 1310720 | bytes 7340032 | tf_op jit(solution)/shard_map/mul | solution.py:63
  9.6 5.7 %collective-permute-start = (f32[1,16384]{1,0:T(1,128)}, f32[1,16384]{1,0:T(1,128)S(1)}, u32[]{:S(2)}, u32[]{:S(2)}) collective-permute-start(f32[1,16384]{1,0:T(1,128)} %slice.128), channel_id=1, source_target_pairs={{0,1},{1,2},{2,3},{3,4},{4,5},{5,6},{6,7},{7,8},{8,9},{9,10},{10,1... | collective-permute-start | bytes 196616 | tf_op jit(solution)/shard_map/ppermute | solution.py:22
  16.0 2.6 %multiply_cosine_fusion = f32[4,16384]{1,0:T(4,128)S(1)} fusion(f32[16384]{0:T(1024)} %fusion.24, f32[4]{0:T(128)S(1)} %convert_multiply_fusion), kind=kLoop, calls=%fused_computation.47 | loop fusion | flops 131072 | bytes 327696 | tf_op jit(solution)/shard_map/cos | solution.py:74
  21.8 3.2 %mul.275 = f32[16,256,64]{2,1,0:T(8,128)} reshape(f32[4,4,16384]{2,1,0:T(4,128)} %broadcast_multiply_fusion.1) | data formatting | bytes 2097152 | tf_op jit(solution)/shard_map/mul | solution.py:90
  27.4 14.5 %psum.108 = f32[64,16]{0,1:T(8,128)S(1)} all-reduce(f32[64,16]{0,1:T(8,128)S(1)} %fusion.22), channel_id=1, replica_groups=mesh['ens'=2,'gy_0'=8,'gy_1'=8,'gy_2'=2] {'gy_0'}, use_global_device_ids=true, to_apply=%region_5.6 | all-reduce | flops 1024 | bytes 8192 | tf_op jit(solution)/shard_map/psum | solution.py:39
  41.9 19.1 %psum.109 = f32[64,16]{0,1:T(8,128)S(1)} all-reduce(f32[64,16]{0,1:T(8,128)S(1)} %psum.108), channel_id=1, replica_groups=mesh['ens'=2,'gy_0'=8,'gy_1'=8,'gy_2'=2] {'gy_1'}, use_global_device_ids=true, to_apply=%region_6.7 | all-reduce | flops 1024 | bytes 8192 | tf_op jit(solution)/shard_map/psum | solution.py:39
  61.1 13.5 %psum.110 = f32[64,16]{0,1:T(8,128)S(1)} all-reduce(f32[64,16]{0,1:T(8,128)S(1)} %psum.109), channel_id=1, replica_groups=mesh['ens'=2,'gy_0'=8,'gy_1'=8,'gy_2'=2] {'gy_2'}, use_global_device_ids=true, to_apply=%region_7.8 | all-reduce | flops 1024 | bytes 8192 | tf_op jit(solution)/shard_map/psum | solution.py:39
  77.8 3.0 %reshape_reshape.6 = f32[4,4,16384]{2,1,0:T(4,128)} reshape(f32[16,256,64]{2,1,0:T(8,128)} %broadcast_in_dim.10) | data formatting | bytes 2097152 | tf_op jit(solution)/shard_map/reshape;reshape | solution.py:96
  83.6 2.4 %multiply_reduce_fusion.5 = (f32[]{:T(128)}, f32[16,16384]{1,0:T(8,128)S(1)}) fusion(f32[16,16384]{1,0:T(8,128)S(1)} %copy-done.1, f32[15,16384]{1,0:T(8,128)S(1)} %bitcast.21, f32[1,16384]{1,0:T(1,128)S(1)} %collective-permute-done, f32[16,16384]{1,0:T(8,128)S(1)} %get-tuple-element.31, f32[16,16383]{1,0:T(8,128)S(1)} %bitcast.24, f32[16,1]{1,0:T(8,128)S(1)} %slice.125, ...), kind=kLoop, calls=%fused_computation.41 | loop fusion | flops 3407871 | bytes 8388612 | tf_op jit(solution)/shard_map/reduce_sum | solution.py:110
  87.8 2.3 %collective-permute-start.1 = (f32[1,16384]{1,0:T(1,128)S(1)}, f32[1,16384]{1,0:T(1,128)S(1)}, u32[]{:S(2)}, u32[]{:S(2)}) collective-permute-start(f32[1,16384]{1,0:T(1,128)S(1)} %get-tuple-element.28), channel_id=1, source_target_pairs={{1,0},{2,1},{3,2},{4,3},{5,4},{6,5},{7,6},{8,7},{9,8},{10,9},{11,1... | collective-permute-start | bytes 196616 | tf_op jit(solution)/shard_map/ppermute | solution.py:33
  90.1 3.7 %collective-permute-start.2 = (f32[1,16384]{1,0:T(1,128)S(1)}, f32[1,16384]{1,0:T(1,128)S(1)}, u32[]{:S(2)}, u32[]{:S(2)}) collective-permute-start(f32[1,16384]{1,0:T(1,128)S(1)} %get-tuple-element.29), channel_id=1, source_target_pairs={{0,1},{1,2},{2,3},{3,4},{4,5},{5,6},{6,7},{7,8},{8,9},{9,10},{10,1... | collective-permute-start | bytes 196616 | tf_op jit(solution)/shard_map/ppermute | solution.py:32
  99.4 3.2 %mul.294 = f32[16,256,64]{2,1,0:T(8,128)} reshape(f32[4,4,16384]{2,1,0:T(4,128)} %broadcast_multiply_fusion) | data formatting | bytes 2097152 | tf_op jit(solution)/shard_map/mul | solution.py:90
  105.8 13.5 %all-reduce.1 = (f32[64,16]{0,1:T(8,128)S(1)}, f32[1]{0:T(128)}, f32[1]{0:T(128)}) all-reduce(f32[64,16]{0,1:T(8,128)S(1)} %fusion.20, f32[1]{0:T(128)} %bitcast.2, f32[1]{0:T(128)} %bitcast.5), channel_id=1, replica_groups=mesh['ens'=2,'gy_0'=8,'gy_1'=8,'gy_2'=2] {'gy_0'}, use_global_device_ids=true, to_apply=%region_16.17 | all-reduce | flops 1026 | bytes 8208 | tf_op jit(solution)/shard_map/psum | solution.py:39
  119.3 15.3 %all-reduce = (f32[64,16]{0,1:T(8,128)S(1)}, f32[1]{0:T(128)}, f32[1]{0:T(128)}) all-reduce(f32[64,16]{0,1:T(8,128)S(1)} %get-tuple-element.5, f32[1]{0:T(128)} %get-tuple-element.6, f32[1]{0:T(128)} %get-tuple-element.7), channel_id=1, replica_groups=mesh['ens'=2,'gy_0'=8,'gy_1'=8,'gy_2'=2] {'gy_1'}, use_global_device_ids=true, to_apply=%region_17.18 | all-reduce | flops 1026 | bytes 8208 | tf_op jit(solution)/shard_map/psum | solution.py:39
  134.6 10.5 %all-reduce.2 = (f32[64,16]{0,1:T(8,128)S(1)}, f32[]{:T(128)}, f32[]{:T(128)}) all-reduce(f32[64,16]{0,1:T(8,128)S(1)} %get-tuple-element.2, f32[]{:T(128)} %bitcast.3, f32[]{:T(128)} %bitcast.6), channel_id=1, replica_groups=mesh['ens'=2,'gy_0'=8,'gy_1'=8,'gy_2'=2] {'gy_2'}, use_global_device_ids=true, to_apply=%region_18.19 | all-reduce | flops 1026 | bytes 8208 | tf_op jit(solution)/shard_map/psum | solution.py:39
  150.9 3.0 %reshape_reshape.7 = f32[4,4,16384]{2,1,0:T(4,128)} reshape(f32[16,256,64]{2,1,0:T(8,128)} %broadcast_in_dim.11) | data formatting | bytes 2097152 | tf_op jit(solution)/shard_map/reshape;reshape | solution.py:96
  156.0 2.9 %fusion = f32[16,16384]{1,0:T(8,128)S(1)} fusion(f32[16,16384]{1,0:T(8,128)S(1)} %slice.95, f32[4,16384]{1,0:T(4,128)S(1)} %multiply_reduce_fusion.1, f32[16,16384]{1,0:T(8,128)S(1)} %copy-done.2, f32[16,16384]{1,0:T(8,128)} %copy-done.8, f32[]{:T(128)S(6)} %div.65, f32[16]{0:T(128)S(1)} %convert_add_fusion, f32[4]{0:T(128)S(1)} %convert_multiply_fusion, ...), kind=kOutput, calls=%fused_computation.1 | convolution fusion | flops 14155904 | bytes 5505108 | tf_op jit(solution)/shard_map/dot_general | solution.py:98
  159.3 2.4 %collective-permute-start.3 = (f32[1,16384]{1,0:T(1,128)S(1)}, f32[1,16384]{1,0:T(1,128)S(1)}, u32[]{:S(2)}, u32[]{:S(2)}) collective-permute-start(f32[1,16384]{1,0:T(1,128)S(1)} %get-tuple-element.22), channel_id=1, source_target_pairs={{1,0},{2,1},{3,2},{4,3},{5,4},{6,5},{7,6},{8,7},{9,8},{10,9},{11,1... | collective-permute-start | bytes 196616 | tf_op jit(solution)/shard_map/ppermute | solution.py:33
  161.7 3.5 %collective-permute-start.4 = (f32[1,16384]{1,0:T(1,128)S(1)}, f32[1,16384]{1,0:T(1,128)S(1)}, u32[]{:S(2)}, u32[]{:S(2)}) collective-permute-start(f32[1,16384]{1,0:T(1,128)S(1)} %get-tuple-element.23), channel_id=1, source_target_pairs={{0,1},{1,2},{2,3},{3,4},{4,5},{5,6},{6,7},{7,8},{8,9},{9,10},{10,1... | collective-permute-start | bytes 196616 | tf_op jit(solution)/shard_map/ppermute | solution.py:32
  166.6 2.7 %multiply_reduce_fusion = (f32[]{:T(128)}, f32[16,16384]{1,0:T(8,128)}, f32[]{:T(128)}) fusion(f32[16,16384]{1,0:T(8,128)S(1)} %fusion, f32[1,16384]{1,0:T(1,128)S(1)} %collective-permute-done.4, f32[15,16384]{1,0:T(8,128)S(1)} %bitcast.23, f32[1,16384]{1,0:T(1,128)S(1)} %collective-permute-done, f32[16,16384]{1,0:T(8,128)S(1)} %get-tuple-element.31, ...), kind=kLoop, calls=%fused_computation.31 | loop fusion | flops 6029310 | bytes 11665420 | tf_op jit(solution)/shard_map/reduce_sum | solution.py:129
  170.6 12.6 %psum.117 = f32[2]{0:T(128)S(1)} all-reduce(f32[2]{0:T(128)S(1)} %pad_maximum_fusion.6), channel_id=1, replica_groups=mesh['ens'=2,'gy_0'=8,'gy_1'=8,'gy_2'=2] {'gy_0'}, use_global_device_ids=true, to_apply=%region_21.22 | all-reduce | flops 2 | bytes 16 | tf_op jit(solution)/shard_map/psum | solution.py:39
  183.2 14.4 %psum.118 = f32[2]{0:T(128)S(1)} all-reduce(f32[2]{0:T(128)S(1)} %psum.117), channel_id=1, replica_groups=mesh['ens'=2,'gy_0'=8,'gy_1'=8,'gy_2'=2] {'gy_1'}, use_global_device_ids=true, to_apply=%region_22.23 | all-reduce | flops 2 | bytes 16 | tf_op jit(solution)/shard_map/psum | solution.py:39
  198.2 9.6 %psum.119 = f32[2]{0:T(128)S(1)} all-reduce(f32[2]{0:T(128)S(1)} %psum.118), channel_id=1, replica_groups=mesh['ens'=2,'gy_0'=8,'gy_1'=8,'gy_2'=2] {'gy_2'}, use_global_device_ids=true, to_apply=%region_23.24 | all-reduce | flops 2 | bytes 16 | tf_op jit(solution)/shard_map/psum | solution.py:39
  211.1 3.9 %multiply_subtract_fusion = (f32[16,16384]{1,0:T(8,128)}, f32[16,16384]{1,0:T(8,128)}) fusion(f32[16,16384]{1,0:T(8,128)} %get-tuple-element.12, f32[16,16384]{1,0:T(8,128)} %copy-done.8, f32[]{:T(128)S(6)} %div.66, f32[]{:T(128)S(6)} %div.68, f32[16,16384]{1,0:T(8,128)S(1)} %copy-done.3, f32[]{:T(128)S(6)} %div.65, f32[16,16384]{1,0:T(8,128)} %copy-done.5, ...), kind=kLoop, calls=%fused_computation.29 | loop fusion | flops 2883584 | bytes 7340044 | tf_op jit(solution)/shard_map/sub | solution.py:121
  (72 shorter events, 39.3 us)
Async XLA Ops:
  0.6 24.4 %copy-start = (s32[32,256]{1,0:T(8,128)S(1)}, s32[32,256]{1,0:T(8,128)}, u32[]{:S(2)}) copy-start(s32[32,256]{1,0:T(8,128)} %param.12) | copy-start | bytes 98308
  9.6 74.0 %collective-permute-start = (f32[1,16384]{1,0:T(1,128)}, f32[1,16384]{1,0:T(1,128)S(1)}, u32[]{:S(2)}, u32[]{:S(2)}) collective-permute-start(f32[1,16384]{1,0:T(1,128)} %slice.128), channel_id=1, source_target_pairs={{0,1},{1,2},{2,3},{3,4},{4,5},{5,6},{6,7},{7,8},{8,9},{9,10},{10,1... | collective-permute-start | bytes 196616 | tf_op jit(solution)/shard_map/ppermute | solution.py:22
  25.0 52.8 %copy-start.10 = (s32[1,256]{1,0:T(1,128)}, s32[1,256]{1,0:T(1,128)S(1)}, u32[]{:S(2)}) copy-start(s32[1,256]{1,0:T(1,128)S(1)} %constant_dynamic-slice_fusion) | copy-start | bytes 3076
  80.9 2.7 %copy-start.1 = (f32[16,16384]{1,0:T(8,128)S(1)}, f32[16,16384]{1,0:T(8,128)}, u32[]{:S(2)}) copy-start(f32[16,16384]{1,0:T(8,128)} %param.7) | copy-start | bytes 3145732
  86.0 8.9 %copy-start.6 = (f32[16,16384]{1,0:T(8,128)}, f32[16,16384]{1,0:T(8,128)S(1)}, u32[]{:S(2)}) copy-start(f32[16,16384]{1,0:T(8,128)S(1)} %get-tuple-element.16) | copy-start | bytes 3145732
  87.4 7.6 %copy-start.4 = (f32[16,16384]{1,0:T(8,128)}, f32[16,16384]{1,0:T(8,128)S(1)}, u32[]{:S(2)}) copy-start(f32[16,16384]{1,0:T(8,128)S(1)} %fusion.1) | copy-start | bytes 3145732
  87.8 6.1 %collective-permute-start.1 = (f32[1,16384]{1,0:T(1,128)S(1)}, f32[1,16384]{1,0:T(1,128)S(1)}, u32[]{:S(2)}, u32[]{:S(2)}) collective-permute-start(f32[1,16384]{1,0:T(1,128)S(1)} %get-tuple-element.28), channel_id=1, source_target_pairs={{1,0},{2,1},{3,2},{4,3},{5,4},{6,5},{7,6},{8,7},{9,8},{10,9},{11,1... | collective-permute-start | bytes 196616 | tf_op jit(solution)/shard_map/ppermute | solution.py:33
  90.1 4.9 %collective-permute-start.2 = (f32[1,16384]{1,0:T(1,128)S(1)}, f32[1,16384]{1,0:T(1,128)S(1)}, u32[]{:S(2)}, u32[]{:S(2)}) collective-permute-start(f32[1,16384]{1,0:T(1,128)S(1)} %get-tuple-element.29), channel_id=1, source_target_pairs={{0,1},{1,2},{2,3},{3,4},{4,5},{5,6},{6,7},{7,8},{8,9},{9,10},{10,1... | collective-permute-start | bytes 196616 | tf_op jit(solution)/shard_map/ppermute | solution.py:32
  96.6 1.0 copy-start.8
  153.9 2.1 copy-start.2
  158.8 7.7 %copy-start.5 = (f32[16,16384]{1,0:T(8,128)}, f32[16,16384]{1,0:T(8,128)S(1)}, u32[]{:S(2)}) copy-start(f32[16,16384]{1,0:T(8,128)S(1)} %fusion) | copy-start | bytes 3145732
  158.9 7.6 %copy-start.7 = (f32[16,16384]{1,0:T(8,128)S(1)}, f32[16,16384]{1,0:T(8,128)}, u32[]{:S(2)}) copy-start(f32[16,16384]{1,0:T(8,128)} %copy-done.6) | copy-start | bytes 3145732
  159.0 7.6 %copy-start.9 = (f32[16,16384]{1,0:T(8,128)S(1)}, f32[16,16384]{1,0:T(8,128)}, u32[]{:S(2)}) copy-start(f32[16,16384]{1,0:T(8,128)} %copy-done.8) | copy-start | bytes 3145732
  159.3 6.0 %collective-permute-start.3 = (f32[1,16384]{1,0:T(1,128)S(1)}, f32[1,16384]{1,0:T(1,128)S(1)}, u32[]{:S(2)}, u32[]{:S(2)}) collective-permute-start(f32[1,16384]{1,0:T(1,128)S(1)} %get-tuple-element.22), channel_id=1, source_target_pairs={{1,0},{2,1},{3,2},{4,3},{5,4},{6,5},{7,6},{8,7},{9,8},{10,9},{11,1... | collective-permute-start | bytes 196616 | tf_op jit(solution)/shard_map/ppermute | solution.py:33
  161.7 4.9 %collective-permute-start.4 = (f32[1,16384]{1,0:T(1,128)S(1)}, f32[1,16384]{1,0:T(1,128)S(1)}, u32[]{:S(2)}, u32[]{:S(2)}) collective-permute-start(f32[1,16384]{1,0:T(1,128)S(1)} %get-tuple-element.23), channel_id=1, source_target_pairs={{0,1},{1,2},{2,3},{3,4},{4,5},{5,6},{6,7},{7,8},{8,9},{9,10},{10,1... | collective-permute-start | bytes 196616 | tf_op jit(solution)/shard_map/ppermute | solution.py:32
  166.6 44.5 %copy-start.3 = (f32[16,16384]{1,0:T(8,128)S(1)}, f32[16,16384]{1,0:T(8,128)}, u32[]{:S(2)}) copy-start(f32[16,16384]{1,0:T(8,128)} %param.7) | copy-start | bytes 3145732
where the time goes:
time: 216 us; the launch traced here: 215 us
  blocking collectives  123 us (57%)
  other arithmetic  31.6 us (15%)
  local copies, waits for them, and re-layouts  24.8 us (11%)
  starting transfers between devices  17.7 us (8%)
  matrix products  9.99 us (5%)
  between operations  5.55 us (3%)
  waiting for transfers between devices  2.29 us (1%)
    psum x9, blocking collectives, by_axis(): return functools.reduce(lax.psum, axes, shard)  123 us
    ppermute x2, starting transfers between devices, padded_2(): before = lax.ppermute(last, axis, up)  7.25 us
    mul x2, local copies, waits for them, and re-layouts, moments(): lifted[:, None, :] * col_modes[None, :, :]  6.46 us
    another operation x2, local copies, waits for them, and re-layouts, spread(): per_col = jnp.repeat(per_tile.T, tile, axis=1).reshape(order, order, width)  6.05 us
    ppermute x1, starting transfers between devices, shifted(): return lax.ppermute(block, axis, route)  5.73 us
    ppermute x2, starting transfers between devices, padded_2(): after = lax.ppermute(leading, axis, down)  4.7 us
    reduce_sum x2, other arithmetic, moments(): per_tile = jnp.sum(product, axis=2)  4.4 us
  transfers between devices with their start and end apart: 5, of which 2 were waited for; matrix products, arithmetic and copies ran while one was open for 10% of the time, Pallas kernels for 0%

commit v1 on v0

v1 whole, which is shorter than its diff:
```python
import jax
import jax.numpy as jnp
import numpy as np
from jax import lax
from jax.experimental import pallas as pl
from jax.experimental.pallas import tpu as pltpu
from jax.sharding import Mesh
from jax.sharding import PartitionSpec as P

TILE = 64
ORDER = 4
GY = ("gy_0", "gy_1", "gy_2")
ENS_GY = ("ens", "gy_0", "gy_1", "gy_2")
F32, BF16, I32 = jnp.float32, jnp.bfloat16, jnp.int32
STEP = 16
PIECE = 8
BLOCK = 32


def tables():
    degree = np.arange(ORDER)[:, None]
    mode = np.cos(np.pi * degree * (np.arange(TILE)[None, :] + 0.5) / TILE)
    p_of = np.tile(np.repeat(np.arange(ORDER), ORDER), 2)
    q_of = np.tile(np.arange(ORDER), 2 * ORDER)
    half = np.repeat(np.arange(2), ORDER * ORDER)
    lane = np.arange(128)
    cols = (mode[q_of][:, lane % TILE] * (half[:, None] == lane[None, :] // TILE)).astype(np.float32)
    high = cols.astype(BF16)
    low = (cols - high.astype(np.float32)).astype(BF16)
    gather = np.concatenate([high, low], axis=0)
    scatter = np.concatenate([high, high, low, np.zeros_like(low)], axis=0)
    rows = mode[p_of].reshape(32, 8, 8).transpose(1, 0, 2).astype(np.float32)
    row_lanes = np.tile(rows, (1, 1, 16))
    row_subs = np.tile(rows.transpose(0, 2, 1), (1, 1, 4))
    ends = np.zeros((TILE // 16, 8, 128), np.float32)
    for k in range(TILE // 16):
        ends[k] = row_subs[(2 * k - 1) % 8, 7]
        ends[k, 0] = row_subs[(2 * k + 2) % 8, 0]
    return gather, scatter, row_lanes, row_subs, ends


def iotas(n):
    return lax.broadcasted_iota(I32, (n, 8, 128), 1), lax.broadcasted_iota(I32, (n, 8, 128), 2)


def onehot(left, right):
    lane = lax.broadcasted_iota(I32, (8, 128), 1)
    return jnp.where(jnp.where(lane < TILE, left, right) == lane % TILE, 1.0, 0.0)


def dot_nt(a, b):
    return lax.dot_general(a, b, (((1,), (1,)), ((), ())), preferred_element_type=F32)


def dot_nn(a, b):
    return lax.dot_general(a, b, (((1,), (0,)), ((), ())), preferred_element_type=F32)


def split(x):
    high = x.astype(BF16)
    return high, (x - high.astype(F32)).astype(BF16)


def moments(field, own, gather, row_lanes, block):
    lanes = [jnp.concatenate([row_lanes[block + r]] * (BLOCK * 8 // 128), axis=1) for r in range(2)]

    def step(k, total):
        first = pl.multiple_of(k * BLOCK, BLOCK)
        lifted = jnp.zeros((32, BLOCK * 8), F32)
        for r in range(2):
            high, low = split(field[r, pl.ds(first, BLOCK)].reshape(BLOCK * 8, 128))
            both = dot_nt(gather[...], high)
            lifted = lifted + lanes[r] * (both[:32] + both[32:] + dot_nt(gather[0:32], low))
        parts = dot_nn(jnp.concatenate(split(lifted), axis=0), own[pl.ds(first * 8, BLOCK * 8)])
        return total + parts[:32] + parts[32:]

    total = lax.fori_loop(0, field.shape[1] // BLOCK, step, jnp.zeros((32, 128), F32))
    sums = total[:16] + pltpu.roll(total[16:], TILE, 1)
    lane = lax.broadcasted_iota(I32, (8, 128), 1)
    return jnp.where(lane < TILE, sums[:8], pltpu.roll(sums[8:], TILE, 1))


def unpack(tile):
    return jnp.concatenate([tile, pltpu.roll(tile, TILE, 1)], axis=0)[:, :TILE]


def coarse_solve(inverse, sums):
    coef = jnp.zeros_like(sums)
    for j in range(sums.shape[0]):
        coef = coef + inverse[j] * sums[j : j + 1]
    return coef


def total_of(x):
    return jnp.sum(jnp.sum(x, axis=1, keepdims=True), axis=0, keepdims=True)


def spreader(coef, scatter, row_subs, ends, block):
    zero = jnp.zeros_like(coef)
    rows = [jnp.concatenate([coef, zero], axis=1), jnp.concatenate([zero, coef], axis=1)]
    high, low = split(jnp.concatenate(rows * 4, axis=0))
    patterns = [row_subs[block], row_subs[block + 1], ends[block // 2]]
    lane = lax.broadcasted_iota(I32, (1, 8, 128), 2)
    middle = (lane >= 32) & (lane < 64)

    def spread(own, ids):
        per_tile = (dot_nt(own, high) + dot_nt(own, low)).reshape(-1, 8, 128)
        result = []
        for r in ids:
            scaled = per_tile * patterns[r][None]
            rounded = scaled.astype(BF16).astype(F32)
            pieces = jnp.where(middle, scaled - rounded, rounded).astype(BF16)
            result.append(dot_nn(pieces.reshape(-1, 128), scatter[...]).reshape(-1, 8, 128))
        return result

    return spread


def first_kernel(codes, info, forcing, east, north, storage, gather, row_lanes,
                 east_o, north_o, center_o, own_o, own_end_o, sums_o, down_o, up_o):
    chunks = forcing.shape[1]
    basins = TILE
    lane = lax.broadcasted_iota(I32, (8, 128), 1)
    sub = lax.broadcasted_iota(I32, (8, 128), 0)

    def wet_of(code):
        return jnp.where(code < basins, 1.0, 0.0)

    def east_of(c):
        left, right = codes[0, 2 * c], codes[0, 2 * c + 1]
        after = codes[0, lax.rem(2 * c + 2, 2 * chunks)]
        wet = wet_of(jnp.where(lane < TILE, left, right))
        other = wet_of(jnp.where(lane < TILE - 1, left, jnp.where(lane < 127, right, after)))
        mask = wet * other
        return wet, [east[r, c] * mask for r in range(2)]

    def rolled(pair):
        return [pltpu.roll(x, 1, 1) for x in pair]

    last = east_of(chunks - 1)[1]
    for r in range(2):
        east_o[r, 0] = last[r]

    def pair_step(k, carry):
        owns, owns_end = [], []
        for j in range(2):
            c = 2 * k + j
            wet, face = east_of(c)
            up = wet_of(jnp.where(lane < TILE, codes[1, 2 * c], codes[1, 2 * c + 1]))
            turned = rolled(face)
            west = [jnp.where(lane == 0, carry[r], turned[r]) for r in range(2)]
            norths = [north[0, c] * wet, north[1, c] * jnp.where(sub < 7, wet, wet * up)]
            shifted = [pltpu.roll(x, 1, 0) for x in norths]
            south = [jnp.where(sub == 0, 0.0, shifted[0]), jnp.where(sub == 0, shifted[0], shifted[1])]
            for r in range(2):
                center = (1.0 - wet) + wet * storage[r, c] + face[r] + west[r] + norths[r] + south[r]
                east_o[r, c + 1] = face[r]
                north_o[r, c] = norths[r]
                center_o[r, c] = center
                if r == 0:
                    down_o[0, c] = forcing[0, c, 0:1]
                    down_o[1, c] = center[0:1]
                else:
                    up_o[0, c] = forcing[1, c, 7:8]
                    up_o[1, c] = center[7:8]
                    up_o[2, c] = norths[1][7:8]
            owns.append(onehot(codes[0, 2 * c], codes[0, 2 * c + 1]))
            owns_end.append(onehot(*[jnp.where(sub == 0, codes[1, 2 * c + i], codes[2, 2 * c + i]) for i in range(2)]))
            carry = turned
        own_o[pl.ds(pl.multiple_of(k * 16, 16), 16)] = jnp.concatenate(owns, axis=0).astype(BF16)
        own_end_o[pl.ds(pl.multiple_of(k * 16, 16), 16)] = jnp.concatenate(owns_end, axis=0).astype(BF16)
        return carry

    lax.fori_loop(0, chunks // 2, pair_step, rolled(last), unroll=2)
    tile = moments(forcing, own_o, gather, row_lanes, info[0])
    sums_o[...] = jnp.broadcast_to(tile[None], sums_o.shape)


def ends_of(from_up, from_down):
    sub = iotas(from_up.shape[0])[0]
    return jnp.where(sub == 0, from_up, from_down)


def apply_operator(z_pad, east, north, center, from_down, out, down_o, up_o):
    chunks = north.shape[1]
    z_pad[:, 0] = z_pad[:, chunks]
    z_pad[:, chunks + 1] = z_pad[:, 1]
    n = PIECE
    sub, lane = iotas(n)

    def step(k, total):
        c = pl.multiple_of(k * n, n)
        near = z_pad[2, pl.ds(c + 1, n)]
        own = [z_pad[r, pl.ds(c + 1, n)] for r in range(2)]
        faces = [north[r, pl.ds(c, n)] for r in range(2)]
        south_face = from_down[2, pl.ds(c, n)]
        below = [pltpu.roll(x, 1, 1) for x in (near * south_face, faces[0] * own[0], faces[1] * own[1])]
        above = [pltpu.roll(x, 7, 1) for x in (own[0], own[1], near)]
        for r in range(2):
            middle = center[r, pl.ds(c, n)]
            if r == 0:
                middle = middle + jnp.where(sub == 0, south_face, 0.0)
            ahead = pltpu.roll(z_pad[r, pl.ds(c + 1, n + 1)], 127, 2)
            ahead = jnp.where(lane == 127, ahead[1:], ahead[:-1])
            behind = pltpu.roll(east[r, pl.ds(c, n + 1)] * z_pad[r, pl.ds(c, n + 1)], 1, 2)
            behind = jnp.where(lane == 0, behind[:-1], behind[1:])
            image = (middle * own[r] - east[r, pl.ds(c + 1, n)] * ahead - behind
                     - faces[r] * jnp.where(sub == 7, above[r + 1], above[r])
                     - jnp.where(sub == 0, below[r], below[r + 1]))
            out[r, pl.ds(c, n)] = image
            if r == 0 and down_o is not None:
                down_o[pl.ds(c, n)] = image[:, 0:1]
            if r == 1 and up_o is not None:
                up_o[pl.ds(c, n)] = image[:, 7:8]
            total = total + jnp.sum(own[r] * image, axis=0)
        return total

    return lax.fori_loop(0, chunks // n, step, jnp.zeros((8, 128), F32))


def scalar_rows(values):
    sub = lax.broadcasted_iota(I32, (8, 128), 0)
    tile = jnp.zeros((8, 128), F32)
    for k, value in enumerate(values):
        tile = jnp.where(sub == k, value, tile)
    return tile


def second_kernel(info, parts, inverse, forcing, east, north, center, own, own_end, from_up, from_down,
                  gather, scatter, row_lanes, row_subs, ends,
                  z_o, image_o, jacobi_o, sums_o, kept_o, down_o, up_o, z_pad):
    chunks = forcing.shape[1]
    tile = jnp.sum(parts[...], axis=0)
    sums = unpack(tile)
    coef = coarse_solve(inverse, sums)
    kept_o[0:8] = tile
    kept_o[8:16] = jnp.broadcast_to(total_of(sums * coef), (8, 128))
    spread = spreader(coef, scatter, row_subs, ends, info[0])
    sub = iotas(STEP)[0]

    def step(k, total):
        c = pl.multiple_of(k * STEP, STEP)
        rows = pl.multiple_of(k * STEP * 8, STEP * 8)
        added = spread(own[pl.ds(rows, STEP * 8)], (0, 1)) + spread(own_end[pl.ds(rows, STEP * 8)], (2,))
        part = pl.ds(c, STEP)
        above = from_up[1, part] + pltpu.roll(north[1, part], 1, 1)
        below = jnp.broadcast_to(from_down[1, part], (STEP, 8, 128))
        near = jnp.where(sub == 0, above, below)
        centers = [center[0, part] + jnp.where(sub == 0, from_down[2, part], 0.0), center[1, part],
                   jnp.where(near == 0.0, 1.0, near)]
        fields = [forcing[0, part], forcing[1, part], ends_of(from_up[0, part], from_down[0, part])]
        for r in range(3):
            jacobi = 1.0 / centers[r]
            smooth = jacobi * fields[r]
            jacobi_o[r, part] = jacobi
            z = smooth + added[r]
            z_pad[r, pl.ds(c + 1, STEP)] = z
            if r < 2:
                z_o[r, part] = z
                total = total + jnp.sum(fields[r] * smooth, axis=0)
        return total

    smooth_total = lax.fori_loop(0, chunks // STEP, step, jnp.zeros((8, 128), F32))
    image_total = apply_operator(z_pad, east, north, center, from_down, image_o, down_o, up_o)
    tile = moments(image_o, own, gather, row_lanes, info[0])
    scalars = scalar_rows([jnp.sum(smooth_total, axis=0, keepdims=True), jnp.sum(image_total, axis=0, keepdims=True)])
    sums_o[...] = jnp.broadcast_to(jnp.concatenate([tile, scalars], axis=0)[None], sums_o.shape)


def third_kernel(info, parts, kept, inverse, forcing, image, jacobi, east, north, center, own, own_end,
                 from_up, from_down, image_up, image_down, scatter, row_subs, ends,
                 z_o, image_o, sums_o, scalars_o, z_pad):
    chunks = forcing.shape[1]
    tile = jnp.sum(parts[...], axis=0)
    energy = jnp.sum(tile[8:9], axis=1, keepdims=True) + kept[8:9, 0:1]
    alpha = energy / jnp.sum(tile[9:10], axis=1, keepdims=True)
    sums = unpack(kept[0:8] - alpha * tile[0:8])
    coef = coarse_solve(inverse, sums)
    scalars_o[...] = scalar_rows([alpha, energy, total_of(sums * coef)])
    spread = spreader(coef, scatter, row_subs, ends, info[0])
    factor = alpha.reshape(1, 1, 1)

    def step(k, total):
        c = pl.multiple_of(k * STEP, STEP)
        rows = pl.multiple_of(k * STEP * 8, STEP * 8)
        added = spread(own[pl.ds(rows, STEP * 8)], (0, 1)) + spread(own_end[pl.ds(rows, STEP * 8)], (2,))
        part = pl.ds(c, STEP)
        fields = [forcing[0, part], forcing[1, part], ends_of(from_up[0, part], from_down[0, part])]
        images = [image[0, part], image[1, part], ends_of(image_up[part], image_down[part])]
        for r in range(3):
            residual = fields[r] - factor * images[r]
            smooth = jacobi[r, part] * residual
            z = smooth + added[r]
            z_pad[r, pl.ds(c + 1, STEP)] = z
            if r < 2:
                z_o[r, part] = z
                total = total + jnp.sum(residual * smooth, axis=0)
        return total

    smooth_total = lax.fori_loop(0, chunks // STEP, step, jnp.zeros((8, 128), F32))
    image_total = apply_operator(z_pad, east, north, center, from_down, image_o, None, None)
    scalars = scalar_rows([jnp.sum(smooth_total, axis=0, keepdims=True), jnp.sum(image_total, axis=0, keepdims=True)])
    sums_o[...] = jnp.broadcast_to(scalars[None], sums_o.shape)


def last_kernel(parts, scalars, forcing, z_first, image_first, z_second, image_second, solution_o, residual_o):
    tile = jnp.sum(parts[...], axis=0)
    alpha, energy = scalars[0:1, 0:1], scalars[1:2, 0:1]
    energy_next = jnp.sum(tile[0:1], axis=1, keepdims=True) + scalars[2:3, 0:1]
    beta = energy_next / energy
    alpha_next = energy_next / (jnp.sum(tile[1:2], axis=1, keepdims=True) - beta * energy_next / alpha)
    alpha, beta, alpha_next = [x.reshape(1, 1, 1, 1) for x in (alpha, beta, alpha_next)]
    z, image = z_first[...], image_first[...]
    solution_o[...] = alpha * z + alpha_next * (z_second[...] + beta * z)
    residual_o[...] = (forcing[...] - alpha * image) - alpha_next * (image_second[...] + beta * image)


def body(forcing, east, north, storage, coarse_inverse, membership, land):
    rows, width = forcing.shape
    chunks = width // 128
    basins, coarse = coarse_inverse.shape[:2]
    tile_rows = membership.shape[0]
    total_rows = tile_rows * TILE
    start = lax.axis_index(GY) * rows
    code = membership + basins * land

    def codes_of(row, inside):
        at = jnp.clip(row // TILE, 0, tile_rows - 1)
        return jnp.where(inside, lax.dynamic_slice_in_dim(code, at, 1, 0), basins)

    codes = jnp.concatenate(
        [codes_of(start, True), codes_of(start + rows, start + rows < total_rows), codes_of(start - 1, start > 0)],
        axis=0,
    )
    info = (start % TILE // 8).reshape(1)
    gather, scatter, row_lanes, row_subs, ends = [jnp.asarray(x) for x in tables()]
    inverse = jnp.transpose(coarse_inverse, (2, 1, 0))

    def blocked(x):
        return x.reshape(2, 8, chunks, 128).transpose(0, 2, 1, 3)

    forcing, east, north, storage = [blocked(x) for x in (forcing, east, north, storage)]
    devices = lax.axis_size(GY)
    upward = [(i, i + 1) for i in range(devices - 1)]
    downward = [(j, i) for i, j in upward]
    inner, outer = lax.axis_size(GY[1]) * lax.axis_size(GY[2]), lax.axis_size(GY[0])

    def everywhere(copies):
        near = lax.all_to_all(copies, GY[1:], 0, 0)
        return lax.all_to_all(jnp.broadcast_to(jnp.sum(near, axis=0)[None], (outer,) + near.shape[1:]), GY[0], 0, 0)

    def call(kernel, outs, *args, scratch=()):
        places = [pl.BlockSpec(memory_space=pltpu.SMEM if x.dtype == I32 else pltpu.VMEM) for x in args]
        return pl.pallas_call(
            kernel,
            out_shape=[jax.ShapeDtypeStruct(s, d) for s, d in outs],
            in_specs=places,
            out_specs=[pl.BlockSpec(memory_space=pltpu.VMEM) for _ in outs],
            scratch_shapes=list(scratch),
        )(*args)

    own_shape = (2, chunks, 8, 128)
    line = (chunks, 1, 128)
    hot = (chunks * 8, 128)
    pad = pltpu.VMEM((3, chunks + 2, 8, 128), F32)
    east, north, center, own, own_end, sums, down, up = call(
        first_kernel,
        [((2, chunks + 1, 8, 128), F32), (own_shape, F32), (own_shape, F32), (hot, BF16), (hot, BF16),
         ((inner, 8, 128), F32), ((2,) + line, F32), ((3,) + line, F32)],
        codes, info, forcing, east, north, storage, gather, row_lanes,
    )
    from_up = lax.ppermute(down, GY, downward)
    from_down = lax.ppermute(up, GY, upward)
    parts = everywhere(sums)
    z_first, image_first, jacobi, sums, kept, down, up = call(
        second_kernel,
        [(own_shape, F32), (own_shape, F32), ((3, chunks, 8, 128), F32), ((inner, 16, 128), F32), ((16, 128), F32),
         (line, F32), (line, F32)],
        info, parts, inverse, forcing, east, north, center, own, own_end, from_up, from_down,
        gather, scatter, row_lanes, row_subs, ends,
        scratch=(pad,),
    )
    image_up = lax.ppermute(down, GY, downward)
    image_down = lax.ppermute(up, GY, upward)
    parts = everywhere(sums)
    z_second, image_second, sums, scalars = call(
        third_kernel,
        [(own_shape, F32), (own_shape, F32), ((inner, 8, 128), F32), ((8, 128), F32)],
        info, parts, kept, inverse, forcing, image_first, jacobi, east, north, center, own, own_end,
        from_up, from_down, image_up, image_down, scatter, row_subs, ends,
        scratch=(pad,),
    )
    parts = everywhere(sums)
    fields = (forcing, z_first, image_first, z_second, image_second)
    steps = chunks // STEP
    piece = pl.BlockSpec((2, STEP, 8, 128), lambda k: (0, k, 0, 0))
    answer = pl.pallas_call(
        last_kernel,
        grid=(steps,),
        out_shape=[jax.ShapeDtypeStruct(own_shape, F32)] * 2,
        in_specs=[pl.BlockSpec(parts.shape, lambda k: (0, 0, 0)), pl.BlockSpec((8, 128), lambda k: (0, 0))]
        + [piece] * len(fields),
        out_specs=[piece] * 2,
    )(parts, scalars, *fields)
    return tuple(x.transpose(0, 2, 1, 3).reshape(rows, width) for x in answer)


def solution(mesh):
    finer = Mesh(mesh.devices.reshape(mesh.shape["ens"], 8, 8, 2), ("ens", "gy_0", "gy_1", "gy_2"))
    return jax.shard_map(
        body,
        mesh=finer,
        in_specs=(P(ENS_GY, None), P(GY, None), P(GY, None), P(GY, None), P(), P(), P()),
        out_specs=(P(ENS_GY, None), P(ENS_GY, None)),
        check_vma=False,
    )
```

time: 216 us -> 141 us (0.65)
  blocking collectives: 123 us -> 42.5 us
  Pallas kernels: 0 us -> 38.6 us
  other arithmetic: 31.6 us -> 1.45 us
  starting transfers between devices: 17.7 us -> 40.3 us
  local copies, waits for them, and re-layouts: 24.8 us -> 3.24 us
  waiting for transfers between devices: 2.29 us -> 13.2 us
  matrix products: 9.99 us -> 0 us
  between operations: 5.55 us -> 0.8 us
    psum x9 -> x0, blocking collectives: 123 us -> none  [by_axis(): return functools.reduce(lax.psum, axes, shard)]
    all_to_all x0 -> x3, blocking collectives: none -> 42.5 us  [the longest x2 28 us: everywhere(): near = lax.all_to_all(copies, GY[1:], 0, 0)]
    pallas_call x0 -> x4, Pallas kernels: none -> 38.6 us  [the longest x3 31.6 us: call(): pl.pallas_call(kernel, out_shape=[jax.ShapeDtypeStruct(s, d) for s, d in...]
    all_to_all x0 -> x3, starting transfers between devices: none -> 26.4 us  [the longest x1 19.3 us: everywhere(): near = lax.all_to_all(copies, GY[1:], 0, 0)]
    reduce_sum x9 -> x3, other arithmetic: 16.5 us -> 0.06 us  [everywhere(): jnp.sum(near, axis=0)[None]]
    all_to_all x0 -> x3, waiting for transfers between devices: none -> 11.6 us  [the longest x2 6.25 us: everywhere(): lax.all_to_all(jnp.broadcast_to(jnp.sum(near, axis=0)[None], (outer,) + n...]
    dot_general x9 -> x0, matrix products: 9.99 us -> none  [the longest x2 4.19 us: spread(): return wet * jnp.dot(row_modes.T, lifted, precision=HIGHEST)]
    mul x2 -> x0, local copies, waits for them, and re-layouts: 6.46 us -> none  [moments(): lifted[:, None, :] * col_modes[None, :, :]]
  transfers between devices with their start and end apart: 5 -> 7, of which waited for: 2 -> 5; matrix products, arithmetic and copies ran while one was open for 10% -> 1% of each run, Pallas kernels for 0% -> 0%
where the time goes in v1:
time: 141 us; the launch traced here: 140 us
  blocking collectives  42.5 us (30%)
  starting transfers between devices  40.3 us (29%)
  Pallas kernels  38.6 us (27%)
  waiting for transfers between devices  13.2 us (9%)
  local copies, waits for them, and re-layouts  3.24 us (2%)
  other arithmetic  1.45 us (1%)
    pallas_call x3, Pallas kernels, call(): pl.pallas_call(kernel, out_shape=[jax.ShapeDtypeStruct(s, d) for s, d in...  31.6 us
    all_to_all x2, blocking collectives, everywhere(): near = lax.all_to_all(copies, GY[1:], 0, 0)  28 us
    all_to_all x1, starting transfers between devices, everywhere(): near = lax.all_to_all(copies, GY[1:], 0, 0)  19.3 us
    all_to_all x1, blocking collectives, everywhere(): lax.all_to_all(jnp.broadcast_to(jnp.sum(near, axis=0)[None], (outer,) + n...  14.5 us
    all_to_all x2, starting transfers between devices, everywhere(): lax.all_to_all(jnp.broadcast_to(jnp.sum(near, axis=0)[None], (outer,) + n...  7.09 us
    pallas_call x1, Pallas kernels, body(): pl.pallas_call(last_kernel, grid=(steps,), out_shape=[jax.ShapeDtypeStruc...  6.95 us
    all_to_all x2, waiting for transfers between devices, everywhere(): lax.all_to_all(jnp.broadcast_to(jnp.sum(near, axis=0)[None], (outer,) + n...  6.25 us
    ppermute x1, starting transfers between devices, body(): from_down = lax.ppermute(up, GY, upward)  5.73 us
  transfers between devices with their start and end apart: 7, of which 5 were waited for; matrix products, arithmetic and copies ran while one was open for 1% of the time, Pallas kernels for 0%

profile of v1, /device:TPU:513, one launch (start us, length us, event | category | flops | bytes accessed | tf_op | source)
XLA Modules:
  0.0 140.1 jit_solution(6311690207789381233)
XLA Ops:
  0.7 0.8 multiply_add_fusion
  1.5 0.6 pad_add_fusion.codes
  2.1 8.8 %shard_map.131 = (f32[2,129,8,128]{3,2,1,0:T(8,128)}, f32[2,128,8,128]{3,2,1,0:T(8,128)}, f32[2,128,8,128]{3,2,1,0:T(8,128)}, bf16[1024,128]{1,0:T(8,128)(2,1)},...) custom-call(s32[3,256]{1,0:T(4,128)} %pad_add_fusion.codes, ...), custom_call_target="tpu_custom_call" | custom-call | tf_op jit(solution)/shard_map/pallas_call | solution.py:354
  10.9 5.7 %collective-permute-start.1 = (f32[3,128,1,128]{3,2,1,0:T(1,128)}, f32[3,128,1,128]{3,2,1,0:T(1,128)S(1)}, u32[]{:S(2)}, u32[]{:S(2)}) collective-permute-start(f32[3,128,1,128]{3,2,1,0:T(1,128)} %get-tuple-element.30), channel_id=1, source_target_pairs={{0,1},{1,2},{2,3},{3,4},{4,5},{5,6},{6,7},{7,8},{8,9},{9,10},{10,1... | collective-permute-start | bytes 589832 | tf_op jit(solution)/shard_map/ppermute | solution.py:373
  16.6 19.3 %all-to-all-start = ((f32[16,8,128]{2,1,0:T(8,128)}), f32[16,8,128]{2,1,0:T(8,128)S(1)}, u32[]{:S(2)}, u32[]{:S(2)}) async-start(f32[16,8,128]{2,1,0:T(8,128)} %get-tuple-element.23), calls=%async_computation | async-start | bytes 131072 | tf_op jit(solution)/shard_map/all_to_all | solution.py:349
  35.9 2.6 %collective-permute-start = (f32[2,128,1,128]{3,2,1,0:T(1,128)}, f32[2,128,1,128]{3,2,1,0:T(1,128)S(1)}, u32[]{:S(2)}, u32[]{:S(2)}) collective-permute-start(f32[2,128,1,128]{3,2,1,0:T(1,128)} %get-tuple-element.29), channel_id=1, source_target_pairs={{1,0},{2,1},{3,2},{4,3},{5,4},{6,5},{7,6},{8,7},{9,8},{10,9},{11,1... | collective-permute-start | bytes 393224 | tf_op jit(solution)/shard_map/ppermute | solution.py:372
  38.5 5.3 %all-to-all-done = f32[16,8,128]{2,1,0:T(8,128)S(1)} async-done(((f32[16,8,128]{2,1,0:T(8,128)}), f32[16,8,128]{2,1,0:T(8,128)S(1)}, u32[]{:S(2)}, u32[]{:S(2)}) %all-to-all-start) | async-done | bytes 65568 | tf_op jit(solution)/shard_map/all_to_all | solution.py:349
  43.9 0.6 broadcast_in_dim.14
  44.5 3.5 %all-to-all-start.1 = ((f32[8,8,128]{2,1,0:T(8,128)}), f32[8,8,128]{2,1,0:T(8,128)S(1)}, u32[]{:S(2)}, u32[]{:S(2)}) async-start(f32[8,8,128]{2,1,0:T(8,128)} %broadcast_in_dim.14), calls=%async_computation.1 | async-start | bytes 65536 | tf_op jit(solution)/shard_map/all_to_all | solution.py:350
  48.0 0.7 copy.16
  48.7 5.9 %all-to-all-done.1.parts = f32[8,8,128]{2,1,0:T(8,128)S(1)} async-done(((f32[8,8,128]{2,1,0:T(8,128)}), f32[8,8,128]{2,1,0:T(8,128)S(1)}, u32[]{:S(2)}, u32[]{:S(2)}) %all-to-all-start.1) | async-done | bytes 32800 | tf_op jit(solution)/shard_map/all_to_all | solution.py:350
  54.7 0.6 copy-done.3
  55.4 11.8 %shard_map.132 = (f32[2,128,8,128]{3,2,1,0:T(8,128)}, f32[2,128,8,128]{3,2,1,0:T(8,128)}, f32[3,128,8,128]{3,2,1,0:T(8,128)}, f32[16,16,128]{2,1,0:T(8,128)}, f3...) custom-call(s32[1]{0:T(128)} %bitcast.info, f32[8,8,128]{2,1,0:T(8,128)} %copy-done.3, ...), custom_call_target="tpu_custom_call" | custom-call | tf_op jit(solution)/shard_map/pallas_call | solution.py:354
  67.2 14.0 %all_to_all.30 = f32[16,16,128]{2,1,0:T(8,128)S(1)} all-to-all(f32[16,16,128]{2,1,0:T(8,128)} %get-tuple-element.31), channel_id=1, replica_groups=mesh['ens'=2,'gy_0'=8,'gy_1'=8,'gy_2'=2] {'gy_1','gy_2'}, dimensions={0} | all-to-all | bytes 262144 | tf_op jit(solution)/shard_map/all_to_all | solution.py:349
  81.2 0.6 broadcast_in_dim.15
  81.8 3.6 %all-to-all-start.3 = ((f32[8,16,128]{2,1,0:T(8,128)}), f32[8,16,128]{2,1,0:T(8,128)S(1)}, u32[]{:S(2)}, u32[]{:S(2)}) async-start(f32[8,16,128]{2,1,0:T(8,128)} %broadcast_in_dim.15), calls=%async_computation.3 | async-start | bytes 131072 | tf_op jit(solution)/shard_map/all_to_all | solution.py:350
  85.4 2.0 %collective-permute-start.2 = (f32[128,1,128]{2,1,0:T(1,128)}, f32[128,1,128]{2,1,0:T(1,128)S(1)}, u32[]{:S(2)}, u32[]{:S(2)}) collective-permute-start(f32[128,1,128]{2,1,0:T(1,128)} %get-tuple-element.35), channel_id=1, source_target_pairs={{1,0},{2,1},{3,2},{4,3},{5,4},{6,5},{7,6},{8,7},{9,8},{10,9},{11,1... | collective-permute-start | bytes 196616 | tf_op jit(solution)/shard_map/ppermute | solution.py:383
  87.3 3.7 %collective-permute-start.3 = (f32[128,1,128]{2,1,0:T(1,128)}, f32[128,1,128]{2,1,0:T(1,128)S(1)}, u32[]{:S(2)}, u32[]{:S(2)}) collective-permute-start(f32[128,1,128]{2,1,0:T(1,128)} %get-tuple-element.36), channel_id=1, source_target_pairs={{0,1},{1,2},{2,3},{3,4},{4,5},{5,6},{6,7},{7,8},{8,9},{9,10},{10,1... | collective-permute-start | bytes 196616 | tf_op jit(solution)/shard_map/ppermute | solution.py:384
  91.0 0.5 collective-permute-done.2.image_up
  91.5 1.1 collective-permute-done.3.image_down
  93.6 11.1 %shard_map.133 = (f32[2,128,8,128]{3,2,1,0:T(8,128)}, f32[2,128,8,128]{3,2,1,0:T(8,128)}, f32[16,8,128]{2,1,0:T(8,128)}, f32[8,128]{1,0:T(8,128)}) custom-call(s32[1]{0:T(128)} %bitcast.info, f32[8,16,128]{2,1,0:T(8,128)} %copy-done.2, f32[16,128]{1,0:T(8,128)} %get-tuple-element.32.kept, f32[16,16,64]{2,1,0:T(8,128)} %bitcast.27, ...), custom_call_target="tpu_custom_call" | custom-call | tf_op jit(solution)/shard_map/pallas_call | solution.py:354
  104.7 14.0 %all_to_all.31 = f32[16,8,128]{2,1,0:T(8,128)S(1)} all-to-all(f32[16,8,128]{2,1,0:T(8,128)} %get-tuple-element.37), channel_id=1, replica_groups=mesh['ens'=2,'gy_0'=8,'gy_1'=8,'gy_2'=2] {'gy_1','gy_2'}, dimensions={0} | all-to-all | bytes 131072 | tf_op jit(solution)/shard_map/all_to_all | solution.py:349
  118.6 14.5 %all_to_all.32.parts = f32[8,8,128]{2,1,0:T(8,128)} all-to-all(f32[8,8,128]{2,1,0:T(8,128)S(1)} %broadcast_in_dim.28), channel_id=1, replica_groups=mesh['ens'=2,'gy_0'=8,'gy_1'=8,'gy_2'=2] {'gy_0'}, dimensions={0} | all-to-all | bytes 65536 | tf_op jit(solution)/shard_map/all_to_all | solution.py:350
  133.2 6.9 %shard_map.134 = (f32[2,128,8,128]{3,2,1,0:T(8,128)}, f32[2,128,8,128]{3,2,1,0:T(8,128)}) custom-call(f32[8,8,128]{2,1,0:T(8,128)} %all_to_all.32.parts, f32[8,128]{1,0:T(8,128)} %get-tuple-element.38.scalars, f32[2,128,8,128]{3,2,1,0:T(8,128)} %bitcast.25, f32[2,128,8,128]{3,2,1,0:T(8,128)} %get-tuple-element.39.z_first, ...), custom_call_target="tpu_custom_call" | custom-call | tf_op jit(solution)/shard_map/pallas_call | solution.py:397
  (21 shorter events, 1.1 us)
Async XLA Ops:
  2.1 45.9 %copy-start.4 = (f32[64,16,16]{0,2,1:T(8,128)S(1)}, f32[64,16,16]{0,2,1:T(8,128)}, u32[]{:S(2)}) copy-start(f32[64,16,16]{0,2,1:T(8,128)} %param.16) | copy-start | bytes 196612
  10.9 43.8 %collective-permute-start.1 = (f32[3,128,1,128]{3,2,1,0:T(1,128)}, f32[3,128,1,128]{3,2,1,0:T(1,128)S(1)}, u32[]{:S(2)}, u32[]{:S(2)}) collective-permute-start(f32[3,128,1,128]{3,2,1,0:T(1,128)} %get-tuple-element.30), channel_id=1, source_target_pairs={{0,1},{1,2},{2,3},{3,4},{4,5},{5,6},{6,7},{7,8},{8,9},{9,10},{10,1... | collective-permute-start | bytes 589832 | tf_op jit(solution)/shard_map/ppermute | solution.py:373
  16.6 27.2 %all-to-all-start = ((f32[16,8,128]{2,1,0:T(8,128)}), f32[16,8,128]{2,1,0:T(8,128)S(1)}, u32[]{:S(2)}, u32[]{:S(2)}) async-start(f32[16,8,128]{2,1,0:T(8,128)} %get-tuple-element.23), calls=%async_computation | async-start | bytes 131072 | tf_op jit(solution)/shard_map/all_to_all | solution.py:349
  35.9 12.8 %collective-permute-start = (f32[2,128,1,128]{3,2,1,0:T(1,128)}, f32[2,128,1,128]{3,2,1,0:T(1,128)S(1)}, u32[]{:S(2)}, u32[]{:S(2)}) collective-permute-start(f32[2,128,1,128]{3,2,1,0:T(1,128)} %get-tuple-element.29), channel_id=1, source_target_pairs={{1,0},{2,1},{3,2},{4,3},{5,4},{6,5},{7,6},{8,7},{9,8},{10,9},{11,1... | collective-permute-start | bytes 393224 | tf_op jit(solution)/shard_map/ppermute | solution.py:372
  44.5 10.2 %all-to-all-start.1 = ((f32[8,8,128]{2,1,0:T(8,128)}), f32[8,8,128]{2,1,0:T(8,128)S(1)}, u32[]{:S(2)}, u32[]{:S(2)}) async-start(f32[8,8,128]{2,1,0:T(8,128)} %broadcast_in_dim.14), calls=%async_computation.1 | async-start | bytes 65536 | tf_op jit(solution)/shard_map/all_to_all | solution.py:350
  48.7 5.9 %copy-start.1 = (f32[2,128,1,128]{3,2,1,0:T(1,128)}, f32[2,128,1,128]{3,2,1,0:T(1,128)S(1)}, u32[]{:S(2)}) copy-start(f32[2,128,1,128]{3,2,1,0:T(1,128)S(1)} %collective-permute-done.from_up) | copy-start | bytes 393220
  54.7 0.6 copy-start.3
  54.7 0.7 copy-start
  81.8 11.1 %all-to-all-start.3 = ((f32[8,16,128]{2,1,0:T(8,128)}), f32[8,16,128]{2,1,0:T(8,128)S(1)}, u32[]{:S(2)}, u32[]{:S(2)}) async-start(f32[8,16,128]{2,1,0:T(8,128)} %broadcast_in_dim.15), calls=%async_computation.3 | async-start | bytes 131072 | tf_op jit(solution)/shard_map/all_to_all | solution.py:350
  85.4 6.1 %collective-permute-start.2 = (f32[128,1,128]{2,1,0:T(1,128)}, f32[128,1,128]{2,1,0:T(1,128)S(1)}, u32[]{:S(2)}, u32[]{:S(2)}) collective-permute-start(f32[128,1,128]{2,1,0:T(1,128)} %get-tuple-element.35), channel_id=1, source_target_pairs={{1,0},{2,1},{3,2},{4,3},{5,4},{6,5},{7,6},{8,7},{9,8},{10,9},{11,1... | collective-permute-start | bytes 196616 | tf_op jit(solution)/shard_map/ppermute | solution.py:383
  87.3 5.3 %collective-permute-start.3 = (f32[128,1,128]{2,1,0:T(1,128)}, f32[128,1,128]{2,1,0:T(1,128)S(1)}, u32[]{:S(2)}, u32[]{:S(2)}) collective-permute-start(f32[128,1,128]{2,1,0:T(1,128)} %get-tuple-element.36), channel_id=1, source_target_pairs={{0,1},{1,2},{2,3},{3,4},{4,5},{5,6},{6,7},{7,8},{8,9},{9,10},{10,1... | collective-permute-start | bytes 196616 | tf_op jit(solution)/shard_map/ppermute | solution.py:384
  91.5 1.5 %copy-start.5 = (f32[128,1,128]{2,1,0:T(1,128)}, f32[128,1,128]{2,1,0:T(1,128)S(1)}, u32[]{:S(2)}) copy-start(f32[128,1,128]{2,1,0:T(1,128)S(1)} %collective-permute-done.2.image_up) | copy-start | bytes 196612
  92.7 0.6 copy-start.6
  93.0 0.6 copy-start.2

commit v2 on v1

v2 whole, which is shorter than its diff:
```python
import jax
import jax.numpy as jnp
import numpy as np
from jax import lax
from jax.experimental import pallas as pl
from jax.experimental.pallas import tpu as pltpu
from jax.sharding import Mesh
from jax.sharding import PartitionSpec as P

TILE = 64
ORDER = 4
GY = ("gy_0", "gy_1", "gy_2")
ENS_GY = ("ens", "gy_0", "gy_1", "gy_2")
F32, BF16, I32 = jnp.float32, jnp.bfloat16, jnp.int32
STEP = 16
PIECE = 8
BLOCK = 32
GROUPS = 4
SPACES = {"R": pltpu.HBM, "V": pltpu.VMEM}
VMEM_LIMIT = 24 * 2**20


def tables():
    degree = np.arange(ORDER)[:, None]
    mode = np.cos(np.pi * degree * (np.arange(TILE)[None, :] + 0.5) / TILE)
    p_of = np.tile(np.repeat(np.arange(ORDER), ORDER), 2)
    q_of = np.tile(np.arange(ORDER), 2 * ORDER)
    half = np.repeat(np.arange(2), ORDER * ORDER)
    lane = np.arange(128)
    cols = (mode[q_of][:, lane % TILE] * (half[:, None] == lane[None, :] // TILE)).astype(np.float32)
    high = cols.astype(BF16)
    low = (cols - high.astype(np.float32)).astype(BF16)
    gather = np.concatenate([high, low], axis=0)
    scatter = np.concatenate([high, high, low, np.zeros_like(low)], axis=0)
    rows = mode[p_of].reshape(32, 8, 8).transpose(1, 0, 2).astype(np.float32)
    row_lanes = np.tile(rows, (1, 1, 16))
    row_subs = np.tile(rows.transpose(0, 2, 1), (1, 1, 4))
    ends = np.zeros((TILE // 16, 8, 128), np.float32)
    for k in range(TILE // 16):
        ends[k, :4] = row_subs[(2 * k + 2) % 8, :4]
        ends[k, 4:] = row_subs[(2 * k - 1) % 8, 4:]
    return gather, scatter, row_lanes, row_subs, ends


def iotas(n):
    return lax.broadcasted_iota(I32, (n, 8, 128), 1), lax.broadcasted_iota(I32, (n, 8, 128), 2)


def onehot(codes):
    lane = lax.broadcasted_iota(I32, codes.shape, 2)
    return jnp.where(codes == (lane % TILE).astype(F32), 1.0, 0.0).reshape(-1, 128).astype(BF16)


def dot_nt(a, b):
    return lax.dot_general(a, b, (((1,), (1,)), ((), ())), preferred_element_type=F32)


def dot_nn(a, b):
    return lax.dot_general(a, b, (((1,), (0,)), ((), ())), preferred_element_type=F32)


def split(x):
    high = x.astype(BF16)
    return high, (x - high.astype(F32)).astype(BF16)


def moments(field, codes, gather, lanes, ready=None):
    wide = [jnp.concatenate([lanes[r]] * (BLOCK * 8 // 128), axis=1) for r in range(2)]

    def step(k, total):
        first = pl.multiple_of(k * BLOCK, BLOCK)
        if ready is not None:
            ready(k)
        lifted = jnp.zeros((32, BLOCK * 8), F32)
        for r in range(2):
            high, low = split(field[r, pl.ds(first, BLOCK)].reshape(BLOCK * 8, 128))
            both = dot_nt(gather[...], high)
            lifted = lifted + wide[r] * (both[:32] + both[32:] + dot_nt(gather[0:32], low))
        own = onehot(jnp.broadcast_to(codes[0, pl.ds(first, BLOCK)], (BLOCK, 8, 128)))
        parts = dot_nn(jnp.concatenate(split(lifted), axis=0), own)
        return total + parts[:32] + parts[32:]

    total = lax.fori_loop(0, codes.shape[1] // BLOCK, step, jnp.zeros((32, 128), F32))
    sums = total[:16] + pltpu.roll(total[16:], TILE, 1)
    lane = lax.broadcasted_iota(I32, (8, 128), 1)
    return jnp.where(lane < TILE, sums[:8], pltpu.roll(sums[8:], TILE, 1))


def unpack(tile):
    return jnp.concatenate([tile, pltpu.roll(tile, TILE, 1)], axis=0)[:, :TILE]


def coarse_solve(inverse, sums):
    coef = jnp.zeros_like(sums)
    for j in range(sums.shape[0]):
        coef = coef + inverse[j] * sums[j : j + 1]
    return coef


def total_of(x):
    return jnp.sum(jnp.sum(x, axis=1, keepdims=True), axis=0, keepdims=True)


def spreader(coef, scatter, patterns):
    zero = jnp.zeros_like(coef)
    rows = [jnp.concatenate([coef, zero], axis=1), jnp.concatenate([zero, coef], axis=1)]
    high, low = split(jnp.concatenate(rows * 4, axis=0))
    lane = lax.broadcasted_iota(I32, (1, 8, 128), 2)
    middle = (lane >= 32) & (lane < 64)

    def spread(codes, ids):
        own = onehot(codes)
        per_tile = (dot_nt(own, high) + dot_nt(own, low)).reshape(-1, 8, 128)
        result = []
        for r in ids:
            scaled = per_tile * patterns[r][None]
            rounded = scaled.astype(BF16).astype(F32)
            pieces = jnp.where(middle, scaled - rounded, rounded).astype(BF16)
            result.append(dot_nn(pieces.reshape(-1, 128), scatter[...]).reshape(-1, 8, 128))
        return result

    def all_of(codes, part):
        n = part.size
        sub = iotas(n)[0]
        own = jnp.broadcast_to(codes[0, part], (n, 8, 128))
        return spread(own, (0, 1)) + spread(jnp.where(sub < 4, codes[1, part], codes[2, part]), (2,))

    return all_of


def sum_kernel(parts, out):
    out[...] = jnp.broadcast_to(jnp.sum(parts[...], axis=0)[None], out.shape)


def scalar_rows(values):
    sub = lax.broadcasted_iota(I32, (8, 128), 0)
    tile = jnp.zeros((8, 128), F32)
    for k, value in enumerate(values):
        tile = jnp.where(sub == k, value, tile)
    return tile


def part_of(k, n):
    return pl.ds(pl.multiple_of(k * n, n), n)


class Loads:
    def __init__(self, pairs, sems, chunks):
        self.pairs, self.sems, self.size = pairs, sems, chunks // GROUPS

    def copy(self, i, group):
        source, target = self.pairs[i]
        part = part_of(group, self.size)
        return pltpu.make_async_copy(source.at[:, part], target.at[:, part], self.sems.at[i, group])

    def start(self, groups=range(4)):
        for group in groups:
            for i in range(len(self.pairs)):
                self.copy(i, group).start()

    def wait(self, group):
        for i in range(len(self.pairs)):
            self.copy(i, group).wait()

    def step(self, k, per_group):
        @pl.when(lax.rem(k, per_group) == 0)
        def _():
            self.wait(lax.div(k, per_group))


def moments_kernel(codes, info, forcing, gather, scatter, row_lanes, row_subs, ends,
                   sums_o, codes_o, gather_o, scatter_o, lanes_o, patterns_o, field, sems):
    chunks = forcing.shape[1]
    loads = Loads([(forcing, field)], sems, chunks)
    loads.start()
    lane = lax.broadcasted_iota(I32, (1, 128), 1)
    block = info[0]
    gather_o[...] = gather[...]
    scatter_o[...] = scatter[...]
    for r in range(2):
        lanes_o[r] = row_lanes[block + r]
        patterns_o[r] = row_subs[block + r]
    patterns_o[2] = ends[block // 2]

    def expand(c, carry):
        for row in range(3):
            codes_o[row, c] = jnp.where(lane < TILE, codes[row, 2 * c], codes[row, 2 * c + 1]).astype(F32)
        return carry

    lax.fori_loop(0, chunks, expand, 0, unroll=8)
    tile = moments(field, codes_o, gather, lanes_o, loads.wait)
    sums_o[...] = jnp.broadcast_to(tile[None], sums_o.shape)


def faces_kernel(codes, info, forcing, east, north, storage, east_o, north_o, center_o, mate_o, other_o,
                 f_in, e_in, n_in, s_in, sems):
    chunks = forcing.shape[1]
    basins = TILE
    loads = Loads([(forcing, f_in), (east, e_in), (north, n_in), (storage, s_in)], sems, chunks)
    loads.start((3, 0, 1, 2))
    lane = lax.broadcasted_iota(I32, (8, 128), 1)
    sub = lax.broadcasted_iota(I32, (8, 128), 0)
    odd = info[1] == 1

    def wet_of(code):
        return jnp.where(code < basins, 1.0, 0.0)

    def east_of(c):
        left, right = codes[0, 2 * c], codes[0, 2 * c + 1]
        after = codes[0, lax.rem(2 * c + 2, 2 * chunks)]
        wet = wet_of(jnp.where(lane < TILE, left, right))
        other = wet_of(jnp.where(lane < TILE - 1, left, jnp.where(lane < 127, right, after)))
        mask = wet * other
        return wet, [e_in[r, c] * mask for r in range(2)]

    def rolled(pair):
        return [pltpu.roll(x, 1, 1) for x in pair]

    loads.wait(3)
    last = east_of(chunks - 1)[1]
    for r in range(2):
        east_o[r, 0] = last[r]

    def chunk(c, carry):
        wet, face = east_of(c)
        up = wet_of(jnp.where(lane < TILE, codes[1, 2 * c], codes[1, 2 * c + 1]))
        turned = rolled(face)
        west = [jnp.where(lane == 0, carry[r], turned[r]) for r in range(2)]
        norths = [n_in[0, c] * wet, n_in[1, c] * jnp.where(sub < 7, wet, wet * up)]
        shifted = [pltpu.roll(x, 1, 0) for x in norths]
        south = [jnp.where(sub == 0, 0.0, shifted[0]), jnp.where(sub == 0, shifted[0], shifted[1])]
        centers = []
        for r in range(2):
            center = (1.0 - wet) + wet * s_in[r, c] + face[r] + west[r] + norths[r] + south[r]
            east_o[r, c + 1] = face[r]
            north_o[r, c] = norths[r]
            center_o[r, c] = center
            centers.append(center)
        fields = [f_in[0, c], f_in[1, c]]
        inner = jnp.where(sub < 4, fields[0], fields[1]) / jnp.where(sub < 4, centers[0], centers[1])
        first = [x[0][0:1] for x in (fields, centers, face, norths)] + [inner[1:2], inner[1:2]]
        final = [x[1][7:8] for x in (fields, centers, face, norths)] + [inner[6:7], norths[1][6:7]]
        for j in range(6):
            mate_o[j, c] = jnp.where(odd, first[j], final[j])
            other_o[j, c] = jnp.where(odd, final[j], first[j])
        return turned

    size = chunks // GROUPS

    def step(k, carry):
        @pl.when((lax.rem(k, size // 4) == 0) & (k < 3 * (size // 4)))
        def _():
            loads.wait(lax.div(k, size // 4))

        for j in range(4):
            carry = chunk(4 * k + j, carry)
        return carry

    lax.fori_loop(0, chunks // 4, step, rolled(last))


def apply_operator(z_pad, faces, blocks, out):
    east, north, center = faces
    chunks = z_pad.shape[1] - 2
    z_pad[:, 0] = z_pad[:, chunks]
    z_pad[:, chunks + 1] = z_pad[:, 1]
    n = PIECE
    sub, lane = iotas(n)

    def step(k, total):
        c = pl.multiple_of(k * n, n)
        own = [z_pad[r, pl.ds(c + 1, n)] for r in range(3)]
        faced = [north(r, pl.ds(c, n)) for r in range(3)]
        below = [pltpu.roll(faced[r] * own[r], 1, 1) for r in range(3)]
        above = [pltpu.roll(own[r], 7, 1) for r in range(3)]
        for r in range(blocks):
            ahead = pltpu.roll(z_pad[r, pl.ds(c + 1, n + 1)], 127, 2)
            ahead = jnp.where(lane == 127, ahead[1:], ahead[:-1])
            face = east(r, pl.ds(c, n + 1))
            behind = pltpu.roll(face * z_pad[r, pl.ds(c, n + 1)], 1, 2)
            behind = jnp.where(lane == 0, behind[:-1], behind[1:])
            image = (center(r, pl.ds(c, n)) * own[r] - face[1:] * ahead - behind
                     - faced[r] * jnp.where(sub == 7, above[(r + 1) % 3], above[r])
                     - jnp.where(sub == 0, below[(r + 2) % 3], below[r]))
            out[r, pl.ds(c, n)] = image
            if r < 2:
                total = total + jnp.sum(own[r] * image, axis=0)
        return total

    return lax.fori_loop(0, chunks // n, step, jnp.zeros((8, 128), F32))


def chooser(own, end):
    return lambda r, part: own[r, part] if r < 2 else end[part]


def beyond(mate, other, odd, part):
    sub = iotas(part.size)[0]
    after = jnp.logical_xor(sub < 4, odd)
    return lambda j: jnp.where(after, mate[j, part], other[j, part])


def end_rows(rows, north_last):
    sub = iotas(north_last.shape[0])[0]
    faced = jnp.where(sub == 6, rows(5), rows(3))
    center = rows(1) + jnp.where(sub == 0, pltpu.roll(north_last, 1, 1), 0.0)
    return rows(0), jnp.where(center == 0.0, 1.0, center), faced


def second_kernel(info, parts, inverse, forcing, mate, other, codes, gather, scatter, lanes, patterns, east, north, center_in,
                  z_o, image_o, sums_o, kept_o, center, field, mate_in, other_in, z_pad, image, end_e, end_n, end_c, sems, small):
    chunks = forcing.shape[1]
    loads = Loads([(forcing, field)], sems, chunks)
    halos = [pltpu.make_async_copy(x, y, small.at[i]) for i, (x, y) in enumerate([(mate, mate_in), (other, other_in)])]
    for copy in halos:
        copy.start()
    loads.start()
    tile = jnp.sum(parts[...], axis=0)
    sums = unpack(tile)
    coef = coarse_solve(inverse, sums)
    kept_o[0:8] = tile
    kept_o[8:16] = jnp.broadcast_to(total_of(sums * coef), (8, 128))
    spread = spreader(coef, scatter, patterns)
    sub = iotas(STEP)[0]
    odd = info[1] == 1
    for copy in halos:
        copy.wait()

    def step(k, total):
        part = part_of(k, STEP)
        loads.step(k, chunks // GROUPS // STEP)
        added = spread(codes, part)
        rows = beyond(mate_in, other_in, odd, part)
        end_f, end_center, end_north = end_rows(rows, north[1, part])
        end_n[part] = end_north
        end_c[part] = end_center
        end_e[pl.ds(k * STEP + 1, STEP)] = rows(2)
        first = center_in[0, part] + jnp.where(sub == 0, pltpu.roll(end_north, 1, 1), 0.0)
        center[0, part] = first
        center[1, part] = center_in[1, part]
        fields = [field[0, part], field[1, part], end_f]
        centers = [first, center[1, part], end_center]
        for r in range(3):
            smooth = fields[r] / centers[r]
            if r == 2:
                smooth = jnp.where((sub == 1) | (sub == 6), rows(4), smooth)
            z_pad[r, pl.ds(k * STEP + 1, STEP)] = smooth + added[r]
            if r < 2:
                total = total + jnp.sum(fields[r] * smooth, axis=0)
        return total

    smooth_total = lax.fori_loop(0, chunks // STEP, step, jnp.zeros((8, 128), F32))
    end_e[0] = end_e[chunks]
    save_z = pltpu.make_async_copy(z_pad.at[0:2, 1 : chunks + 1], z_o, small.at[2])
    save_z.start()
    faces = chooser(east, end_e), chooser(north, end_n), chooser(center, end_c)
    image_total = apply_operator(z_pad, faces, 3, image)
    save_image = pltpu.make_async_copy(image, image_o, small.at[3])
    save_image.start()
    tile = moments(image, codes, gather, lanes)
    scalars = scalar_rows([jnp.sum(smooth_total, axis=0, keepdims=True), jnp.sum(image_total, axis=0, keepdims=True)])
    sums_o[...] = jnp.broadcast_to(jnp.concatenate([tile, scalars], axis=0)[None], sums_o.shape)
    save_z.wait()
    save_image.wait()


def third_kernel(info, parts, kept, inverse, forcing, image, mate, other, codes, scatter, patterns, east, north, center,
                 z_o, image_o, sums_o, scalars_o, field, image_in, mate_in, other_in, z_pad, end_n, sems, small):
    chunks = forcing.shape[1]
    loads = Loads([(forcing, field), (image, image_in)], sems, chunks)
    halos = [pltpu.make_async_copy(x, y, small.at[i]) for i, (x, y) in enumerate([(mate, mate_in), (other, other_in)])]
    for copy in halos:
        copy.start()
    loads.start()
    tile = jnp.sum(parts[...], axis=0)
    energy = jnp.sum(tile[8:9], axis=1, keepdims=True) + kept[8:9, 0:1]
    alpha = energy / jnp.sum(tile[9:10], axis=1, keepdims=True)
    sums = unpack(kept[0:8] - alpha * tile[0:8])
    coef = coarse_solve(inverse, sums)
    scalars_o[...] = scalar_rows([alpha, energy, total_of(sums * coef)])
    spread = spreader(coef, scatter, patterns)
    factor = alpha.reshape(1, 1, 1)
    odd = info[1] == 1
    for copy in halos:
        copy.wait()

    def step(k, total):
        part = part_of(k, STEP)
        loads.step(k, chunks // GROUPS // STEP)
        added = spread(codes, part)
        end_f, end_center, end_n[part] = end_rows(beyond(mate_in, other_in, odd, part), north[1, part])
        fields = [field[0, part], field[1, part], end_f]
        centers = [center[0, part], center[1, part], end_center]
        for r in range(3):
            residual = fields[r] - factor * image_in[r, part]
            smooth = residual / centers[r]
            z = smooth + added[r]
            z_pad[r, pl.ds(k * STEP + 1, STEP)] = z
            if r < 2:
                z_o[r, part] = z
                total = total + jnp.sum(residual * smooth, axis=0)
        return total

    smooth_total = lax.fori_loop(0, chunks // STEP, step, jnp.zeros((8, 128), F32))
    faces = chooser(east, None), chooser(north, end_n), chooser(center, None)
    image_total = apply_operator(z_pad, faces, 2, image_o)
    scalars = scalar_rows([jnp.sum(smooth_total, axis=0, keepdims=True), jnp.sum(image_total, axis=0, keepdims=True)])
    sums_o[...] = jnp.broadcast_to(scalars[None], sums_o.shape)


def last_kernel(parts, scalars, forcing, z_first, image_first, z_second, image_second, solution_o, residual_o,
                f_in, z_in, image_in, solution_v, residual_v, sems, out_sems):
    chunks = forcing.shape[1]
    loads = Loads([(forcing, f_in), (z_first, z_in), (image_first.at[0:2], image_in)], sems, chunks)
    saves = Loads([(solution_v, solution_o), (residual_v, residual_o)], out_sems, chunks)
    loads.start()
    tile = jnp.sum(parts[...], axis=0)
    alpha, energy = scalars[0:1, 0:1], scalars[1:2, 0:1]
    energy_next = jnp.sum(tile[0:1], axis=1, keepdims=True) + scalars[2:3, 0:1]
    beta = energy_next / energy
    alpha_next = energy_next / (jnp.sum(tile[1:2], axis=1, keepdims=True) - beta * energy_next / alpha)
    alpha, beta, alpha_next = [x.reshape(1, 1, 1) for x in (alpha, beta, alpha_next)]
    per_group = chunks // GROUPS // PIECE

    def step(k, carry):
        loads.step(k, per_group)
        part = part_of(k, PIECE)
        for r in range(2):
            z, image = z_in[r, part], image_in[r, part]
            solution_v[r, part] = alpha * z + alpha_next * (z_second[r, part] + beta * z)
            residual_v[r, part] = (f_in[r, part] - alpha * image) - alpha_next * (image_second[r, part] + beta * image)

        @pl.when(lax.rem(k, per_group) == per_group - 1)
        def _():
            for i in range(2):
                saves.copy(i, lax.div(k, per_group)).start()

        return carry

    lax.fori_loop(0, chunks // PIECE, step, 0)
    for group in range(GROUPS):
        saves.wait(group)


def body(forcing, east, north, storage, coarse_inverse, membership, land):
    rows, width = forcing.shape
    chunks = width // 128
    basins = coarse_inverse.shape[0]
    tile_rows = membership.shape[0]
    total_rows = tile_rows * TILE
    index = lax.axis_index(GY)
    start = index * rows
    code = membership + basins * land

    def codes_of(row, inside):
        at = jnp.clip(row // TILE, 0, tile_rows - 1)
        return jnp.where(inside, lax.dynamic_slice_in_dim(code, at, 1, 0), basins)

    codes = jnp.concatenate(
        [codes_of(start, True), codes_of(start + rows, start + rows < total_rows), codes_of(start - 1, start > 0)],
        axis=0,
    )
    info = jnp.stack([start % TILE // 8, index % 2])
    inverse, codes = lax.optimization_barrier((jnp.transpose(coarse_inverse, (2, 1, 0)), codes))

    def blocked(x):
        return x.reshape(2, 8, chunks, 128).transpose(0, 2, 1, 3)

    forcing, east, north, storage = [blocked(x) for x in (forcing, east, north, storage)]
    devices = lax.axis_size(GY)
    mates = [(i, i ^ 1) for i in range(devices)]
    others = [(i, j) for i in range(devices) if (j := ((i + 1) ^ 1) - 1) in range(devices)]
    inner, outer = lax.axis_size(GY[1]) * lax.axis_size(GY[2]), lax.axis_size(GY[0])

    def call(kernel, outs, *args, scratch=(), label=""):
        places, values = [], []
        for x in args:
            kind = ""
            if isinstance(x, tuple):
                kind, x = x
            if x.dtype == I32:
                places.append(pl.BlockSpec(memory_space=pltpu.SMEM))
            elif kind in ("H", "R"):
                places.append(pl.BlockSpec(memory_space=pltpu.HBM if kind == "R" else pl.ANY))
            else:
                places.append(pl.BlockSpec(memory_space=pltpu.VMEM))
            values.append(pltpu.with_memory_space_constraint(x, SPACES[kind]) if kind in SPACES else x)
        shapes = [pltpu.VMEM(s, d) if k == "V" else jax.ShapeDtypeStruct(s, d) for k, s, d in outs]
        return pl.pallas_call(
            kernel,
            out_shape=shapes,
            in_specs=places,
            out_specs=[pl.BlockSpec(memory_space=pl.ANY if k == "H" else pltpu.VMEM) for k, _, _ in outs],
            scratch_shapes=list(scratch),
            compiler_params=pltpu.CompilerParams(vmem_limit_bytes=VMEM_LIMIT),
            name=label,
        )(*values)

    def everywhere(copies):
        near = lax.all_to_all(copies, GY[1:], 0, 0)
        (copies,) = call(sum_kernel, [("", (outer,) + near.shape[1:], F32)], near, label="middle")
        return lax.all_to_all(copies, GY[0], 0, 0)

    own_shape = (2, chunks, 8, 128)
    all_shape = (3, chunks, 8, 128)
    end_shape = (chunks, 8, 128)
    halo = (6, chunks, 1, 128)
    own_v, all_v, end_v, halo_v = [pltpu.VMEM(s, F32) for s in (own_shape, all_shape, end_shape, halo)]
    pad = pltpu.VMEM((3, chunks + 2, 8, 128), F32)

    def dma(*shape):
        return pltpu.SemaphoreType.DMA(shape)

    sums, lane_codes, gather, scatter, lanes, patterns = call(
        moments_kernel,
        [("", (inner, 8, 128), F32), ("V", (3, chunks, 1, 128), F32), ("V", (64, 128), BF16), ("V", (128, 128), BF16),
         ("V", (2, 32, 128), F32), ("V", (3, 8, 128), F32)],
        codes, info, ("R", forcing), *[jnp.asarray(x) for x in tables()],
        scratch=(own_v, dma(1, GROUPS)), label="moments",
    )
    parts = everywhere(sums)
    east, north, center, mate, other = call(
        faces_kernel,
        [("V", (2, chunks + 1, 8, 128), F32), ("V", own_shape, F32), ("V", own_shape, F32), ("", halo, F32), ("", halo, F32)],
        codes, info, ("R", forcing), ("R", east), ("R", north), ("R", storage),
        scratch=(own_v,) * 4 + (dma(4, GROUPS),), label="faces",
    )
    mate = lax.ppermute(mate, GY, mates)
    other = lax.ppermute(other, GY, others)
    kept_tables = [("V", x) for x in (gather, scatter, lanes, patterns)]
    z_first, image_first, sums, kept, center = call(
        second_kernel,
        [("H", own_shape, F32), ("H", all_shape, F32), ("", (inner, 16, 128), F32), ("", (16, 128), F32), ("V", own_shape, F32)],
        info, parts, inverse, ("H", forcing), ("H", mate), ("H", other), ("V", lane_codes), *kept_tables,
        ("V", east), ("V", north), ("V", center),
        scratch=(own_v, halo_v, halo_v, pad, all_v, pltpu.VMEM((chunks + 1, 8, 128), F32), end_v, end_v,
                 dma(1, GROUPS), dma(4)), label="second",
    )
    parts = everywhere(sums)
    z_second, image_second, sums, scalars = call(
        third_kernel,
        [("V", own_shape, F32), ("V", own_shape, F32), ("", (inner, 8, 128), F32), ("", (8, 128), F32)],
        info, parts, kept, inverse, ("H", forcing), ("H", image_first), ("H", mate), ("H", other), ("V", lane_codes),
        ("V", scatter), ("V", patterns), ("V", east), ("V", north), ("V", center),
        scratch=(own_v, all_v, halo_v, halo_v, pad, end_v, dma(2, GROUPS), dma(2)), label="third",
    )
    parts = everywhere(sums)
    answer = call(
        last_kernel,
        [("H", own_shape, F32)] * 2,
        parts, scalars, ("H", forcing), ("H", z_first), ("H", image_first), ("V", z_second), ("V", image_second),
        scratch=(own_v,) * 5 + (dma(3, GROUPS), dma(2, GROUPS)), label="last",
    )
    return tuple(x.transpose(0, 2, 1, 3).reshape(rows, width) for x in answer)


def solution(mesh):
    finer = Mesh(mesh.devices.reshape(mesh.shape["ens"], 8, 8, 2), ("ens", "gy_0", "gy_1", "gy_2"))
    return jax.shard_map(
        body,
        mesh=finer,
        in_specs=(P(ENS_GY, None), P(GY, None), P(GY, None), P(GY, None), P(), P(), P()),
        out_specs=(P(ENS_GY, None), P(ENS_GY, None)),
        check_vma=False,
    )
```

time: 141 us -> 118 us (0.84)
  blocking collectives: 42.5 us -> 63.9 us
  starting transfers between devices: 40.3 us -> 22.5 us
  waiting for transfers between devices: 13.2 us -> 0.01 us
  Pallas kernels: 38.6 us -> 28.8 us
  local copies, waits for them, and re-layouts: 3.24 us -> 0.98 us
    all_to_all x3 -> x0, starting transfers between devices: 26.4 us -> none  [the longest x1 19.3 us: everywhere(): near = lax.all_to_all(copies, GY[1:], 0, 0)]
    all_to_all x1 -> x3, blocking collectives: 14.5 us -> 29.2 us  [everywhere(): return lax.all_to_all(copies, GY[0], 0, 0)]
    all_to_all x3 -> x0, waiting for transfers between devices: 11.6 us -> none  [the longest x2 6.25 us: everywhere(): lax.all_to_all(jnp.broadcast_to(jnp.sum(near, axis=0)[None], (outer,) + n...]
    pallas_call x4 -> x8, Pallas kernels: 38.6 us -> 28.8 us  [call(): pl.pallas_call(kernel, out_shape=shapes, in_specs=places, out_specs=[pl.B...]
    ppermute x4 -> x2, starting transfers between devices: 13.9 us -> 22.5 us  [the longest x1 20.5 us: body(): mate = lax.ppermute(mate, GY, mates)]
    all_to_all x2 -> x3, blocking collectives: 28 us -> 34.7 us  [everywhere(): near = lax.all_to_all(copies, GY[1:], 0, 0)]
    ppermute x4 -> x2, waiting for transfers between devices: 1.63 us -> 0.01 us  [the longest x1 0.01 us: body(): mate = lax.ppermute(mate, GY, mates)]
  transfers between devices with their start and end apart: 7 -> 2, of which waited for: 5 -> 0; matrix products, arithmetic and copies ran while one was open for 1% -> 0% of each run, Pallas kernels for 0% -> 3%
where the time goes in v2:
time: 118 us
  blocking collectives  63.9 us (54%)
  Pallas kernels  28.8 us (24%)
  starting transfers between devices  22.5 us (19%)
    all_to_all x3, blocking collectives, everywhere(): near = lax.all_to_all(copies, GY[1:], 0, 0)  34.7 us
    all_to_all x3, blocking collectives, everywhere(): return lax.all_to_all(copies, GY[0], 0, 0)  29.2 us
    pallas_call x8, Pallas kernels, call(): pl.pallas_call(kernel, out_shape=shapes, in_specs=places, out_specs=[pl.B...  28.8 us
    ppermute x1, starting transfers between devices, body(): mate = lax.ppermute(mate, GY, mates)  20.5 us
  transfers between devices with their start and end apart: 2, of which 0 were waited for; matrix products, arithmetic and copies ran while one was open for 0% of the time, Pallas kernels for 3%

profile of v2, /device:TPU:513, one launch (start us, length us, event | category | flops | bytes accessed | tf_op | source)
XLA Modules:
  0.0 117.9 jit_solution(7641016841813860383)
XLA Ops:
  0.7 0.9 copy.16
  1.7 0.8 multiply_add_fusion
  2.5 0.1 pad_add_fusion.1.info
  2.6 0.0 copy-start.5
  2.6 6.2 %faces.1 = (f32[2,129,8,128]{3,2,1,0:T(8,128)S(1)}, f32[2,128,8,128]{3,2,1,0:T(8,128)S(1)}, f32[2,128,8,128]{3,2,1,0:T(8,128)S(1)}, f32[6,128,1,128]{3,2,1,0:T(1,128)S(1)}, f32[6,128,1,128]{3,2,1,0:T(1,128)S(1)}) custom-call(s32[3,256]{1,0:T(4,128)S(1)} %pad_add_fusion.codes, s32[2]{0:T(128)S(1)} %pad_add_fusion.1.info, f32[2,128,8,128]{3,2,1,0:T(8,128)} %bitcast.23, ...), custom_call_target="tpu_custom_call" | custom-call | tf_op jit(solution)/shard_map/faces/pallas_call | solution.py:489
  8.8 0.0 copy-start
  8.8 20.5 %collective-permute-start = (f32[6,128,1,128]{3,2,1,0:T(1,128)S(1)}, f32[6,128,1,128]{3,2,1,0:T(1,128)S(1)}, u32[]{:S(2)}, u32[]{:S(2)}) collective-permute-start(f32[6,128,1,128]{3,2,1,0:T(1,128)S(1)} %get-tuple-element.29), channel_id=1, source_target_pairs={{0,1},{1,0},{2,3},{3,2},{4,5},{5,4},{6,7},{7,6},{8,9},{9,8},{10,11... | collective-permute-start | bytes 1179656 | tf_op jit(solution)/shard_map/ppermute | solution.py:528
  29.3 1.9 %collective-permute-start.1 = (f32[6,128,1,128]{3,2,1,0:T(1,128)S(1)}, f32[6,128,1,128]{3,2,1,0:T(1,128)S(1)}, u32[]{:S(2)}, u32[]{:S(2)}) collective-permute-start(f32[6,128,1,128]{3,2,1,0:T(1,128)S(1)} %get-tuple-element.30), channel_id=1, source_target_pairs={{1,2},{2,1},{3,4},{4,3},{5,6},{6,5},{7,8},{8,7},{9,10},{10,9},{11,... | collective-permute-start | bytes 1179656 | tf_op jit(solution)/shard_map/ppermute | solution.py:529
  31.2 0.0 copy-done.1
  31.3 0.0 copy-done.2
  31.3 0.0 copy-done.3
  31.3 0.0 copy-done.4
  31.3 3.0 %moments.1 = (f32[16,8,128]{2,1,0:T(8,128)S(1)}, f32[3,128,1,128]{3,2,1,0:T(1,128)S(1)}, bf16[64,128]{1,0:T(8,128)(2,1)S(1)}, bf16[128,128]{1,0:T(8,128)(2,1)S(1...) custom-call(s32[3,256]{1,0:T(4,128)S(1)} %pad_add_fusion.codes, s32[2]{0:T(128)S(1)} %pad_add_fusion.1.info, ...), custom_call_target="tpu_custom_call" | custom-call | tf_op jit(solution)/shard_map/moments/pallas_call | solution.py:489
  34.4 11.0 %all_to_all.30.parts = f32[16,8,128]{2,1,0:T(8,128)S(1)} all-to-all(f32[16,8,128]{2,1,0:T(8,128)S(1)} %get-tuple-element.27), channel_id=1, replica_groups=mesh['ens'=2,'gy_0'=8,'gy_1'=8,'gy_2'=2] {'gy_1','gy_2'}, dimensions={0} | all-to-all | bytes 131072 | tf_op jit(solution)/shard_map/all_to_all | solution.py:500
  45.4 9.3 %all_to_all.31.parts = f32[8,8,128]{2,1,0:T(8,128)S(1)} all-to-all(f32[8,8,128]{2,1,0:T(8,128)S(1)} %middle.3), channel_id=1, replica_groups=mesh['ens'=2,'gy_0'=8,'gy_1'=8,'gy_2'=2] {'gy_0'}, dimensions={0} | all-to-all | bytes 65536 | tf_op jit(solution)/shard_map/all_to_all | solution.py:502
  54.7 0.0 collective-permute-done.mate
  54.7 0.0 collective-permute-done.1.other
  54.7 9.4 %second.1 = (f32[2,128,8,128]{3,2,1,0:T(8,128)S(1)}, f32[3,128,8,128]{3,2,1,0:T(8,128)S(1)}, f32[16,16,128]{2,1,0:T(8,128)S(1)}, f32[16,128]{1,0:T(8,128)S(1)}, f32[2,128,8,128]{3,2,1,0:T(8,128)S(1)}) custom-call(s32[2]{0:T(128)S(1)} %pad_add_fusion.1.info, f32[8,8,128]{2,1,0:T(8,128)S(1)} %all_to_all.31.parts, f32[16,16,64]{2,1,0:T(8,128)S(1)} %bitcast.28, ...), custom_call_target="tpu_custom_call" | custom-call | tf_op jit(solution)/shard_map/second/pallas_call | solution.py:489
  64.1 12.9 %all_to_all.32.parts = f32[16,16,128]{2,1,0:T(8,128)S(1)} all-to-all(f32[16,16,128]{2,1,0:T(8,128)S(1)} %get-tuple-element.39), channel_id=1, replica_groups=mesh['ens'=2,'gy_0'=8,'gy_1'=8,'gy_2'=2] {'gy_1','gy_2'}, dimensions={0} | all-to-all | bytes 262144 | tf_op jit(solution)/shard_map/all_to_all | solution.py:500
  77.0 10.6 %all_to_all.33.parts = f32[8,16,128]{2,1,0:T(8,128)S(1)} all-to-all(f32[8,16,128]{2,1,0:T(8,128)S(1)} %middle.4), channel_id=1, replica_groups=mesh['ens'=2,'gy_0'=8,'gy_1'=8,'gy_2'=2] {'gy_0'}, dimensions={0} | all-to-all | bytes 131072 | tf_op jit(solution)/shard_map/all_to_all | solution.py:502
  87.7 7.8 %third.1 = (f32[2,128,8,128]{3,2,1,0:T(8,128)S(1)}, f32[2,128,8,128]{3,2,1,0:T(8,128)S(1)}, f32[16,8,128]{2,1,0:T(8,128)S(1)}, f32[8,128]{1,0:T(8,128)S(1)}) custom-call(s32[2]{0:T(128)S(1)} %pad_add_fusion.1.info, f32[8,16,128]{2,1,0:T(8,128)S(1)} %all_to_all.33.parts, f32[16,128]{1,0:T(8,128)S(1)} %get-tuple-element.40.kept, f32[16,16,64]{2,1,0:T(8,128)S(1)} %bitcast.29, ...), custom_call_target="tpu_custom_call" | custom-call | tf_op jit(solution)/shard_map/third/pallas_call | solution.py:489
  95.5 10.7 %all_to_all.34.parts = f32[16,8,128]{2,1,0:T(8,128)S(1)} all-to-all(f32[16,8,128]{2,1,0:T(8,128)S(1)} %get-tuple-element.43), channel_id=1, replica_groups=mesh['ens'=2,'gy_0'=8,'gy_1'=8,'gy_2'=2] {'gy_1','gy_2'}, dimensions={0} | all-to-all | bytes 131072 | tf_op jit(solution)/shard_map/all_to_all | solution.py:500
  106.3 9.3 %all_to_all.35.parts = f32[8,8,128]{2,1,0:T(8,128)S(1)} all-to-all(f32[8,8,128]{2,1,0:T(8,128)S(1)} %middle.5), channel_id=1, replica_groups=mesh['ens'=2,'gy_0'=8,'gy_1'=8,'gy_2'=2] {'gy_0'}, dimensions={0} | all-to-all | bytes 65536 | tf_op jit(solution)/shard_map/all_to_all | solution.py:502
  115.6 2.3 %last.1 = (f32[2,128,8,128]{3,2,1,0:T(8,128)}, f32[2,128,8,128]{3,2,1,0:T(8,128)}) custom-call(f32[8,8,128]{2,1,0:T(8,128)S(1)} %all_to_all.35.parts, f32[8,128]{1,0:T(8,128)S(1)} %get-tuple-element.44.scalars, f32[2,128,8,128]{3,2,1,0:T(8,128)S(1)} %bitcast.27, f32[2,128,8,128]{3,2,1,0:T(8,128)S(1)} %get-tuple-element.45.z_first, ...), custom_call_target="tpu_custom_call" | custom-call | tf_op jit(solution)/shard_map/last/pallas_call | solution.py:489
  (11 shorter events, 0.1 us)
Async XLA Ops:
  2.6 28.7 %copy-start.1 = (f32[8,32,128]{2,1,0:T(8,128)S(1)}, f32[8,32,128]{2,1,0:T(8,128)}, u32[]{:S(2)}) copy-start(f32[8,32,128]{2,1,0:T(8,128)} %constant.99.clone.row_lanes) | copy-start | bytes 393220
  2.6 28.7 %copy-start.2 = (f32[8,8,128]{2,1,0:T(8,128)S(1)}, f32[8,8,128]{2,1,0:T(8,128)}, u32[]{:S(2)}) copy-start(f32[8,8,128]{2,1,0:T(8,128)} %constant.100.clone.row_subs) | copy-start | bytes 98308
  2.6 28.7 %copy-start.3 = (bf16[128,128]{1,0:T(8,128)(2,1)S(1)}, bf16[128,128]{1,0:T(8,128)(2,1)}, u32[]{:S(2)}) copy-start(bf16[128,128]{1,0:T(8,128)(2,1)} %constant.98.clone.scatter) | copy-start | bytes 98308
  2.6 28.7 %copy-start.4 = (f32[4,8,128]{2,1,0:T(8,128)S(1)}, f32[4,8,128]{2,1,0:T(8,128)}, u32[]{:S(2)}) copy-start(f32[4,8,128]{2,1,0:T(8,128)} %constant.101.clone.ends) | copy-start | bytes 49156
  2.6 28.7 %copy-start.5 = (bf16[64,128]{1,0:T(8,128)(2,1)S(1)}, bf16[64,128]{1,0:T(8,128)(2,1)}, u32[]{:S(2)}) copy-start(bf16[64,128]{1,0:T(8,128)(2,1)} %constant.97.clone.gather) | copy-start | bytes 49156
  8.8 45.9 %copy-start = (f32[16,16384]{1,0:T(8,128)S(1)}, f32[16,16384]{1,0:T(8,128)}, u32[]{:S(2)}) copy-start(f32[16,16384]{1,0:T(8,128)} %param.12) | copy-start | bytes 3145732
  8.8 45.9 %collective-permute-start = (f32[6,128,1,128]{3,2,1,0:T(1,128)S(1)}, f32[6,128,1,128]{3,2,1,0:T(1,128)S(1)}, u32[]{:S(2)}, u32[]{:S(2)}) collective-permute-start(f32[6,128,1,128]{3,2,1,0:T(1,128)S(1)} %get-tuple-element.29), channel_id=1, source_target_pairs={{0,1},{1,0},{2,3},{3,2},{4,5},{5,4},{6,7},{7,6},{8,9},{9,8},{10,11... | collective-permute-start | bytes 1179656 | tf_op jit(solution)/shard_map/ppermute | solution.py:528
  29.3 25.4 %collective-permute-start.1 = (f32[6,128,1,128]{3,2,1,0:T(1,128)S(1)}, f32[6,128,1,128]{3,2,1,0:T(1,128)S(1)}, u32[]{:S(2)}, u32[]{:S(2)}) collective-permute-start(f32[6,128,1,128]{3,2,1,0:T(1,128)S(1)} %get-tuple-element.30), channel_id=1, source_target_pairs={{1,2},{2,1},{3,4},{4,3},{5,6},{6,5},{7,8},{8,7},{9,10},{10,9},{11,... | collective-permute-start | bytes 1179656 | tf_op jit(solution)/shard_map/ppermute | solution.py:529

commit v3 on v2

v3 whole, which is shorter than its diff:
```python
import jax
import jax.numpy as jnp
import numpy as np
from jax import lax
from jax.experimental import pallas as pl
from jax.experimental.pallas import tpu as pltpu
from jax.sharding import Mesh
from jax.sharding import PartitionSpec as P


TILE = 64
ORDER = 4
GY = ("gy_0", "gy_1", "gy_2")
ENS_GY = ("ens", "gy_0", "gy_1", "gy_2")
F32, BF16, I32 = jnp.float32, jnp.bfloat16, jnp.int32
ROWS = 8
PIECE = 8
BLOCK = 32
GROUPS = 4
VMEM_LIMIT = 24 * 2**20


def tables():
    degree = np.arange(ORDER)[:, None]
    mode = np.cos(np.pi * degree * (np.arange(TILE)[None, :] + 0.5) / TILE)
    p_of = np.tile(np.repeat(np.arange(ORDER), ORDER), 2)
    q_of = np.tile(np.arange(ORDER), 2 * ORDER)
    half = np.repeat(np.arange(2), ORDER * ORDER)
    lane = np.arange(128)
    cols = (mode[q_of][:, lane % TILE] * (half[:, None] == lane[None, :] // TILE)).astype(np.float32)
    high = cols.astype(BF16)
    low = (cols - high.astype(np.float32)).astype(BF16)
    gather = np.concatenate([high, low], axis=0)
    scatter = np.concatenate([high, high, low, np.zeros_like(low)], axis=0)
    rows = mode[p_of].reshape(32, 8, 8).transpose(1, 0, 2).astype(np.float32)
    row_lanes = np.tile(rows, (1, 1, 16))
    row_subs = np.broadcast_to(mode.reshape(ORDER, 8, 8, 1).transpose(1, 0, 2, 3), (8, ORDER, 8, 128)).astype(np.float32)
    ends = np.zeros((TILE // 16, ORDER, 8, 128), np.float32)
    for k in range(TILE // 16):
        ends[k, :, :4] = row_subs[(2 * k + 2) % 8, :, :4]
        ends[k, :, 4:] = row_subs[(2 * k - 1) % 8, :, 4:]
    return gather, scatter, row_lanes, row_subs, ends


def iota(shape, dim):
    return lax.broadcasted_iota(I32, shape, dim)


def onehot(codes):
    return jnp.where(codes == (iota(codes.shape, 1) % TILE).astype(F32), 1.0, 0.0).astype(BF16)


def spread_row(ref, row):
    return jnp.broadcast_to(ref[pl.ds(row, 1)], (8, 128))


def dot_nt(a, b):
    return lax.dot_general(a, b, (((1,), (1,)), ((), ())), preferred_element_type=F32)


def dot_nn(a, b):
    return lax.dot_general(a, b, (((1,), (0,)), ((), ())), preferred_element_type=F32)


def split(x):
    high = x.astype(BF16)
    return high, (x - high.astype(F32)).astype(BF16)


def expand(codes_small, out):
    chunks, tiles = out.shape[1], codes_small.shape[1]
    mine = iota((chunks, tiles), 1) // 2 == iota((chunks, tiles), 0)
    halves = jnp.where(iota((tiles, 128), 0) % 2 == iota((tiles, 128), 1) // TILE, 1.0, 0.0).astype(BF16)
    for k in range(3):
        out[k] = dot_nn(jnp.where(mine, codes_small[k : k + 1], 0.0).astype(BF16), halves)


def moments(field, codes, gather, lanes, ready=None):
    wide = [jnp.concatenate([lanes[r]] * (BLOCK * 8 // 128), axis=1) for r in range(2)]

    def step(k, total):
        first = pl.multiple_of(k * BLOCK, BLOCK)
        if ready is not None:
            ready(k)
        lifted = jnp.zeros((32, BLOCK * 8), F32)
        for r in range(2):
            high, low = split(field[r, pl.ds(first, BLOCK)].reshape(BLOCK * 8, 128))
            both = dot_nt(gather[...], high)
            lifted = lifted + wide[r] * (both[:32] + both[32:] + dot_nt(gather[0:32], low))
        own = onehot(jnp.concatenate([spread_row(codes.at[0], first + j) for j in range(BLOCK)], axis=0))
        parts = dot_nn(jnp.concatenate(split(lifted), axis=0), own)
        return total + parts[:32] + parts[32:]

    total = lax.fori_loop(0, codes.shape[1] // BLOCK, step, jnp.zeros((32, 128), F32))
    sums = total[:16] + pltpu.roll(total[16:], TILE, 1)
    return jnp.where(iota((8, 128), 1) < TILE, sums[:8], pltpu.roll(sums[8:], TILE, 1))


def unpack(tile):
    return jnp.concatenate([tile, pltpu.roll(tile, TILE, 1)], axis=0)[:, :TILE]


def coarse_solve(inverse, sums):
    coef = jnp.zeros_like(sums)
    for j in range(sums.shape[0]):
        coef = coef + inverse[j] * sums[j : j + 1]
    return coef


def total_of(x):
    return jnp.sum(jnp.sum(x, axis=1, keepdims=True), axis=0, keepdims=True)


def column_tables(coef, codes, scatter, out):
    zero = jnp.zeros_like(coef)
    rows = [jnp.concatenate([coef, zero], axis=1), jnp.concatenate([zero, coef], axis=1)]
    high, low = split(jnp.concatenate(rows * 4, axis=0))
    for row in range(3):
        own = onehot(codes[row])
        per_tile = dot_nt(own, high) + dot_nt(own, low)
        lane = iota(per_tile.shape, 1)
        rounded = per_tile.astype(BF16).astype(F32)
        pieces = jnp.where(lane // 32 == 1, per_tile - rounded, rounded)
        split_p = [jnp.where(lane // ORDER % ORDER == p, pieces, 0.0).astype(BF16) for p in range(ORDER)]
        columns = dot_nn(jnp.concatenate(split_p, axis=0), scatter[...])
        for p in range(ORDER):
            out[row, p] = columns[p * codes.shape[1] : (p + 1) * codes.shape[1]]


def sum_kernel(parts, out):
    out[...] = jnp.broadcast_to(jnp.sum(parts[...], axis=0)[None], out.shape)


def scalar_rows(values):
    tile = jnp.zeros((8, 128), F32)
    for k, value in enumerate(values):
        tile = jnp.where(iota((8, 128), 0) == k, value, tile)
    return tile


class Loads:
    def __init__(self, pairs, sems, chunks):
        self.pairs, self.sems, self.size = pairs, sems, chunks // GROUPS

    def copy(self, i, group):
        source, target = self.pairs[i]
        part = pl.ds(pl.multiple_of(group * self.size, self.size), self.size)
        return pltpu.make_async_copy(source.at[:, part], target.at[:, part], self.sems.at[i, group])

    def start(self, groups=range(GROUPS)):
        for group in groups:
            for i in range(len(self.pairs)):
                self.copy(i, group).start()

    def wait(self, group):
        for i in range(len(self.pairs)):
            self.copy(i, group).wait()


def moments_kernel(info, forcing, membership, land, gather, scatter, row_lanes, row_subs, ends,
                   sums_o, codes_o, gather_o, scatter_o, lanes_o, patterns_o, field, codes, member_in, land_in, sems, small):
    chunks = forcing.shape[1]
    block = info[0]
    pairs = [(membership, member_in), (land, land_in), (gather, gather_o), (row_lanes.at[pl.ds(block, 2)], lanes_o),
             (scatter, scatter_o), (row_subs.at[pl.ds(block, 2)], patterns_o.at[0:2]), (ends.at[lax.div(block, 2)], patterns_o.at[2])]
    copies = [pltpu.make_async_copy(x, y, small.at[i]) for i, (x, y) in enumerate(pairs)]
    for copy in copies:
        copy.start()
    loads = Loads([(forcing, field)], sems, chunks)
    loads.start()
    for copy in copies:
        copy.wait()
    for k in range(3):
        row = pl.ds(jnp.maximum(info[2 + k], 0), 1)
        dry = (land_in[row] == 1) | (info[2 + k] < 0)
        codes_o[k : k + 1] = jnp.where(dry, TILE, member_in[row]).astype(F32)
    expand(codes_o, codes)
    tile = moments(field, codes, gather_o, lanes_o, loads.wait)
    sums_o[...] = jnp.broadcast_to(tile[None], sums_o.shape)


def faces_kernel(info, codes_small, forcing, east, north, storage, east_o, north_o, center_o, mate_h, other_h,
                 mate_o, other_o, codes, f_in, e_in, n_in, s_in, sems, small):
    chunks = forcing.shape[1]
    loads = Loads([(east, e_in), (north, n_in), (storage, s_in), (forcing, f_in)], sems, chunks)
    loads.start((3, 0, 1, 2))
    expand(codes_small, codes)
    lane, sub = iota((8, 128), 1), iota((8, 128), 0)
    odd = info[1] == 1

    def rolled(x):
        return pltpu.roll(x, 1, 1)

    def after_of(row):
        code = spread_row(codes.at[0], row)
        return code, pltpu.roll(code, 127, 1)

    def east_of(c, here, turned, turned_next):
        mask = (here < TILE) & (jnp.where(lane == 127, turned_next, turned) < TILE)
        return [jnp.where(mask, e_in[r, c], 0.0) for r in range(2)]

    first_code, first_turned = after_of(0)
    loads.wait(3)
    last = east_of(chunks - 1, *after_of(chunks - 1), first_turned)
    for r in range(2):
        east_o[r, 0] = last[r]

    def chunk(k, j, carry):
        west_before, here, turned = carry
        c = k * ROWS + j
        ahead = k * ROWS + j + 1 if j + 1 < ROWS else lax.rem(k * ROWS + ROWS, chunks)
        coming, coming_turned = after_of(ahead)
        face = east_of(c, here, turned, coming_turned)
        wet = here < TILE
        open_north = wet & ((sub < 7) | (spread_row(codes.at[1], c) < TILE))
        west_next = [rolled(x) for x in face]
        west = [jnp.where(lane == 0, west_before[r], west_next[r]) for r in range(2)]
        norths = [jnp.where(wet, n_in[0, c], 0.0), jnp.where(open_north, n_in[1, c], 0.0)]
        shifted = [pltpu.roll(x, 1, 0) for x in norths]
        south = [jnp.where(sub == 0, 0.0, shifted[0]), jnp.where(sub == 0, shifted[0], shifted[1])]
        fields, centers = [f_in[0, c], f_in[1, c]], []
        for r in range(2):
            center = jnp.where(wet, s_in[r, c], 1.0) + face[r] + west[r] + norths[r] + south[r]
            east_o[r, c + 1] = face[r]
            north_o[r, c] = norths[r]
            center_o[r, c] = center
            centers.append(center)
        smooth = jnp.where(sub < 4, fields[0], fields[1]) / jnp.where(sub < 4, centers[0], centers[1])
        first = [x[0][0:1] for x in (fields, centers, face, norths)] + [smooth[1:2]] * 2
        final = [x[1][7:8] for x in (fields, centers, face, norths)] + [smooth[6:7], norths[1][6:7]]
        for j in range(6):
            mate_o[j, c] = jnp.where(odd, first[j], final[j])
            other_o[j, c] = jnp.where(odd, final[j], first[j])
        return west_next, coming, coming_turned

    size = chunks // GROUPS // ROWS

    def step(k, carry):
        @pl.when((lax.rem(k, size) == 0) & (k < (GROUPS - 1) * size))
        def _():
            loads.wait(lax.div(k, size))

        for j in range(ROWS):
            carry = chunk(k, j, carry)
        return carry

    lax.fori_loop(0, chunks // ROWS, step, ([rolled(x) for x in last], first_code, first_turned))
    saves = [pltpu.make_async_copy(x, y, small.at[i]) for i, (x, y) in enumerate([(mate_o, mate_h), (other_o, other_h)])]
    for copy in saves:
        copy.start()
    for copy in saves:
        copy.wait()


def apply_operator(z_pad, faces, blocks, out):
    east, north, center = faces
    chunks = z_pad.shape[1] - 2
    z_pad[:, 0] = z_pad[:, chunks]
    z_pad[:, chunks + 1] = z_pad[:, 1]
    n = PIECE
    sub, lane = iota((n, 8, 128), 1), iota((n, 8, 128), 2)

    def step(k, total):
        c = pl.multiple_of(k * n, n)
        own = [z_pad[r, pl.ds(c + 1, n)] for r in range(3)]
        faced = [north(r, pl.ds(c, n)) for r in range(3)]
        below = [pltpu.roll(faced[r] * own[r], 1, 1) for r in range(3)]
        above = [pltpu.roll(own[r], 7, 1) for r in range(3)]
        for r in range(blocks):
            ahead = pltpu.roll(z_pad[r, pl.ds(c + 1, n + 1)], 127, 2)
            ahead = jnp.where(lane == 127, ahead[1:], ahead[:-1])
            face = east(r, pl.ds(c, n + 1))
            behind = pltpu.roll(face * z_pad[r, pl.ds(c, n + 1)], 1, 2)
            behind = jnp.where(lane == 0, behind[:-1], behind[1:])
            image = (center(r, pl.ds(c, n)) * own[r] - face[1:] * ahead - behind
                     - faced[r] * jnp.where(sub == 7, above[(r + 1) % 3], above[r])
                     - jnp.where(sub == 0, below[(r + 2) % 3], below[r]))
            out[r, pl.ds(c, n)] = image
            if r < 2:
                total = total + jnp.sum(own[r] * image, axis=0)
        return total

    return lax.fori_loop(0, chunks // n, step, jnp.zeros((8, 128), F32))


def chooser(*views):
    return lambda r, part: views[r][part]


class Spread:
    def __init__(self, columns, patterns):
        self.columns = columns
        self.patterns = [[patterns[r, p] for p in range(ORDER)] for r in range(3)]
        self.sub = iota((8, 128), 0)

    def at(self, c):
        def row(k, p):
            return spread_row(self.columns.at[k, p], c)

        own = [row(0, p) for p in range(ORDER)]
        end = [jnp.where(self.sub < 4, row(1, p), row(2, p)) for p in range(ORDER)]
        return [sum(self.patterns[r][p] * x[p] for p in range(ORDER)) for r, x in enumerate((own, own, end))]


def second_kernel(info, parts, forcing, mate_h, other_h, inverse, codes_small, gather, scatter, lanes, patterns, east, north, center,
                  field, z_pad, image_o, sums_o, kept_o, center_o, jacobi_o, end_f, end_n,
                  mate, other, codes, end_e, end_c, columns, sems, small):
    chunks = forcing.shape[1]
    halos = [pltpu.make_async_copy(x, y, small.at[i]) for i, (x, y) in enumerate([(mate_h, mate), (other_h, other)])]
    for copy in halos:
        copy.start()
    loads = Loads([(forcing, field)], sems, chunks)
    loads.start()
    expand(codes_small, codes)
    tile = jnp.sum(parts[...], axis=0)
    sums = unpack(tile)
    coef = coarse_solve(inverse, sums)
    kept_o[0:8] = tile
    kept_o[8:16] = jnp.broadcast_to(total_of(sums * coef), (8, 128))
    column_tables(coef, codes, scatter, columns)
    spread = Spread(columns, patterns)
    sub = iota((8, 128), 0)
    after = jnp.logical_xor(sub < 4, info[1] == 1)

    def chunk(c, total):
        added = spread.at(c)

        def rows(j):
            return jnp.where(after, mate[j, c], other[j, c])

        faced = jnp.where(sub == 6, rows(5), rows(3))
        far = rows(0)
        beyond = rows(1) + jnp.where(sub == 0, pltpu.roll(north[1, c], 1, 0), 0.0)
        first = center[0, c] + jnp.where(sub == 0, pltpu.roll(faced, 1, 0), 0.0)
        both = jnp.where(sub == 3, pltpu.roll(first, 3, 0), jnp.where(beyond == 0.0, 1.0, beyond))
        inverted = 1.0 / both
        own = [jnp.where(sub == 0, pltpu.roll(inverted, 5, 0), 1.0 / center[0, c]), 1.0 / center[1, c]]
        end_f[c] = far
        end_n[c] = faced
        end_e[c + 1] = rows(2)
        end_c[c] = both
        center_o[c] = first
        jacobi_o[0, c] = own[0]
        jacobi_o[1, c] = own[1]
        jacobi_o[2, c] = inverted
        smooth = [field[0, c] * own[0], field[1, c] * own[1],
                  jnp.where((sub == 1) | (sub == 6), rows(4), far * inverted)]
        for r in range(3):
            z_pad[r, c + 1] = smooth[r] + added[r]
        return total + (field[0, c] * smooth[0] + field[1, c] * smooth[1])

    size = chunks // GROUPS // ROWS
    for copy in halos:
        copy.wait()

    def step(k, total):
        @pl.when(lax.rem(k, size) == 0)
        def _():
            loads.wait(lax.div(k, size))

        for j in range(ROWS):
            total = chunk(k * ROWS + j, total)
        return total

    smooth_total = lax.fori_loop(0, chunks // ROWS, step, jnp.zeros((8, 128), F32))
    end_e[0] = end_e[chunks]
    faces = (chooser(east.at[0], east.at[1], end_e), chooser(north.at[0], north.at[1], end_n),
             chooser(center_o, center.at[1], end_c))
    image_total = apply_operator(z_pad, faces, 3, image_o)
    tile = moments(image_o, codes, gather, lanes)
    scalars = scalar_rows([jnp.sum(smooth_total, axis=0, keepdims=True), jnp.sum(image_total, axis=0, keepdims=True)])
    sums_o[...] = jnp.broadcast_to(jnp.concatenate([tile, scalars], axis=0)[None], sums_o.shape)


def third_kernel(parts, kept, inverse, forcing, image, codes_small, scatter, patterns, east, north, center,
                 first_center, jacobi, end_f, end_n, z_pad, image_o, sums_o, scalars_o, codes, columns):
    chunks = forcing.shape[1]
    expand(codes_small, codes)
    tile = jnp.sum(parts[...], axis=0)
    energy = jnp.sum(tile[8:9], axis=1, keepdims=True) + kept[8:9, 0:1]
    alpha = energy / jnp.sum(tile[9:10], axis=1, keepdims=True)
    sums = unpack(kept[0:8] - alpha * tile[0:8])
    coef = coarse_solve(inverse, sums)
    scalars_o[...] = scalar_rows([alpha, energy, total_of(sums * coef)])
    column_tables(coef, codes, scatter, columns)
    spread = Spread(columns, patterns)
    factor = jnp.broadcast_to(alpha, (8, 128))

    def chunk(c, total):
        added = spread.at(c)
        fields = [forcing[0, c], forcing[1, c], end_f[c]]
        for r in range(3):
            residual = fields[r] - factor * image[r, c]
            smooth = jacobi[r, c] * residual
            z_pad[r, c + 1] = smooth + added[r]
            if r < 2:
                total = total + residual * smooth
        return total

    def step(k, total):
        for j in range(ROWS):
            total = chunk(k * ROWS + j, total)
        return total

    smooth_total = lax.fori_loop(0, chunks // ROWS, step, jnp.zeros((8, 128), F32))
    faces = (chooser(east.at[0], east.at[1]), chooser(north.at[0], north.at[1], end_n), chooser(first_center, center.at[1]))
    image_total = apply_operator(z_pad, faces, 2, image_o)
    scalars = scalar_rows([jnp.sum(smooth_total, axis=0, keepdims=True), jnp.sum(image_total, axis=0, keepdims=True)])
    sums_o[...] = jnp.broadcast_to(scalars[None], sums_o.shape)


def last_kernel(parts, scalars, forcing, z_first, image_first, z_second, image_second, solution_o, residual_o,
                solution_v, residual_v, out_sems):
    chunks = forcing.shape[1]
    saves = Loads([(solution_v, solution_o), (residual_v, residual_o)], out_sems, chunks)
    tile = jnp.sum(parts[...], axis=0)
    alpha, energy = scalars[0:1, 0:1], scalars[1:2, 0:1]
    energy_next = jnp.sum(tile[0:1], axis=1, keepdims=True) + scalars[2:3, 0:1]
    beta = energy_next / energy
    alpha_next = energy_next / (jnp.sum(tile[1:2], axis=1, keepdims=True) - beta * energy_next / alpha)
    alpha, beta, alpha_next = [x.reshape(1, 1, 1) for x in (alpha, beta, alpha_next)]
    per_group = chunks // GROUPS // PIECE

    def step(k, carry):
        c = pl.multiple_of(k * PIECE, PIECE)
        part, shifted = pl.ds(c, PIECE), pl.ds(c + 1, PIECE)
        for r in range(2):
            z, image = z_first[r, shifted], image_first[r, part]
            solution_v[r, part] = alpha * z + alpha_next * (z_second[r, shifted] + beta * z)
            residual_v[r, part] = (forcing[r, part] - alpha * image) - alpha_next * (image_second[r, part] + beta * image)

        @pl.when(lax.rem(k, per_group) == per_group - 1)
        def _():
            for i in range(2):
                saves.copy(i, lax.div(k, per_group)).start()

        return carry

    lax.fori_loop(0, chunks // PIECE, step, 0)
    for group in range(GROUPS):
        saves.wait(group)


def body(forcing, east, north, storage, coarse_inverse, membership, land):
    rows, width = forcing.shape
    chunks = width // 128
    tile_rows = membership.shape[0]
    total_rows = tile_rows * TILE
    index = lax.axis_index(GY)
    start = index * rows
    info = jnp.stack([
        start % TILE // 8, index % 2, start // TILE,
        jnp.where(start + rows < total_rows, (start + rows) // TILE, -1), jnp.where(start > 0, (start - 1) // TILE, -1),
    ])
    inverse = jnp.transpose(coarse_inverse, (1, 2, 0))

    def blocked(x):
        return x.reshape(2, 8, chunks, 128).transpose(0, 2, 1, 3)

    forcing, east, north, storage = [blocked(x) for x in (forcing, east, north, storage)]
    devices = lax.axis_size(GY)
    mates = [(i, i ^ 1) for i in range(devices)]
    others = [(i, j) for i in range(devices) if (j := ((i + 1) ^ 1) - 1) in range(devices)]
    inner, outer = lax.axis_size(GY[1]) * lax.axis_size(GY[2]), lax.axis_size(GY[0])

    def call(kernel, outs, *args, scratch=()):
        places, kept_in = {"S": pltpu.SMEM, "H": pltpu.HBM}, {"V": pltpu.VMEM, "H": pltpu.HBM}
        kinds, values = [], []
        for kind, items in args:
            for x in items:
                kinds.append(kind)
                space = kept_in.get(kind)
                values.append(pltpu.with_memory_space_constraint(x, space) if space is not None else x)
        return pl.pallas_call(
            kernel,
            out_shape=[kept_in[k](s, d) if k in kept_in else jax.ShapeDtypeStruct(s, d) for k, s, d in outs],
            in_specs=[pl.BlockSpec(memory_space=places.get(k, pltpu.VMEM)) for k in kinds],
            out_specs=[pl.BlockSpec(memory_space=places.get(k, pltpu.VMEM)) for k, _, _ in outs],
            scratch_shapes=list(scratch),
            compiler_params=pltpu.CompilerParams(vmem_limit_bytes=VMEM_LIMIT),
        )(*values)

    def everywhere(copies):
        near = lax.all_to_all(copies, GY[1:], 0, 0)
        (copies,) = call(sum_kernel, [("", (outer,) + near.shape[1:], F32)], ("", [near]))
        return lax.all_to_all(copies, GY[0], 0, 0)

    own_shape, all_shape, end_shape = (2, chunks, 8, 128), (3, chunks, 8, 128), (chunks, 8, 128)
    halo, pad_shape = (6, chunks, 1, 128), (3, chunks + 2, 8, 128)
    own_v, halo_v = pltpu.VMEM(own_shape, F32), pltpu.VMEM(halo, F32)
    codes_v, columns = pltpu.VMEM((3, chunks, 128), F32), pltpu.VMEM((3, ORDER, chunks, 128), F32)

    def dma(*shape):
        return pltpu.SemaphoreType.DMA(shape)

    sums, codes, gather, scatter, lanes, patterns = call(
        moments_kernel,
        [("", (inner, 8, 128), F32), ("V", (8, membership.shape[1]), F32), ("V", (64, 128), BF16), ("V", (128, 128), BF16),
         ("V", (2, 32, 128), F32), ("V", (3, ORDER, 8, 128), F32)],
        ("S", [info]), ("H", [forcing, membership, land, *[jnp.asarray(x) for x in tables()]]),
        scratch=(own_v, codes_v, pltpu.VMEM(membership.shape, I32), pltpu.VMEM(land.shape, I32), dma(1, GROUPS), dma(7)),
    )
    parts = everywhere(sums)
    east, north, center, mate, other = call(
        faces_kernel,
        [("V", (2, chunks + 1, 8, 128), F32)] + [("V", own_shape, F32)] * 2 + [("H", halo, F32)] * 2,
        ("S", [info]), ("V", [codes]), ("H", [forcing, east, north, storage]),
        scratch=(halo_v, halo_v, codes_v) + (own_v,) * 4 + (dma(4, GROUPS), dma(2)),
    )
    mate = lax.ppermute(mate, GY, mates)
    other = lax.ppermute(other, GY, others)
    field, z_first, image_first, sums, kept, first_center, jacobi, end_f, end_n = call(
        second_kernel,
        [("V", own_shape, F32), ("V", pad_shape, F32), ("V", all_shape, F32), ("", (inner, 16, 128), F32), ("V", (16, 128), F32),
         ("V", end_shape, F32), ("V", all_shape, F32), ("V", end_shape, F32), ("V", end_shape, F32)],
        ("S", [info]), ("", [parts]), ("H", [forcing, mate, other]),
        ("V", [inverse, codes, gather, scatter, lanes, patterns, east, north, center]),
        scratch=(halo_v, halo_v, codes_v, pltpu.VMEM((chunks + 1, 8, 128), F32), pltpu.VMEM(end_shape, F32), columns,
                 dma(1, GROUPS), dma(2)),
    )
    parts = everywhere(sums)
    z_second, image_second, sums, scalars = call(
        third_kernel,
        [("V", pad_shape, F32), ("V", own_shape, F32), ("", (inner, 8, 128), F32), ("V", (8, 128), F32)],
        ("", [parts]),
        ("V", [kept, inverse, field, image_first, codes, scatter, patterns, east, north, center, first_center, jacobi, end_f, end_n]),
        scratch=(codes_v, columns),
    )
    parts = everywhere(sums)
    answer = call(
        last_kernel,
        [("H", own_shape, F32)] * 2,
        ("", [parts]), ("V", [scalars, field, z_first, image_first, z_second, image_second]),
        scratch=(own_v,) * 2 + (dma(2, GROUPS),),
    )
    return tuple(x.transpose(0, 2, 1, 3).reshape(rows, width) for x in answer)


def solution(mesh):
    finer = Mesh(mesh.devices.reshape(mesh.shape["ens"], 8, 8, 2), ("ens", "gy_0", "gy_1", "gy_2"))
    return jax.shard_map(
        body,
        mesh=finer,
        in_specs=(P(ENS_GY, None), P(GY, None), P(GY, None), P(GY, None), P(), P(), P()),
        out_specs=(P(ENS_GY, None), P(ENS_GY, None)),
        check_vma=False,
    )
```

time: 118 us -> 112 us (0.949)
  Pallas kernels: 28.8 us -> 22.3 us
    pallas_call x8, Pallas kernels: 28.8 us -> 22.3 us  [call(): pl.pallas_call(kernel, out_shape=[kept_in[k](s, d) if k in kept_in else j...]
    all_to_all x3, blocking collectives: 34.7 us -> 36.1 us  [everywhere(): near = lax.all_to_all(copies, GY[1:], 0, 0)]
  transfers between devices with their start and end apart: 2 -> 2, of which waited for: 0 -> 0; matrix products, arithmetic and copies ran while one was open for 0% -> 0% of each run, Pallas kernels for 3% -> 0%
where the time goes in v3:
time: 112 us; the launch traced here: 111 us
  blocking collectives  64.7 us (58%)
  starting transfers between devices  22.5 us (20%)
  Pallas kernels  22.3 us (20%)
    all_to_all x3, blocking collectives, everywhere(): near = lax.all_to_all(copies, GY[1:], 0, 0)  36.1 us
    all_to_all x3, blocking collectives, everywhere(): return lax.all_to_all(copies, GY[0], 0, 0)  28.6 us
    pallas_call x8, Pallas kernels, call(): pl.pallas_call(kernel, out_shape=[kept_in[k](s, d) if k in kept_in else j...  22.3 us
    ppermute x1, starting transfers between devices, body(): mate = lax.ppermute(mate, GY, mates)  20.5 us
  transfers between devices with their start and end apart: 2, of which 0 were waited for; matrix products, arithmetic and copies ran while one was open for 0% of the time, Pallas kernels for 0%

profile of v3, /device:TPU:513, one launch (start us, length us, event | category | flops | bytes accessed | tf_op | source)
XLA Modules:
  0.0 111.3 jit_solution(10859074826804729200)
XLA Ops:
  0.7 0.1 stack.23.info
  0.8 3.4 %shard_map.131 = (f32[16,8,128]{2,1,0:T(8,128)S(1)}, f32[8,256]{1,0:T(8,128)S(1)}, bf16[64,128]{1,0:T(8,128)(2,1)S(1)}, bf16[128,128]{1,0:T(8,128)(2,1)S(1)}, f3...) custom-call(s32[5]{0:T(128)S(1)} %stack.23.info, f32[2,128,8,128]{3,2,1,0:T(8,128)} %bitcast.26, ...), custom_call_target="tpu_custom_call" | custom-call | tf_op jit(solution)/shard_map/pallas_call | solution.py:474
  4.2 0.0 copy-start
  4.2 5.9 %shard_map.133 = (f32[2,129,8,128]{3,2,1,0:T(8,128)S(1)}, f32[2,128,8,128]{3,2,1,0:T(8,128)S(1)}, f32[2,128,8,128]{3,2,1,0:T(8,128)S(1)}, f32[6,128,1,128]{3,2,1,0:T(1,128)}, f32[6,128,1,128]{3,2,1,0:T(1,128)}) custom-call(s32[5]{0:T(128)S(1)} %stack.23.info, f32[8,256]{1,0:T(8,128)S(1)} %get-tuple-element.29.codes_small, f32[2,128,8,128]{3,2,1,0:T(8,128)} %bitcast.27, ...), custom_call_target="tpu_custom_call" | custom-call | tf_op jit(solution)/shard_map/pallas_call | solution.py:474
  10.1 20.5 %collective-permute-start = (f32[6,128,1,128]{3,2,1,0:T(1,128)}, f32[6,128,1,128]{3,2,1,0:T(1,128)S(1)}, u32[]{:S(2)}, u32[]{:S(2)}) collective-permute-start(f32[6,128,1,128]{3,2,1,0:T(1,128)} %get-tuple-element.30), channel_id=1, source_target_pairs={{0,1},{1,0},{2,3},{3,2},{4,5},{5,4},{6,7},{7,6},{8,9},{9,8},{10,11... | collective-permute-start | bytes 1179656 | tf_op jit(solution)/shard_map/ppermute | solution.py:510
  30.6 1.9 %collective-permute-start.1 = (f32[6,128,1,128]{3,2,1,0:T(1,128)}, f32[6,128,1,128]{3,2,1,0:T(1,128)S(1)}, u32[]{:S(2)}, u32[]{:S(2)}) collective-permute-start(f32[6,128,1,128]{3,2,1,0:T(1,128)} %get-tuple-element.31), channel_id=1, source_target_pairs={{1,2},{2,1},{3,4},{4,3},{5,6},{6,5},{7,8},{8,7},{9,10},{10,9},{11,... | collective-permute-start | bytes 1179656 | tf_op jit(solution)/shard_map/ppermute | solution.py:511
  32.5 11.0 %all_to_all.30.parts = f32[16,8,128]{2,1,0:T(8,128)S(1)} all-to-all(f32[16,8,128]{2,1,0:T(8,128)S(1)} %get-tuple-element.28), channel_id=1, replica_groups=mesh['ens'=2,'gy_0'=8,'gy_1'=8,'gy_2'=2] {'gy_1','gy_2'}, dimensions={0} | all-to-all | bytes 131072 | tf_op jit(solution)/shard_map/all_to_all | solution.py:484
  43.6 9.3 %all_to_all.31.parts = f32[8,8,128]{2,1,0:T(8,128)S(1)} all-to-all(f32[8,8,128]{2,1,0:T(8,128)S(1)} %shard_map.132), channel_id=1, replica_groups=mesh['ens'=2,'gy_0'=8,'gy_1'=8,'gy_2'=2] {'gy_0'}, dimensions={0} | all-to-all | bytes 65536 | tf_op jit(solution)/shard_map/all_to_all | solution.py:486
  52.9 0.0 collective-permute-done.mate_h
  52.9 0.0 copy-start.1
  52.9 0.0 collective-permute-done.1.other_h
  52.9 0.0 copy-start.2
  52.9 0.7 copy-done.1
  53.6 0.1 copy-done.2
  53.7 0.0 copy-done
  53.7 7.3 %shard_map.134 = (f32[2,128,8,128]{3,2,1,0:T(8,128)S(1)}, f32[3,130,8,128]{3,2,1,0:T(8,128)S(1)}, f32[3,128,8,128]{3,2,1,0:T(8,128)S(1)}, f32[16,16,128]{2,1,0:T...) custom-call(s32[5]{0:T(128)S(1)} %stack.23.info, ...), custom_call_target="tpu_custom_call" | custom-call | tf_op jit(solution)/shard_map/pallas_call | solution.py:474
  61.0 13.8 %all_to_all.32.parts = f32[16,16,128]{2,1,0:T(8,128)S(1)} all-to-all(f32[16,16,128]{2,1,0:T(8,128)S(1)} %get-tuple-element.39), channel_id=1, replica_groups=mesh['ens'=2,'gy_0'=8,'gy_1'=8,'gy_2'=2] {'gy_1','gy_2'}, dimensions={0} | all-to-all | bytes 262144 | tf_op jit(solution)/shard_map/all_to_all | solution.py:484
  74.8 10.0 %all_to_all.33.parts = f32[8,16,128]{2,1,0:T(8,128)S(1)} all-to-all(f32[8,16,128]{2,1,0:T(8,128)S(1)} %shard_map.135), channel_id=1, replica_groups=mesh['ens'=2,'gy_0'=8,'gy_1'=8,'gy_2'=2] {'gy_0'}, dimensions={0} | all-to-all | bytes 131072 | tf_op jit(solution)/shard_map/all_to_all | solution.py:486
  84.8 3.8 %shard_map.136 = (f32[3,130,8,128]{3,2,1,0:T(8,128)S(1)}, f32[2,128,8,128]{3,2,1,0:T(8,128)S(1)}, f32[16,8,128]{2,1,0:T(8,128)S(1)}, f32[8,128]{1,0:T(8,128)S(1)}) custom-call(f32[8,16,128]{2,1,0:T(8,128)S(1)} %all_to_all.33.parts, f32[16,128]{1,0:T(8,128)S(1)} %get-tuple-element.40.kept, f32[16,16,64]{2,1,0:T(8,128)S(1)} %bitcast.25, ...), custom_call_target="tpu_custom_call" | custom-call | tf_op jit(solution)/shard_map/pallas_call | solution.py:474
  88.6 11.3 %all_to_all.34.parts = f32[16,8,128]{2,1,0:T(8,128)S(1)} all-to-all(f32[16,8,128]{2,1,0:T(8,128)S(1)} %get-tuple-element.47), channel_id=1, replica_groups=mesh['ens'=2,'gy_0'=8,'gy_1'=8,'gy_2'=2] {'gy_1','gy_2'}, dimensions={0} | all-to-all | bytes 131072 | tf_op jit(solution)/shard_map/all_to_all | solution.py:484
  100.0 9.3 %all_to_all.35.parts = f32[8,8,128]{2,1,0:T(8,128)S(1)} all-to-all(f32[8,8,128]{2,1,0:T(8,128)S(1)} %shard_map.137), channel_id=1, replica_groups=mesh['ens'=2,'gy_0'=8,'gy_1'=8,'gy_2'=2] {'gy_0'}, dimensions={0} | all-to-all | bytes 65536 | tf_op jit(solution)/shard_map/all_to_all | solution.py:486
  109.3 2.0 %shard_map.138 = (f32[2,128,8,128]{3,2,1,0:T(8,128)}, f32[2,128,8,128]{3,2,1,0:T(8,128)}) custom-call(f32[8,8,128]{2,1,0:T(8,128)S(1)} %all_to_all.35.parts, f32[8,128]{1,0:T(8,128)S(1)} %get-tuple-element.48.scalars, f32[2,128,8,128]{3,2,1,0:T(8,128)S(1)} %get-tuple-element.41.forcing, f32[3,130,8,128]{3,2,1,0:T(8,128)S(1)} %get-tuple-element.49.z_first, ...), custom_call_target="tpu_custom_call" | custom-call | tf_op jit(solution)/shard_map/pallas_call | solution.py:474
  (3 shorter events, 0.1 us)
Async XLA Ops:
  4.2 49.6 %copy-start = (f32[64,16,16]{0,2,1:T(8,128)S(1)}, f32[64,16,16]{0,2,1:T(8,128)}, u32[]{:S(2)}) copy-start(f32[64,16,16]{0,2,1:T(8,128)} %param.16) | copy-start | bytes 196612
  10.1 42.8 %collective-permute-start = (f32[6,128,1,128]{3,2,1,0:T(1,128)}, f32[6,128,1,128]{3,2,1,0:T(1,128)S(1)}, u32[]{:S(2)}, u32[]{:S(2)}) collective-permute-start(f32[6,128,1,128]{3,2,1,0:T(1,128)} %get-tuple-element.30), channel_id=1, source_target_pairs={{0,1},{1,0},{2,3},{3,2},{4,5},{5,4},{6,7},{7,6},{8,9},{9,8},{10,11... | collective-permute-start | bytes 1179656 | tf_op jit(solution)/shard_map/ppermute | solution.py:510
  30.6 22.3 %collective-permute-start.1 = (f32[6,128,1,128]{3,2,1,0:T(1,128)}, f32[6,128,1,128]{3,2,1,0:T(1,128)S(1)}, u32[]{:S(2)}, u32[]{:S(2)}) collective-permute-start(f32[6,128,1,128]{3,2,1,0:T(1,128)} %get-tuple-element.31), channel_id=1, source_target_pairs={{1,2},{2,1},{3,4},{4,3},{5,6},{6,5},{7,8},{8,7},{9,10},{10,9},{11,... | collective-permute-start | bytes 1179656 | tf_op jit(solution)/shard_map/ppermute | solution.py:511
  52.9 0.7 copy-start.1
  52.9 0.9 copy-start.2

commit v4 on v3

--- a/solution.py
+++ b/solution.py
@@ -179,11 +179,12 @@
     sums_o[...] = jnp.broadcast_to(tile[None], sums_o.shape)
 
 
-def faces_kernel(info, codes_small, forcing, east, north, storage, east_o, north_o, center_o, mate_h, other_h,
-                 mate_o, other_o, codes, f_in, e_in, n_in, s_in, sems, small):
+def faces_kernel(info, codes_small, forcing, east, north, storage, east_o, north_h, center_h, mate_o, other_o,
+                 north_o, center_o, codes, f_in, e_in, n_in, s_in, sems, out_sems):
     chunks = forcing.shape[1]
     loads = Loads([(east, e_in), (north, n_in), (storage, s_in), (forcing, f_in)], sems, chunks)
     loads.start((3, 0, 1, 2))
+    saves = Loads([(north_o, north_h), (center_o, center_h)], out_sems, chunks)
     expand(codes_small, codes)
     lane, sub = iota((8, 128), 1), iota((8, 128), 0)
     odd = info[1] == 1
@@ -242,14 +243,17 @@
 
         for j in range(ROWS):
             carry = chunk(k, j, carry)
+
+        @pl.when(lax.rem(k, size) == size - 1)
+        def _():
+            for i in range(2):
+                saves.copy(i, lax.div(k, size)).start()
+
         return carry
 
     lax.fori_loop(0, chunks // ROWS, step, ([rolled(x) for x in last], first_code, first_turned))
-    saves = [pltpu.make_async_copy(x, y, small.at[i]) for i, (x, y) in enumerate([(mate_o, mate_h), (other_o, other_h)])]
-    for copy in saves:
-        copy.start()
-    for copy in saves:
-        copy.wait()
+    for group in range(GROUPS):
+        saves.wait(group)
 
 
 def apply_operator(z_pad, faces, blocks, out):
@@ -302,14 +306,11 @@
         return [sum(self.patterns[r][p] * x[p] for p in range(ORDER)) for r, x in enumerate((own, own, end))]
 
 
-def second_kernel(info, parts, forcing, mate_h, other_h, inverse, codes_small, gather, scatter, lanes, patterns, east, north, center,
-                  field, z_pad, image_o, sums_o, kept_o, center_o, jacobi_o, end_f, end_n,
-                  mate, other, codes, end_e, end_c, columns, sems, small):
+def second_kernel(info, parts, forcing, north_h, center_h, mate, other, inverse, codes_small, gather, scatter, lanes, patterns, east,
+                  field, north, center, z_pad, image_o, sums_o, kept_o, jacobi_o, end_f, end_n,
+                  codes, end_e, end_c, columns, sems):
     chunks = forcing.shape[1]
-    halos = [pltpu.make_async_copy(x, y, small.at[i]) for i, (x, y) in enumerate([(mate_h, mate), (other_h, other)])]
-    for copy in halos:
-        copy.start()
-    loads = Loads([(forcing, field)], sems, chunks)
+    loads = Loads([(forcing, field), (north_h, north), (center_h, center)], sems, chunks)
     loads.start()
     expand(codes_small, codes)
     tile = jnp.sum(parts[...], axis=0)
@@ -334,12 +335,12 @@
         first = center[0, c] + jnp.where(sub == 0, pltpu.roll(faced, 1, 0), 0.0)
         both = jnp.where(sub == 3, pltpu.roll(first, 3, 0), jnp.where(beyond == 0.0, 1.0, beyond))
         inverted = 1.0 / both
-        own = [jnp.where(sub == 0, pltpu.roll(inverted, 5, 0), 1.0 / center[0, c]), 1.0 / center[1, c]]
+        own = [jnp.where(sub == 0, pltpu.roll(inverted, 5, 0), 1.0 / first), 1.0 / center[1, c]]
         end_f[c] = far
         end_n[c] = faced
         end_e[c + 1] = rows(2)
         end_c[c] = both
-        center_o[c] = first
+        center[0, c] = first
         jacobi_o[0, c] = own[0]
         jacobi_o[1, c] = own[1]
         jacobi_o[2, c] = inverted
@@ -350,8 +351,6 @@
         return total + (field[0, c] * smooth[0] + field[1, c] * smooth[1])
 
     size = chunks // GROUPS // ROWS
-    for copy in halos:
-        copy.wait()
 
     def step(k, total):
         @pl.when(lax.rem(k, size) == 0)
@@ -365,7 +364,7 @@
     smooth_total = lax.fori_loop(0, chunks // ROWS, step, jnp.zeros((8, 128), F32))
     end_e[0] = end_e[chunks]
     faces = (chooser(east.at[0], east.at[1], end_e), chooser(north.at[0], north.at[1], end_n),
-             chooser(center_o, center.at[1], end_c))
+             chooser(center.at[0], center.at[1], end_c))
     image_total = apply_operator(z_pad, faces, 3, image_o)
     tile = moments(image_o, codes, gather, lanes)
     scalars = scalar_rows([jnp.sum(smooth_total, axis=0, keepdims=True), jnp.sum(image_total, axis=0, keepdims=True)])
@@ -373,7 +372,7 @@
 
 
 def third_kernel(parts, kept, inverse, forcing, image, codes_small, scatter, patterns, east, north, center,
-                 first_center, jacobi, end_f, end_n, z_pad, image_o, sums_o, scalars_o, codes, columns):
+                 jacobi, end_f, end_n, z_pad, image_o, sums_o, scalars_o, codes, columns):
     chunks = forcing.shape[1]
     expand(codes_small, codes)
     tile = jnp.sum(parts[...], axis=0)
@@ -403,21 +402,27 @@
         return total
 
     smooth_total = lax.fori_loop(0, chunks // ROWS, step, jnp.zeros((8, 128), F32))
-    faces = (chooser(east.at[0], east.at[1]), chooser(north.at[0], north.at[1], end_n), chooser(first_center, center.at[1]))
+    faces = (chooser(east.at[0], east.at[1]), chooser(north.at[0], north.at[1], end_n), chooser(center.at[0], center.at[1]))
     image_total = apply_operator(z_pad, faces, 2, image_o)
-    scalars = scalar_rows([jnp.sum(smooth_total, axis=0, keepdims=True), jnp.sum(image_total, axis=0, keepdims=True)])
-    sums_o[...] = jnp.broadcast_to(scalars[None], sums_o.shape)
+    smooth_row, image_row = [x + pltpu.roll(x, TILE, 1) for x in (smooth_total, image_total)]
+    packed = jnp.where(iota((8, 128), 1) < TILE, smooth_row, image_row)
+    sums_o[...] = jnp.sum(packed, axis=0, keepdims=True)
+
+
+def pair_kernel(mine, mates, out):
+    out[...] = jnp.broadcast_to((mine[...] + mates[...])[None], out.shape)
 
 
 def last_kernel(parts, scalars, forcing, z_first, image_first, z_second, image_second, solution_o, residual_o,
                 solution_v, residual_v, out_sems):
     chunks = forcing.shape[1]
     saves = Loads([(solution_v, solution_o), (residual_v, residual_o)], out_sems, chunks)
-    tile = jnp.sum(parts[...], axis=0)
+    row = jnp.sum(parts[...], axis=0)
+    left = iota(row.shape, 1) < TILE
     alpha, energy = scalars[0:1, 0:1], scalars[1:2, 0:1]
-    energy_next = jnp.sum(tile[0:1], axis=1, keepdims=True) + scalars[2:3, 0:1]
+    energy_next = jnp.sum(jnp.where(left, row, 0.0), axis=1, keepdims=True) + scalars[2:3, 0:1]
     beta = energy_next / energy
-    alpha_next = energy_next / (jnp.sum(tile[1:2], axis=1, keepdims=True) - beta * energy_next / alpha)
+    alpha_next = energy_next / (jnp.sum(jnp.where(left, 0.0, row), axis=1, keepdims=True) - beta * energy_next / alpha)
     alpha, beta, alpha_next = [x.reshape(1, 1, 1) for x in (alpha, beta, alpha_next)]
     per_group = chunks // GROUPS // PIECE
 
@@ -487,7 +492,7 @@
 
     own_shape, all_shape, end_shape = (2, chunks, 8, 128), (3, chunks, 8, 128), (chunks, 8, 128)
     halo, pad_shape = (6, chunks, 1, 128), (3, chunks + 2, 8, 128)
-    own_v, halo_v = pltpu.VMEM(own_shape, F32), pltpu.VMEM(halo, F32)
+    own_v = pltpu.VMEM(own_shape, F32)
     codes_v, columns = pltpu.VMEM((3, chunks, 128), F32), pltpu.VMEM((3, ORDER, chunks, 128), F32)
 
     def dma(*shape):
@@ -503,30 +508,32 @@
     parts = everywhere(sums)
     east, north, center, mate, other = call(
         faces_kernel,
-        [("V", (2, chunks + 1, 8, 128), F32)] + [("V", own_shape, F32)] * 2 + [("H", halo, F32)] * 2,
+        [("V", (2, chunks + 1, 8, 128), F32)] + [("H", own_shape, F32)] * 2 + [("V", halo, F32)] * 2,
         ("S", [info]), ("V", [codes]), ("H", [forcing, east, north, storage]),
-        scratch=(halo_v, halo_v, codes_v) + (own_v,) * 4 + (dma(4, GROUPS), dma(2)),
+        scratch=(own_v, own_v, codes_v) + (own_v,) * 4 + (dma(4, GROUPS), dma(2, GROUPS)),
     )
     mate = lax.ppermute(mate, GY, mates)
     other = lax.ppermute(other, GY, others)
-    field, z_first, image_first, sums, kept, first_center, jacobi, end_f, end_n = call(
+    field, north, center, z_first, image_first, sums, kept, jacobi, end_f, end_n = call(
         second_kernel,
-        [("V", own_shape, F32), ("V", pad_shape, F32), ("V", all_shape, F32), ("", (inner, 16, 128), F32), ("V", (16, 128), F32),
-         ("V", end_shape, F32), ("V", all_shape, F32), ("V", end_shape, F32), ("V", end_shape, F32)],
-        ("S", [info]), ("", [parts]), ("H", [forcing, mate, other]),
-        ("V", [inverse, codes, gather, scatter, lanes, patterns, east, north, center]),
-        scratch=(halo_v, halo_v, codes_v, pltpu.VMEM((chunks + 1, 8, 128), F32), pltpu.VMEM(end_shape, F32), columns,
-                 dma(1, GROUPS), dma(2)),
+        [("V", own_shape, F32)] * 3 + [("V", pad_shape, F32), ("V", all_shape, F32), ("", (inner, 16, 128), F32), ("V", (16, 128), F32),
+         ("V", all_shape, F32), ("V", end_shape, F32), ("V", end_shape, F32)],
+        ("S", [info]), ("", [parts]), ("H", [forcing, north, center]),
+        ("V", [mate, other, inverse, codes, gather, scatter, lanes, patterns, east]),
+        scratch=(codes_v, pltpu.VMEM((chunks + 1, 8, 128), F32), pltpu.VMEM(end_shape, F32), columns, dma(3, GROUPS)),
     )
     parts = everywhere(sums)
     z_second, image_second, sums, scalars = call(
         third_kernel,
-        [("V", pad_shape, F32), ("V", own_shape, F32), ("", (inner, 8, 128), F32), ("V", (8, 128), F32)],
+        [("V", pad_shape, F32), ("V", own_shape, F32), ("", (1, 128), F32), ("V", (8, 128), F32)],
         ("", [parts]),
-        ("V", [kept, inverse, field, image_first, codes, scatter, patterns, east, north, center, first_center, jacobi, end_f, end_n]),
+        ("V", [kept, inverse, field, image_first, codes, scatter, patterns, east, north, center, jacobi, end_f, end_n]),
         scratch=(codes_v, columns),
     )
-    parts = everywhere(sums)
+    chips = lax.axis_size(GY[:2])
+    swapped = lax.ppermute(sums, GY[2], [(0, 1), (1, 0)])
+    (sums,) = call(pair_kernel, [("", (chips, 1, 128), F32)], ("", [sums, swapped]))
+    parts = lax.all_to_all(sums, GY[:2], 0, 0)
     answer = call(
         last_kernel,
         [("H", own_shape, F32)] * 2,

time: 112 us -> 107 us (0.955)
  blocking collectives: 64.7 us -> 59.2 us
    all_to_all x0 -> x1, blocking collectives: none -> 15.5 us  [body(): parts = lax.all_to_all(sums, GY[:2], 0, 0)]
    all_to_all x3 -> x2, blocking collectives: 36.1 us -> 24.4 us  [everywhere(): near = lax.all_to_all(copies, GY[1:], 0, 0)]
    all_to_all x3 -> x2, blocking collectives: 28.6 us -> 19.3 us  [everywhere(): return lax.all_to_all(copies, GY[0], 0, 0)]
  transfers between devices with their start and end apart: 2 -> 3, of which waited for: 0 -> 1; matrix products, arithmetic and copies ran while one was open for 0% -> 0% of each run, Pallas kernels for 0% -> 0%
where the time goes in v4:
time: 107 us; the launch traced here: 106 us
  blocking collectives  59.2 us (55%)
  starting transfers between devices  23.6 us (22%)
  Pallas kernels  21.8 us (20%)
    all_to_all x2, blocking collectives, everywhere(): near = lax.all_to_all(copies, GY[1:], 0, 0)  24.4 us
    pallas_call x8, Pallas kernels, call(): pl.pallas_call(kernel, out_shape=[kept_in[k](s, d) if k in kept_in else j...  21.8 us
    ppermute x1, starting transfers between devices, body(): mate = lax.ppermute(mate, GY, mates)  20.5 us
    all_to_all x2, blocking collectives, everywhere(): return lax.all_to_all(copies, GY[0], 0, 0)  19.3 us
    all_to_all x1, blocking collectives, body(): parts = lax.all_to_all(sums, GY[:2], 0, 0)  15.5 us
  transfers between devices with their start and end apart: 3, of which 1 were waited for; matrix products, arithmetic and copies ran while one was open for 0% of the time, Pallas kernels for 0%

profile of v4, /device:TPU:513, one launch (start us, length us, event | category | flops | bytes accessed | tf_op | source)
XLA Modules:
  0.0 106.3 jit_solution(9435470390305293699)
XLA Ops:
  0.7 0.1 stack.23.info
  0.8 3.4 %shard_map.131 = (f32[16,8,128]{2,1,0:T(8,128)S(1)}, f32[8,256]{1,0:T(8,128)S(1)}, bf16[64,128]{1,0:T(8,128)(2,1)S(1)}, bf16[128,128]{1,0:T(8,128)(2,1)S(1)}, f3...) custom-call(s32[5]{0:T(128)S(1)} %stack.23.info, f32[2,128,8,128]{3,2,1,0:T(8,128)} %bitcast.26, ...), custom_call_target="tpu_custom_call" | custom-call | tf_op jit(solution)/shard_map/pallas_call | solution.py:479
  4.2 0.0 copy-start
  4.2 5.8 %shard_map.133 = (f32[2,129,8,128]{3,2,1,0:T(8,128)S(1)}, f32[2,128,8,128]{3,2,1,0:T(8,128)}, f32[2,128,8,128]{3,2,1,0:T(8,128)}, f32[6,128,1,128]{3,2,1,0:T(1,128)S(1)}, f32[6,128,1,128]{3,2,1,0:T(1,128)S(1)}) custom-call(s32[5]{0:T(128)S(1)} %stack.23.info, f32[8,256]{1,0:T(8,128)S(1)} %get-tuple-element.30.codes_small, f32[2,128,8,128]{3,2,1,0:T(8,128)} %bitcast.27, ...), custom_call_target="tpu_custom_call" | custom-call | tf_op jit(solution)/shard_map/pallas_call | solution.py:479
  9.9 20.5 %collective-permute-start = (f32[6,128,1,128]{3,2,1,0:T(1,128)S(1)}, f32[6,128,1,128]{3,2,1,0:T(1,128)S(1)}, u32[]{:S(2)}, u32[]{:S(2)}) collective-permute-start(f32[6,128,1,128]{3,2,1,0:T(1,128)S(1)} %get-tuple-element.33), channel_id=1, source_target_pairs={{0,1},{1,0},{2,3},{3,2},{4,5},{5,4},{6,7},{7,6},{8,9},{9,8},{10,11... | collective-permute-start | bytes 1179656 | tf_op jit(solution)/shard_map/ppermute | solution.py:515
  30.5 1.9 %collective-permute-start.1 = (f32[6,128,1,128]{3,2,1,0:T(1,128)S(1)}, f32[6,128,1,128]{3,2,1,0:T(1,128)S(1)}, u32[]{:S(2)}, u32[]{:S(2)}) collective-permute-start(f32[6,128,1,128]{3,2,1,0:T(1,128)S(1)} %get-tuple-element.34), channel_id=1, source_target_pairs={{1,2},{2,1},{3,4},{4,3},{5,6},{6,5},{7,8},{8,7},{9,10},{10,9},{11,... | collective-permute-start | bytes 1179656 | tf_op jit(solution)/shard_map/ppermute | solution.py:516
  32.4 10.9 %all_to_all.25.parts = f32[16,8,128]{2,1,0:T(8,128)S(1)} all-to-all(f32[16,8,128]{2,1,0:T(8,128)S(1)} %get-tuple-element.29), channel_id=1, replica_groups=mesh['ens'=2,'gy_0'=8,'gy_1'=8,'gy_2'=2] {'gy_1','gy_2'}, dimensions={0} | all-to-all | bytes 131072 | tf_op jit(solution)/shard_map/all_to_all | solution.py:489
  43.3 9.3 %all_to_all.26.parts = f32[8,8,128]{2,1,0:T(8,128)S(1)} all-to-all(f32[8,8,128]{2,1,0:T(8,128)S(1)} %shard_map.132), channel_id=1, replica_groups=mesh['ens'=2,'gy_0'=8,'gy_1'=8,'gy_2'=2] {'gy_0'}, dimensions={0} | all-to-all | bytes 65536 | tf_op jit(solution)/shard_map/all_to_all | solution.py:491
  52.6 0.0 collective-permute-done.mate
  52.6 0.0 collective-permute-done.1.other
  52.6 0.0 copy-done
  52.7 6.8 %shard_map.134 = (f32[2,128,8,128]{3,2,1,0:T(8,128)S(1)}, f32[2,128,8,128]{3,2,1,0:T(8,128)S(1)}, f32[2,128,8,128]{3,2,1,0:T(8,128)S(1)}, f32[3,130,8,128]{3,2,1...) custom-call(s32[5]{0:T(128)S(1)} %stack.23.info, ...), custom_call_target="tpu_custom_call" | custom-call | tf_op jit(solution)/shard_map/pallas_call | solution.py:479
  59.5 13.5 %all_to_all.27.parts = f32[16,16,128]{2,1,0:T(8,128)S(1)} all-to-all(f32[16,16,128]{2,1,0:T(8,128)S(1)} %get-tuple-element.40), channel_id=1, replica_groups=mesh['ens'=2,'gy_0'=8,'gy_1'=8,'gy_2'=2] {'gy_1','gy_2'}, dimensions={0} | all-to-all | bytes 262144 | tf_op jit(solution)/shard_map/all_to_all | solution.py:489
  73.0 10.0 %all_to_all.28.parts = f32[8,16,128]{2,1,0:T(8,128)S(1)} all-to-all(f32[8,16,128]{2,1,0:T(8,128)S(1)} %shard_map.135), channel_id=1, replica_groups=mesh['ens'=2,'gy_0'=8,'gy_1'=8,'gy_2'=2] {'gy_0'}, dimensions={0} | all-to-all | bytes 131072 | tf_op jit(solution)/shard_map/all_to_all | solution.py:491
  83.0 3.8 %shard_map.136 = (f32[3,130,8,128]{3,2,1,0:T(8,128)S(1)}, f32[2,128,8,128]{3,2,1,0:T(8,128)S(1)}, f32[1,128]{1,0:T(1,128)S(1)}, f32[8,128]{1,0:T(8,128)S(1)}) custom-call(f32[8,16,128]{2,1,0:T(8,128)S(1)} %all_to_all.28.parts, f32[16,128]{1,0:T(8,128)S(1)} %get-tuple-element.41.kept, f32[16,16,64]{2,1,0:T(8,128)S(1)} %bitcast.25, ...), custom_call_target="tpu_custom_call" | custom-call | tf_op jit(solution)/shard_map/pallas_call | solution.py:479
  86.8 1.1 %collective-permute-start.2 = (f32[1,128]{1,0:T(1,128)S(1)}, f32[1,128]{1,0:T(1,128)S(1)}, u32[]{:S(2)}, u32[]{:S(2)}) collective-permute-start(f32[1,128]{1,0:T(1,128)S(1)} %get-tuple-element.49.mine), channel_id=1, source_target_pairs={{0,1},{1,0},{2,3},{3,2},{4,5},{5,4},{6,7},{7,6},{8,9},{9,8},{10,11... | collective-permute-start | bytes 1544 | tf_op jit(solution)/shard_map/ppermute | solution.py:534
  87.9 0.8 collective-permute-done.2.mates
  88.7 15.5 %all_to_all.29.parts = f32[64,1,128]{2,1,0:T(1,128)S(1)} all-to-all(f32[64,1,128]{2,1,0:T(1,128)S(1)} %shard_map.137), channel_id=1, replica_groups=mesh['ens'=2,'gy_0'=8,'gy_1'=8,'gy_2'=2] {'gy_0','gy_1'}, dimensions={0} | all-to-all | bytes 65536 | tf_op jit(solution)/shard_map/all_to_all | solution.py:536
  104.3 2.0 %shard_map.138 = (f32[2,128,8,128]{3,2,1,0:T(8,128)}, f32[2,128,8,128]{3,2,1,0:T(8,128)}) custom-call(f32[64,1,128]{2,1,0:T(1,128)S(1)} %all_to_all.29.parts, f32[8,128]{1,0:T(8,128)S(1)} %get-tuple-element.50.scalars, f32[2,128,8,128]{3,2,1,0:T(8,128)S(1)} %get-tuple-element.42.forcing, f32[3,130,8,128]{3,2,1,0:T(8,128)S(1)} %get-tuple-element.51.z_first, ...), custom_call_target="tpu_custom_call" | custom-call | tf_op jit(solution)/shard_map/pallas_call | solution.py:479
  (3 shorter events, 0.1 us)
Async XLA Ops:
  4.2 48.5 %copy-start = (f32[64,16,16]{0,2,1:T(8,128)S(1)}, f32[64,16,16]{0,2,1:T(8,128)}, u32[]{:S(2)}) copy-start(f32[64,16,16]{0,2,1:T(8,128)} %param.16) | copy-start | bytes 196612
  9.9 42.7 %collective-permute-start = (f32[6,128,1,128]{3,2,1,0:T(1,128)S(1)}, f32[6,128,1,128]{3,2,1,0:T(1,128)S(1)}, u32[]{:S(2)}, u32[]{:S(2)}) collective-permute-start(f32[6,128,1,128]{3,2,1,0:T(1,128)S(1)} %get-tuple-element.33), channel_id=1, source_target_pairs={{0,1},{1,0},{2,3},{3,2},{4,5},{5,4},{6,7},{7,6},{8,9},{9,8},{10,11... | collective-permute-start | bytes 1179656 | tf_op jit(solution)/shard_map/ppermute | solution.py:515
  30.5 22.2 %collective-permute-start.1 = (f32[6,128,1,128]{3,2,1,0:T(1,128)S(1)}, f32[6,128,1,128]{3,2,1,0:T(1,128)S(1)}, u32[]{:S(2)}, u32[]{:S(2)}) collective-permute-start(f32[6,128,1,128]{3,2,1,0:T(1,128)S(1)} %get-tuple-element.34), channel_id=1, source_target_pairs={{1,2},{2,1},{3,4},{4,3},{5,6},{6,5},{7,8},{8,7},{9,10},{10,9},{11,... | collective-permute-start | bytes 1179656 | tf_op jit(solution)/shard_map/ppermute | solution.py:516
  86.8 1.9 %collective-permute-start.2 = (f32[1,128]{1,0:T(1,128)S(1)}, f32[1,128]{1,0:T(1,128)S(1)}, u32[]{:S(2)}, u32[]{:S(2)}) collective-permute-start(f32[1,128]{1,0:T(1,128)S(1)} %get-tuple-element.49.mine), channel_id=1, source_target_pairs={{0,1},{1,0},{2,3},{3,2},{4,5},{5,4},{6,7},{7,6},{8,9},{9,8},{10,11... | collective-permute-start | bytes 1544 | tf_op jit(solution)/shard_map/ppermute | solution.py:534

commit v5 on v4

--- a/solution.py
+++ b/solution.py
@@ -127,8 +127,14 @@
             out[row, p] = columns[p * codes.shape[1] : (p + 1) * codes.shape[1]]
 
 
-def sum_kernel(parts, out):
-    out[...] = jnp.broadcast_to(jnp.sum(parts[...], axis=0)[None], out.shape)
+def two_sums(left, right):
+    left, right = [x + pltpu.roll(x, TILE, 1) for x in (left, right)]
+    return jnp.sum(jnp.where(iota((8, 128), 1) < TILE, left, right), axis=0, keepdims=True)
+
+
+def sums_of(row):
+    left = iota(row.shape, 1) < TILE
+    return [jnp.sum(jnp.where(x, row, 0.0), axis=1, keepdims=True) for x in (left, jnp.logical_not(left))]
 
 
 def scalar_rows(values):
@@ -176,7 +182,7 @@
         codes_o[k : k + 1] = jnp.where(dry, TILE, member_in[row]).astype(F32)
     expand(codes_o, codes)
     tile = moments(field, codes, gather_o, lanes_o, loads.wait)
-    sums_o[...] = jnp.broadcast_to(tile[None], sums_o.shape)
+    sums_o[...] = tile
 
 
 def faces_kernel(info, codes_small, forcing, east, north, storage, east_o, north_h, center_h, mate_o, other_o,
@@ -367,17 +373,21 @@
              chooser(center.at[0], center.at[1], end_c))
     image_total = apply_operator(z_pad, faces, 3, image_o)
     tile = moments(image_o, codes, gather, lanes)
-    scalars = scalar_rows([jnp.sum(smooth_total, axis=0, keepdims=True), jnp.sum(image_total, axis=0, keepdims=True)])
-    sums_o[...] = jnp.broadcast_to(jnp.concatenate([tile, scalars], axis=0)[None], sums_o.shape)
+    for k in range(8):
+        sums_o[k] = tile[k : k + 1]
+    sums_o[8] = two_sums(smooth_total, image_total)
 
 
 def third_kernel(parts, kept, inverse, forcing, image, codes_small, scatter, patterns, east, north, center,
-                 jacobi, end_f, end_n, z_pad, image_o, sums_o, scalars_o, codes, columns):
+                 jacobi, end_f, end_n, z_pad, image_o, sums_o, scalars_o, codes, columns, tile):
     chunks = forcing.shape[1]
     expand(codes_small, codes)
-    tile = jnp.sum(parts[...], axis=0)
-    energy = jnp.sum(tile[8:9], axis=1, keepdims=True) + kept[8:9, 0:1]
-    alpha = energy / jnp.sum(tile[9:10], axis=1, keepdims=True)
+    rows = jnp.sum(parts[...], axis=0)
+    for k in range(9):
+        tile[k : k + 1] = rows[k]
+    energy, image_energy = sums_of(tile[8:9])
+    energy = energy + kept[8:9, 0:1]
+    alpha = energy / image_energy
     sums = unpack(kept[0:8] - alpha * tile[0:8])
     coef = coarse_solve(inverse, sums)
     scalars_o[...] = scalar_rows([alpha, energy, total_of(sums * coef)])
@@ -404,9 +414,7 @@
     smooth_total = lax.fori_loop(0, chunks // ROWS, step, jnp.zeros((8, 128), F32))
     faces = (chooser(east.at[0], east.at[1]), chooser(north.at[0], north.at[1], end_n), chooser(center.at[0], center.at[1]))
     image_total = apply_operator(z_pad, faces, 2, image_o)
-    smooth_row, image_row = [x + pltpu.roll(x, TILE, 1) for x in (smooth_total, image_total)]
-    packed = jnp.where(iota((8, 128), 1) < TILE, smooth_row, image_row)
-    sums_o[...] = jnp.sum(packed, axis=0, keepdims=True)
+    sums_o[...] = two_sums(smooth_total, image_total)
 
 
 def pair_kernel(mine, mates, out):
@@ -417,12 +425,11 @@
                 solution_v, residual_v, out_sems):
     chunks = forcing.shape[1]
     saves = Loads([(solution_v, solution_o), (residual_v, residual_o)], out_sems, chunks)
-    row = jnp.sum(parts[...], axis=0)
-    left = iota(row.shape, 1) < TILE
+    energy_next, image_energy = sums_of(jnp.sum(parts[...], axis=0))
     alpha, energy = scalars[0:1, 0:1], scalars[1:2, 0:1]
-    energy_next = jnp.sum(jnp.where(left, row, 0.0), axis=1, keepdims=True) + scalars[2:3, 0:1]
+    energy_next = energy_next + scalars[2:3, 0:1]
     beta = energy_next / energy
-    alpha_next = energy_next / (jnp.sum(jnp.where(left, 0.0, row), axis=1, keepdims=True) - beta * energy_next / alpha)
+    alpha_next = energy_next / (image_energy - beta * energy_next / alpha)
     alpha, beta, alpha_next = [x.reshape(1, 1, 1) for x in (alpha, beta, alpha_next)]
     per_group = chunks // GROUPS // PIECE
 
@@ -466,7 +473,6 @@
     devices = lax.axis_size(GY)
     mates = [(i, i ^ 1) for i in range(devices)]
     others = [(i, j) for i in range(devices) if (j := ((i + 1) ^ 1) - 1) in range(devices)]
-    inner, outer = lax.axis_size(GY[1]) * lax.axis_size(GY[2]), lax.axis_size(GY[0])
 
     def call(kernel, outs, *args, scratch=()):
         places, kept_in = {"S": pltpu.SMEM, "H": pltpu.HBM}, {"V": pltpu.VMEM, "H": pltpu.HBM}
@@ -485,10 +491,10 @@
             compiler_params=pltpu.CompilerParams(vmem_limit_bytes=VMEM_LIMIT),
         )(*values)
 
-    def everywhere(copies):
-        near = lax.all_to_all(copies, GY[1:], 0, 0)
-        (copies,) = call(sum_kernel, [("", (outer,) + near.shape[1:], F32)], ("", [near]))
-        return lax.all_to_all(copies, GY[0], 0, 0)
+    def everywhere(mine):
+        mates = lax.ppermute(mine, GY[2], [(0, 1), (1, 0)])
+        (copies,) = call(pair_kernel, [("V", (lax.axis_size(GY[:2]),) + mine.shape, F32)], ("", [mine, mates]))
+        return lax.all_to_all(copies, GY[:2], 0, 0)
 
     own_shape, all_shape, end_shape = (2, chunks, 8, 128), (3, chunks, 8, 128), (chunks, 8, 128)
     halo, pad_shape = (6, chunks, 1, 128), (3, chunks + 2, 8, 128)
@@ -500,7 +506,7 @@
 
     sums, codes, gather, scatter, lanes, patterns = call(
         moments_kernel,
-        [("", (inner, 8, 128), F32), ("V", (8, membership.shape[1]), F32), ("V", (64, 128), BF16), ("V", (128, 128), BF16),
+        [("", (8, 128), F32), ("V", (8, membership.shape[1]), F32), ("V", (64, 128), BF16), ("V", (128, 128), BF16),
          ("V", (2, 32, 128), F32), ("V", (3, ORDER, 8, 128), F32)],
         ("S", [info]), ("H", [forcing, membership, land, *[jnp.asarray(x) for x in tables()]]),
         scratch=(own_v, codes_v, pltpu.VMEM(membership.shape, I32), pltpu.VMEM(land.shape, I32), dma(1, GROUPS), dma(7)),
@@ -516,7 +522,7 @@
     other = lax.ppermute(other, GY, others)
     field, north, center, z_first, image_first, sums, kept, jacobi, end_f, end_n = call(
         second_kernel,
-        [("V", own_shape, F32)] * 3 + [("V", pad_shape, F32), ("V", all_shape, F32), ("", (inner, 16, 128), F32), ("V", (16, 128), F32),
+        [("V", own_shape, F32)] * 3 + [("V", pad_shape, F32), ("V", all_shape, F32), ("", (9, 1, 128), F32), ("V", (16, 128), F32),
          ("V", all_shape, F32), ("V", end_shape, F32), ("V", end_shape, F32)],
         ("S", [info]), ("", [parts]), ("H", [forcing, north, center]),
         ("V", [mate, other, inverse, codes, gather, scatter, lanes, patterns, east]),
@@ -528,12 +534,9 @@
         [("V", pad_shape, F32), ("V", own_shape, F32), ("", (1, 128), F32), ("V", (8, 128), F32)],
         ("", [parts]),
         ("V", [kept, inverse, field, image_first, codes, scatter, patterns, east, north, center, jacobi, end_f, end_n]),
-        scratch=(codes_v, columns),
+        scratch=(codes_v, columns, pltpu.VMEM((16, 128), F32)),
     )
-    chips = lax.axis_size(GY[:2])
-    swapped = lax.ppermute(sums, GY[2], [(0, 1), (1, 0)])
-    (sums,) = call(pair_kernel, [("", (chips, 1, 128), F32)], ("", [sums, swapped]))
-    parts = lax.all_to_all(sums, GY[:2], 0, 0)
+    parts = everywhere(sums)
     answer = call(
         last_kernel,
         [("H", own_shape, F32)] * 2,

time: 107 us -> 108 us (level)
  blocking collectives: 59.2 us -> 41.8 us
  waiting for transfers between devices: 0.82 us -> 10 us
  starting transfers between devices: 23.6 us -> 32.5 us
  Pallas kernels: 21.8 us -> 22.9 us
    ppermute x1 -> x3, starting transfers between devices: 1.09 us -> 23.7 us  [everywhere(): mates = lax.ppermute(mine, GY[2], [(0, 1), (1, 0)])]
    ppermute x1, starting transfers between devices: 20.5 us -> 0.47 us  [body(): mate = lax.ppermute(mate, GY, mates)]
    all_to_all x5 -> x2, blocking collectives: 59.2 us -> 41.8 us  [everywhere(): return lax.all_to_all(copies, GY[:2], 0, 0)]
    ppermute x1, waiting for transfers between devices: 0.01 us -> 7.24 us  [body(): other = lax.ppermute(other, GY, others)]
    all_to_all x0 -> x1, starting transfers between devices: none -> 6.47 us  [everywhere(): return lax.all_to_all(copies, GY[:2], 0, 0)]
    ppermute x1 -> x3, waiting for transfers between devices: 0.82 us -> 2.78 us  [everywhere(): mates = lax.ppermute(mine, GY[2], [(0, 1), (1, 0)])]
    pallas_call x8, Pallas kernels: 21.8 us -> 22.9 us  [call(): pl.pallas_call(kernel, out_shape=[kept_in[k](s, d) if k in kept_in else j...]
  transfers between devices with their start and end apart: 3 -> 6, of which waited for: 1 -> 4; matrix products, arithmetic and copies ran while one was open for 0% -> 0% of each run, Pallas kernels for 0% -> 5%
where the time goes in v5:
time: 108 us
  blocking collectives  41.8 us (39%)
  starting transfers between devices  32.5 us (30%)
  Pallas kernels  22.9 us (21%)
  waiting for transfers between devices  10 us (9%)
    all_to_all x2, blocking collectives, everywhere(): return lax.all_to_all(copies, GY[:2], 0, 0)  41.8 us
    ppermute x3, starting transfers between devices, everywhere(): mates = lax.ppermute(mine, GY[2], [(0, 1), (1, 0)])  23.7 us
    pallas_call x8, Pallas kernels, call(): pl.pallas_call(kernel, out_shape=[kept_in[k](s, d) if k in kept_in else j...  22.9 us
    ppermute x1, waiting for transfers between devices, body(): other = lax.ppermute(other, GY, others)  7.24 us
    all_to_all x1, starting transfers between devices, everywhere(): return lax.all_to_all(copies, GY[:2], 0, 0)  6.47 us
    ppermute x3, waiting for transfers between devices, everywhere(): mates = lax.ppermute(mine, GY[2], [(0, 1), (1, 0)])  2.78 us
  transfers between devices with their start and end apart: 6, of which 4 were waited for; matrix products, arithmetic and copies ran while one was open for 0% of the time, Pallas kernels for 5%

profile of v5, /device:TPU:513, one launch (start us, length us, event | category | flops | bytes accessed | tf_op | source)
XLA Modules:
  0.0 108.1 jit_solution(10304368922838557858)
XLA Ops:
  0.7 0.1 stack.23.info
  0.8 3.4 %shard_map.131 = (f32[8,128]{1,0:T(8,128)S(1)}, f32[8,256]{1,0:T(8,128)S(1)}, bf16[64,128]{1,0:T(8,128)(2,1)S(1)}, bf16[128,128]{1,0:T(8,128)(2,1)S(1)}, f32[2,3...) custom-call(s32[5]{0:T(128)S(1)} %stack.23.info, f32[2,128,8,128]{3,2,1,0:T(8,128)} %bitcast.26, s32[32,256]{1,0:T(8,128)} %membership.1, ...), custom_call_target="tpu_custom_call" | custom-call | tf_op jit(solution)/shard_map/pallas_call | solution.py:485
  4.2 20.5 %collective-permute-start = (f32[8,128]{1,0:T(8,128)S(1)}, f32[8,128]{1,0:T(8,128)S(1)}, u32[]{:S(2)}, u32[]{:S(2)}) collective-permute-start(f32[8,128]{1,0:T(8,128)S(1)} %get-tuple-element.29.mine), channel_id=1, source_target_pairs={{0,1},{1,0},{2,3},{3,2},{4,5},{5,4},{6,7},{7,6},{8,9},{9,8},{10,11... | collective-permute-start | bytes 12296 | tf_op jit(solution)/shard_map/ppermute | solution.py:495
  24.7 0.8 collective-permute-done.mates
  25.5 0.7 shard_map.132
  26.2 6.5 %all-to-all-start = ((f32[64,8,128]{2,1,0:T(8,128)}), f32[64,8,128]{2,1,0:T(8,128)S(1)}, u32[]{:S(2)}, u32[]{:S(2)}) async-start(f32[64,8,128]{2,1,0:T(8,128)} %shard_map.132), calls=%async_computation | async-start | bytes 524288 | tf_op jit(solution)/shard_map/all_to_all | solution.py:497
  32.7 0.0 copy-start
  32.7 5.8 %shard_map.133 = (f32[2,129,8,128]{3,2,1,0:T(8,128)S(1)}, f32[2,128,8,128]{3,2,1,0:T(8,128)}, f32[2,128,8,128]{3,2,1,0:T(8,128)}, f32[6,128,1,128]{3,2,1,0:T(1,128)S(1)}, f32[6,128,1,128]{3,2,1,0:T(1,128)S(1)}) custom-call(s32[5]{0:T(128)S(1)} %stack.23.info, f32[8,256]{1,0:T(8,128)S(1)} %get-tuple-element.30.codes_small, f32[2,128,8,128]{3,2,1,0:T(8,128)} %bitcast.27, ...), custom_call_target="tpu_custom_call" | custom-call | tf_op jit(solution)/shard_map/pallas_call | solution.py:485
  38.5 0.5 collective-permute-start.1
  38.9 1.9 %collective-permute-start.2 = (f32[6,128,1,128]{3,2,1,0:T(1,128)S(1)}, f32[6,128,1,128]{3,2,1,0:T(1,128)S(1)}, u32[]{:S(2)}, u32[]{:S(2)}) collective-permute-start(f32[6,128,1,128]{3,2,1,0:T(1,128)S(1)} %get-tuple-element.34), channel_id=1, source_target_pairs={{1,2},{2,1},{3,4},{4,3},{5,6},{6,5},{7,8},{8,7},{9,10},{10,9},{11,... | collective-permute-start | bytes 1179656 | tf_op jit(solution)/shard_map/ppermute | solution.py:522
  40.9 0.0 collective-permute-done.1.mate
  40.9 7.2 %collective-permute-done.2.other = f32[6,128,1,128]{3,2,1,0:T(1,128)S(1)} collective-permute-done((f32[6,128,1,128]{3,2,1,0:T(1,128)S(1)}, f32[6,128,1,128]{3,2,1,0:T(1,128)S(1)}, u32[]{:S(2)}, u32[]{:S(2)}) %collective-permute-start.2) | collective-permute-done | bytes 393248 | tf_op jit(solution)/shard_map/ppermute | solution.py:522
  48.1 0.0 all-to-all-done.parts
  48.1 0.0 copy-done
  48.2 6.9 %shard_map.134 = (f32[2,128,8,128]{3,2,1,0:T(8,128)S(1)}, f32[2,128,8,128]{3,2,1,0:T(8,128)S(1)}, f32[2,128,8,128]{3,2,1,0:T(8,128)S(1)}, f32[3,130,8,128]{3,2,1...) custom-call(s32[5]{0:T(128)S(1)} %stack.23.info, ...), custom_call_target="tpu_custom_call" | custom-call | tf_op jit(solution)/shard_map/pallas_call | solution.py:485
  55.0 0.1 collective-permute-start.3
  55.2 1.1 %collective-permute-done.3.mates = f32[9,1,128]{2,1,0:T(1,128)S(1)} collective-permute-done((f32[9,1,128]{2,1,0:T(1,128)S(1)}, f32[9,1,128]{2,1,0:T(1,128)S(1)}, u32[]{:S(2)}, u32[]{:S(2)}) %collective-permute-start.3) | collective-permute-done | bytes 4640 | tf_op jit(solution)/shard_map/ppermute | solution.py:495
  56.3 0.2 shard_map.135
  56.5 26.2 %all_to_all.15.parts = f32[64,9,1,128]{3,2,1,0:T(1,128)S(1)} all-to-all(f32[64,9,1,128]{3,2,1,0:T(1,128)S(1)} %shard_map.135), channel_id=1, replica_groups=mesh['ens'=2,'gy_0'=8,'gy_1'=8,'gy_2'=2] {'gy_0','gy_1'}, dimensions={0} | all-to-all | bytes 589824 | tf_op jit(solution)/shard_map/all_to_all | solution.py:497
  82.7 4.0 %shard_map.136 = (f32[3,130,8,128]{3,2,1,0:T(8,128)S(1)}, f32[2,128,8,128]{3,2,1,0:T(8,128)S(1)}, f32[1,128]{1,0:T(1,128)S(1)}, f32[8,128]{1,0:T(8,128)S(1)}) custom-call(f32[64,9,1,128]{3,2,1,0:T(1,128)S(1)} %all_to_all.15.parts, f32[16,128]{1,0:T(8,128)S(1)} %get-tuple-element.41.kept, f32[16,16,64]{2,1,0:T(8,128)S(1)} %bitcast.25, ...), custom_call_target="tpu_custom_call" | custom-call | tf_op jit(solution)/shard_map/pallas_call | solution.py:485
  86.7 3.0 %collective-permute-start.4 = (f32[1,128]{1,0:T(1,128)S(1)}, f32[1,128]{1,0:T(1,128)S(1)}, u32[]{:S(2)}, u32[]{:S(2)}) collective-permute-start(f32[1,128]{1,0:T(1,128)S(1)} %get-tuple-element.49.mine), channel_id=1, source_target_pairs={{0,1},{1,0},{2,3},{3,2},{4,5},{5,4},{6,7},{7,6},{8,9},{9,8},{10,11... | collective-permute-start | bytes 1544 | tf_op jit(solution)/shard_map/ppermute | solution.py:495
  89.7 0.8 collective-permute-done.4.mates
  90.6 15.5 %all_to_all.16.parts = f32[64,1,128]{2,1,0:T(1,128)S(1)} all-to-all(f32[64,1,128]{2,1,0:T(1,128)S(1)} %shard_map.137), channel_id=1, replica_groups=mesh['ens'=2,'gy_0'=8,'gy_1'=8,'gy_2'=2] {'gy_0','gy_1'}, dimensions={0} | all-to-all | bytes 65536 | tf_op jit(solution)/shard_map/all_to_all | solution.py:497
  106.1 2.0 %shard_map.138 = (f32[2,128,8,128]{3,2,1,0:T(8,128)}, f32[2,128,8,128]{3,2,1,0:T(8,128)}) custom-call(f32[64,1,128]{2,1,0:T(1,128)S(1)} %all_to_all.16.parts, f32[8,128]{1,0:T(8,128)S(1)} %get-tuple-element.50.scalars, f32[2,128,8,128]{3,2,1,0:T(8,128)S(1)} %get-tuple-element.42.forcing, f32[3,130,8,128]{3,2,1,0:T(8,128)S(1)} %get-tuple-element.51.z_first, ...), custom_call_target="tpu_custom_call" | custom-call | tf_op jit(solution)/shard_map/pallas_call | solution.py:485
  (1 shorter events, 0.0 us)
Async XLA Ops:
  4.2 21.3 %collective-permute-start = (f32[8,128]{1,0:T(8,128)S(1)}, f32[8,128]{1,0:T(8,128)S(1)}, u32[]{:S(2)}, u32[]{:S(2)}) collective-permute-start(f32[8,128]{1,0:T(8,128)S(1)} %get-tuple-element.29.mine), channel_id=1, source_target_pairs={{0,1},{1,0},{2,3},{3,2},{4,5},{5,4},{6,7},{7,6},{8,9},{9,8},{10,11... | collective-permute-start | bytes 12296 | tf_op jit(solution)/shard_map/ppermute | solution.py:495
  26.2 21.9 %all-to-all-start = ((f32[64,8,128]{2,1,0:T(8,128)}), f32[64,8,128]{2,1,0:T(8,128)S(1)}, u32[]{:S(2)}, u32[]{:S(2)}) async-start(f32[64,8,128]{2,1,0:T(8,128)} %shard_map.132), calls=%async_computation | async-start | bytes 524288 | tf_op jit(solution)/shard_map/all_to_all | solution.py:497
  32.7 15.4 %copy-start = (f32[64,16,16]{0,2,1:T(8,128)S(1)}, f32[64,16,16]{0,2,1:T(8,128)}, u32[]{:S(2)}) copy-start(f32[64,16,16]{0,2,1:T(8,128)} %param.16) | copy-start | bytes 196612
  38.5 2.4 %collective-permute-start.1 = (f32[6,128,1,128]{3,2,1,0:T(1,128)S(1)}, f32[6,128,1,128]{3,2,1,0:T(1,128)S(1)}, u32[]{:S(2)}, u32[]{:S(2)}) collective-permute-start(f32[6,128,1,128]{3,2,1,0:T(1,128)S(1)} %get-tuple-element.33), channel_id=1, source_target_pairs={{0,1},{1,0},{2,3},{3,2},{4,5},{5,4},{6,7},{7,6},{8,9},{9,8},{10,11... | collective-permute-start | bytes 1179656 | tf_op jit(solution)/shard_map/ppermute | solution.py:521
  38.9 9.2 %collective-permute-start.2 = (f32[6,128,1,128]{3,2,1,0:T(1,128)S(1)}, f32[6,128,1,128]{3,2,1,0:T(1,128)S(1)}, u32[]{:S(2)}, u32[]{:S(2)}) collective-permute-start(f32[6,128,1,128]{3,2,1,0:T(1,128)S(1)} %get-tuple-element.34), channel_id=1, source_target_pairs={{1,2},{2,1},{3,4},{4,3},{5,6},{6,5},{7,8},{8,7},{9,10},{10,9},{11,... | collective-permute-start | bytes 1179656 | tf_op jit(solution)/shard_map/ppermute | solution.py:522
  55.0 1.3 %collective-permute-start.3 = (f32[9,1,128]{2,1,0:T(1,128)S(1)}, f32[9,1,128]{2,1,0:T(1,128)S(1)}, u32[]{:S(2)}, u32[]{:S(2)}) collective-permute-start(f32[9,1,128]{2,1,0:T(1,128)S(1)} %get-tuple-element.40.mine), channel_id=1, source_target_pairs={{0,1},{1,0},{2,3},{3,2},{4,5},{5,4},{6,7},{7,6},{8,9},{9,8},{10,11... | collective-permute-start | bytes 13832 | tf_op jit(solution)/shard_map/ppermute | solution.py:495
  86.7 3.8 %collective-permute-start.4 = (f32[1,128]{1,0:T(1,128)S(1)}, f32[1,128]{1,0:T(1,128)S(1)}, u32[]{:S(2)}, u32[]{:S(2)}) collective-permute-start(f32[1,128]{1,0:T(1,128)S(1)} %get-tuple-element.49.mine), channel_id=1, source_target_pairs={{0,1},{1,0},{2,3},{3,2},{4,5},{5,4},{6,7},{7,6},{8,9},{9,8},{10,11... | collective-permute-start | bytes 1544 | tf_op jit(solution)/shard_map/ppermute | solution.py:495

commit v6 on v4

--- a/solution.py
+++ b/solution.py
@@ -13,10 +13,11 @@
 GY = ("gy_0", "gy_1", "gy_2")
 ENS_GY = ("ens", "gy_0", "gy_1", "gy_2")
 F32, BF16, I32 = jnp.float32, jnp.bfloat16, jnp.int32
-ROWS = 8
-PIECE = 8
+ROWS = 32
+PIECE = 32
 BLOCK = 32
 GROUPS = 4
+HALVES = 2
 VMEM_LIMIT = 24 * 2**20
 
 
@@ -30,7 +31,7 @@
     cols = (mode[q_of][:, lane % TILE] * (half[:, None] == lane[None, :] // TILE)).astype(np.float32)
     high = cols.astype(BF16)
     low = (cols - high.astype(np.float32)).astype(BF16)
-    gather = np.concatenate([high, low], axis=0)
+    gather = np.concatenate([np.concatenate([high, high], axis=1), np.concatenate([low, np.zeros_like(low)], axis=1)], axis=0)
     scatter = np.concatenate([high, high, low, np.zeros_like(low)], axis=0)
     rows = mode[p_of].reshape(32, 8, 8).transpose(1, 0, 2).astype(np.float32)
     row_lanes = np.tile(rows, (1, 1, 16))
@@ -75,23 +76,21 @@
         out[k] = dot_nn(jnp.where(mine, codes_small[k : k + 1], 0.0).astype(BF16), halves)
 
 
-def moments(field, codes, gather, lanes, ready=None):
+def moments(field, codes, gather, lanes, loads=None):
     wide = [jnp.concatenate([lanes[r]] * (BLOCK * 8 // 128), axis=1) for r in range(2)]
 
-    def step(k, total):
-        first = pl.multiple_of(k * BLOCK, BLOCK)
-        if ready is not None:
-            ready(k)
+    total = jnp.zeros((32, 128), F32)
+    for k in range(codes.shape[1] // BLOCK):
+        first = k * BLOCK
+        if loads is not None and first % loads.size == 0:
+            loads.wait(first // loads.size)
         lifted = jnp.zeros((32, BLOCK * 8), F32)
         for r in range(2):
-            high, low = split(field[r, pl.ds(first, BLOCK)].reshape(BLOCK * 8, 128))
-            both = dot_nt(gather[...], high)
-            lifted = lifted + wide[r] * (both[:32] + both[32:] + dot_nt(gather[0:32], low))
+            both = dot_nt(gather[...], jnp.concatenate(split(field[r, pl.ds(first, BLOCK)].reshape(BLOCK * 8, 128)), axis=1))
+            lifted = lifted + wide[r] * (both[:32] + both[32:])
         own = onehot(jnp.concatenate([spread_row(codes.at[0], first + j) for j in range(BLOCK)], axis=0))
         parts = dot_nn(jnp.concatenate(split(lifted), axis=0), own)
-        return total + parts[:32] + parts[32:]
-
-    total = lax.fori_loop(0, codes.shape[1] // BLOCK, step, jnp.zeros((32, 128), F32))
+        total = total + parts[:32] + parts[32:]
     sums = total[:16] + pltpu.roll(total[16:], TILE, 1)
     return jnp.where(iota((8, 128), 1) < TILE, sums[:8], pltpu.roll(sums[8:], TILE, 1))
 
@@ -139,16 +138,16 @@
 
 
 class Loads:
-    def __init__(self, pairs, sems, chunks):
-        self.pairs, self.sems, self.size = pairs, sems, chunks // GROUPS
+    def __init__(self, pairs, sems, chunks, groups=GROUPS):
+        self.pairs, self.sems, self.size, self.groups = pairs, sems, chunks // groups, groups
 
     def copy(self, i, group):
         source, target = self.pairs[i]
         part = pl.ds(pl.multiple_of(group * self.size, self.size), self.size)
         return pltpu.make_async_copy(source.at[:, part], target.at[:, part], self.sems.at[i, group])
 
-    def start(self, groups=range(GROUPS)):
-        for group in groups:
+    def start(self, order=None):
+        for group in range(self.groups) if order is None else order:
             for i in range(len(self.pairs)):
                 self.copy(i, group).start()
 
@@ -166,7 +165,7 @@
     copies = [pltpu.make_async_copy(x, y, small.at[i]) for i, (x, y) in enumerate(pairs)]
     for copy in copies:
         copy.start()
-    loads = Loads([(forcing, field)], sems, chunks)
+    loads = Loads([(forcing, field)], sems, chunks, HALVES)
     loads.start()
     for copy in copies:
         copy.wait()
@@ -175,7 +174,7 @@
         dry = (land_in[row] == 1) | (info[2 + k] < 0)
         codes_o[k : k + 1] = jnp.where(dry, TILE, member_in[row]).astype(F32)
     expand(codes_o, codes)
-    tile = moments(field, codes, gather_o, lanes_o, loads.wait)
+    tile = moments(field, codes, gather_o, lanes_o, loads)
     sums_o[...] = jnp.broadcast_to(tile[None], sums_o.shape)
 
 
@@ -487,7 +486,7 @@
 
     def everywhere(copies):
         near = lax.all_to_all(copies, GY[1:], 0, 0)
-        (copies,) = call(sum_kernel, [("", (outer,) + near.shape[1:], F32)], ("", [near]))
+        (copies,) = call(sum_kernel, [("V", (outer,) + near.shape[1:], F32)], ("V", [near]))
         return lax.all_to_all(copies, GY[0], 0, 0)
 
     own_shape, all_shape, end_shape = (2, chunks, 8, 128), (3, chunks, 8, 128), (chunks, 8, 128)
@@ -500,10 +499,10 @@
 
     sums, codes, gather, scatter, lanes, patterns = call(
         moments_kernel,
-        [("", (inner, 8, 128), F32), ("V", (8, membership.shape[1]), F32), ("V", (64, 128), BF16), ("V", (128, 128), BF16),
+        [("", (inner, 8, 128), F32), ("V", (8, membership.shape[1]), F32), ("V", (64, 256), BF16), ("V", (128, 128), BF16),
          ("V", (2, 32, 128), F32), ("V", (3, ORDER, 8, 128), F32)],
         ("S", [info]), ("H", [forcing, membership, land, *[jnp.asarray(x) for x in tables()]]),
-        scratch=(own_v, codes_v, pltpu.VMEM(membership.shape, I32), pltpu.VMEM(land.shape, I32), dma(1, GROUPS), dma(7)),
+        scratch=(own_v, codes_v, pltpu.VMEM(membership.shape, I32), pltpu.VMEM(land.shape, I32), dma(1, HALVES), dma(7)),
     )
     parts = everywhere(sums)
     east, north, center, mate, other = call(
@@ -516,28 +515,28 @@
     other = lax.ppermute(other, GY, others)
     field, north, center, z_first, image_first, sums, kept, jacobi, end_f, end_n = call(
         second_kernel,
-        [("V", own_shape, F32)] * 3 + [("V", pad_shape, F32), ("V", all_shape, F32), ("", (inner, 16, 128), F32), ("V", (16, 128), F32),
+        [("V", own_shape, F32)] * 3 + [("V", pad_shape, F32), ("V", all_shape, F32), ("V", (inner, 16, 128), F32), ("V", (16, 128), F32),
          ("V", all_shape, F32), ("V", end_shape, F32), ("V", end_shape, F32)],
-        ("S", [info]), ("", [parts]), ("H", [forcing, north, center]),
+        ("S", [info]), ("V", [parts]), ("H", [forcing, north, center]),
         ("V", [mate, other, inverse, codes, gather, scatter, lanes, patterns, east]),
         scratch=(codes_v, pltpu.VMEM((chunks + 1, 8, 128), F32), pltpu.VMEM(end_shape, F32), columns, dma(3, GROUPS)),
     )
     parts = everywhere(sums)
     z_second, image_second, sums, scalars = call(
         third_kernel,
-        [("V", pad_shape, F32), ("V", own_shape, F32), ("", (1, 128), F32), ("V", (8, 128), F32)],
-        ("", [parts]),
+        [("V", pad_shape, F32), ("V", own_shape, F32), ("V", (1, 128), F32), ("V", (8, 128), F32)],
+        ("V", [parts]),
         ("V", [kept, inverse, field, image_first, codes, scatter, patterns, east, north, center, jacobi, end_f, end_n]),
         scratch=(codes_v, columns),
     )
     chips = lax.axis_size(GY[:2])
     swapped = lax.ppermute(sums, GY[2], [(0, 1), (1, 0)])
-    (sums,) = call(pair_kernel, [("", (chips, 1, 128), F32)], ("", [sums, swapped]))
+    (sums,) = call(pair_kernel, [("V", (chips, 1, 128), F32)], ("V", [sums, swapped]))
     parts = lax.all_to_all(sums, GY[:2], 0, 0)
     answer = call(
         last_kernel,
         [("H", own_shape, F32)] * 2,
-        ("", [parts]), ("V", [scalars, field, z_first, image_first, z_second, image_second]),
+        ("V", [parts]), ("V", [scalars, field, z_first, image_first, z_second, image_second]),
         scratch=(own_v,) * 2 + (dma(2, GROUPS),),
     )
     return tuple(x.transpose(0, 2, 1, 3).reshape(rows, width) for x in answer)

time: 107 us -> 103 us (0.963)
  Pallas kernels: 21.8 us -> 17.7 us
    pallas_call x8, Pallas kernels: 21.8 us -> 17.7 us  [call(): pl.pallas_call(kernel, out_shape=[kept_in[k](s, d) if k in kept_in else j...]
where the time goes in v6:
time: 103 us; the launch traced here: 102 us
  blocking collectives  59.2 us (57%)
  starting transfers between devices  23.6 us (23%)
  Pallas kernels  17.7 us (17%)
    all_to_all x2, blocking collectives, everywhere(): near = lax.all_to_all(copies, GY[1:], 0, 0)  24.4 us
    ppermute x1, starting transfers between devices, body(): mate = lax.ppermute(mate, GY, mates)  20.5 us
    all_to_all x2, blocking collectives, everywhere(): return lax.all_to_all(copies, GY[0], 0, 0)  19.3 us
    pallas_call x8, Pallas kernels, call(): pl.pallas_call(kernel, out_shape=[kept_in[k](s, d) if k in kept_in else j...  17.7 us
    all_to_all x1, blocking collectives, body(): parts = lax.all_to_all(sums, GY[:2], 0, 0)  15.5 us
  transfers between devices with their start and end apart: 3, of which 1 were waited for; matrix products, arithmetic and copies ran while one was open for 0% of the time, Pallas kernels for 0%

profile of v6, /device:TPU:513, one launch (start us, length us, event | category | flops | bytes accessed | tf_op | source)
XLA Modules:
  0.0 102.2 jit_solution(553138275322230189)
XLA Ops:
  0.7 0.1 stack.23.info
  0.8 3.0 %shard_map.131 = (f32[16,8,128]{2,1,0:T(8,128)S(1)}, f32[8,256]{1,0:T(8,128)S(1)}, bf16[64,256]{1,0:T(8,128)(2,1)S(1)}, bf16[128,128]{1,0:T(8,128)(2,1)S(1)}, f3...) custom-call(s32[5]{0:T(128)S(1)} %stack.23.info, f32[2,128,8,128]{3,2,1,0:T(8,128)} %bitcast.26, ...), custom_call_target="tpu_custom_call" | custom-call | tf_op jit(solution)/shard_map/pallas_call | solution.py:478
  3.8 0.0 copy-start
  3.8 4.2 %shard_map.133 = (f32[2,129,8,128]{3,2,1,0:T(8,128)S(1)}, f32[2,128,8,128]{3,2,1,0:T(8,128)}, f32[2,128,8,128]{3,2,1,0:T(8,128)}, f32[6,128,1,128]{3,2,1,0:T(1,128)S(1)}, f32[6,128,1,128]{3,2,1,0:T(1,128)S(1)}) custom-call(s32[5]{0:T(128)S(1)} %stack.23.info, f32[8,256]{1,0:T(8,128)S(1)} %get-tuple-element.30.codes_small, f32[2,128,8,128]{3,2,1,0:T(8,128)} %bitcast.27, ...), custom_call_target="tpu_custom_call" | custom-call | tf_op jit(solution)/shard_map/pallas_call | solution.py:478
  8.0 20.5 %collective-permute-start = (f32[6,128,1,128]{3,2,1,0:T(1,128)S(1)}, f32[6,128,1,128]{3,2,1,0:T(1,128)S(1)}, u32[]{:S(2)}, u32[]{:S(2)}) collective-permute-start(f32[6,128,1,128]{3,2,1,0:T(1,128)S(1)} %get-tuple-element.33), channel_id=1, source_target_pairs={{0,1},{1,0},{2,3},{3,2},{4,5},{5,4},{6,7},{7,6},{8,9},{9,8},{10,11... | collective-permute-start | bytes 1179656 | tf_op jit(solution)/shard_map/ppermute | solution.py:514
  28.6 1.9 %collective-permute-start.1 = (f32[6,128,1,128]{3,2,1,0:T(1,128)S(1)}, f32[6,128,1,128]{3,2,1,0:T(1,128)S(1)}, u32[]{:S(2)}, u32[]{:S(2)}) collective-permute-start(f32[6,128,1,128]{3,2,1,0:T(1,128)S(1)} %get-tuple-element.34), channel_id=1, source_target_pairs={{1,2},{2,1},{3,4},{4,3},{5,6},{6,5},{7,8},{8,7},{9,10},{10,9},{11,... | collective-permute-start | bytes 1179656 | tf_op jit(solution)/shard_map/ppermute | solution.py:515
  30.5 10.9 %all_to_all.25.parts = f32[16,8,128]{2,1,0:T(8,128)S(1)} all-to-all(f32[16,8,128]{2,1,0:T(8,128)S(1)} %get-tuple-element.29), channel_id=1, replica_groups=mesh['ens'=2,'gy_0'=8,'gy_1'=8,'gy_2'=2] {'gy_1','gy_2'}, dimensions={0} | all-to-all | bytes 131072 | tf_op jit(solution)/shard_map/all_to_all | solution.py:488
  41.5 9.3 %all_to_all.26.parts = f32[8,8,128]{2,1,0:T(8,128)S(1)} all-to-all(f32[8,8,128]{2,1,0:T(8,128)S(1)} %shard_map.132), channel_id=1, replica_groups=mesh['ens'=2,'gy_0'=8,'gy_1'=8,'gy_2'=2] {'gy_0'}, dimensions={0} | all-to-all | bytes 65536 | tf_op jit(solution)/shard_map/all_to_all | solution.py:490
  50.8 0.0 collective-permute-done.mate
  50.8 0.0 collective-permute-done.1.other
  50.8 0.0 copy-done
  50.8 5.7 %shard_map.134 = (f32[2,128,8,128]{3,2,1,0:T(8,128)S(1)}, f32[2,128,8,128]{3,2,1,0:T(8,128)S(1)}, f32[2,128,8,128]{3,2,1,0:T(8,128)S(1)}, f32[3,130,8,128]{3,2,1...) custom-call(s32[5]{0:T(128)S(1)} %stack.23.info, ...), custom_call_target="tpu_custom_call" | custom-call | tf_op jit(solution)/shard_map/pallas_call | solution.py:478
  56.5 13.5 %all_to_all.27.parts = f32[16,16,128]{2,1,0:T(8,128)S(1)} all-to-all(f32[16,16,128]{2,1,0:T(8,128)S(1)} %get-tuple-element.40), channel_id=1, replica_groups=mesh['ens'=2,'gy_0'=8,'gy_1'=8,'gy_2'=2] {'gy_1','gy_2'}, dimensions={0} | all-to-all | bytes 262144 | tf_op jit(solution)/shard_map/all_to_all | solution.py:488
  70.0 10.0 %all_to_all.28.parts = f32[8,16,128]{2,1,0:T(8,128)S(1)} all-to-all(f32[8,16,128]{2,1,0:T(8,128)S(1)} %shard_map.135), channel_id=1, replica_groups=mesh['ens'=2,'gy_0'=8,'gy_1'=8,'gy_2'=2] {'gy_0'}, dimensions={0} | all-to-all | bytes 131072 | tf_op jit(solution)/shard_map/all_to_all | solution.py:490
  80.0 3.0 %shard_map.136 = (f32[3,130,8,128]{3,2,1,0:T(8,128)S(1)}, f32[2,128,8,128]{3,2,1,0:T(8,128)S(1)}, f32[1,128]{1,0:T(1,128)S(1)}, f32[8,128]{1,0:T(8,128)S(1)}) custom-call(f32[8,16,128]{2,1,0:T(8,128)S(1)} %all_to_all.28.parts, f32[16,128]{1,0:T(8,128)S(1)} %get-tuple-element.41.kept, f32[16,16,64]{2,1,0:T(8,128)S(1)} %bitcast.25, ...), custom_call_target="tpu_custom_call" | custom-call | tf_op jit(solution)/shard_map/pallas_call | solution.py:478
  83.0 1.1 %collective-permute-start.2 = (f32[1,128]{1,0:T(1,128)S(1)}, f32[1,128]{1,0:T(1,128)S(1)}, u32[]{:S(2)}, u32[]{:S(2)}) collective-permute-start(f32[1,128]{1,0:T(1,128)S(1)} %get-tuple-element.49.mine), channel_id=1, source_target_pairs={{0,1},{1,0},{2,3},{3,2},{4,5},{5,4},{6,7},{7,6},{8,9},{9,8},{10,11... | collective-permute-start | bytes 1544 | tf_op jit(solution)/shard_map/ppermute | solution.py:533
  84.1 0.8 collective-permute-done.2.mates
  84.9 15.5 %all_to_all.29.parts = f32[64,1,128]{2,1,0:T(1,128)S(1)} all-to-all(f32[64,1,128]{2,1,0:T(1,128)S(1)} %shard_map.137), channel_id=1, replica_groups=mesh['ens'=2,'gy_0'=8,'gy_1'=8,'gy_2'=2] {'gy_0','gy_1'}, dimensions={0} | all-to-all | bytes 65536 | tf_op jit(solution)/shard_map/all_to_all | solution.py:535
  100.5 1.7 %shard_map.138 = (f32[2,128,8,128]{3,2,1,0:T(8,128)}, f32[2,128,8,128]{3,2,1,0:T(8,128)}) custom-call(f32[64,1,128]{2,1,0:T(1,128)S(1)} %all_to_all.29.parts, f32[8,128]{1,0:T(8,128)S(1)} %get-tuple-element.50.scalars, f32[2,128,8,128]{3,2,1,0:T(8,128)S(1)} %get-tuple-element.42.forcing, f32[3,130,8,128]{3,2,1,0:T(8,128)S(1)} %get-tuple-element.51.z_first, ...), custom_call_target="tpu_custom_call" | custom-call | tf_op jit(solution)/shard_map/pallas_call | solution.py:478
  (3 shorter events, 0.1 us)
Async XLA Ops:
  3.8 46.9 %copy-start = (f32[64,16,16]{0,2,1:T(8,128)S(1)}, f32[64,16,16]{0,2,1:T(8,128)}, u32[]{:S(2)}) copy-start(f32[64,16,16]{0,2,1:T(8,128)} %param.16) | copy-start | bytes 196612
  8.0 42.7 %collective-permute-start = (f32[6,128,1,128]{3,2,1,0:T(1,128)S(1)}, f32[6,128,1,128]{3,2,1,0:T(1,128)S(1)}, u32[]{:S(2)}, u32[]{:S(2)}) collective-permute-start(f32[6,128,1,128]{3,2,1,0:T(1,128)S(1)} %get-tuple-element.33), channel_id=1, source_target_pairs={{0,1},{1,0},{2,3},{3,2},{4,5},{5,4},{6,7},{7,6},{8,9},{9,8},{10,11... | collective-permute-start | bytes 1179656 | tf_op jit(solution)/shard_map/ppermute | solution.py:514
  28.6 22.2 %collective-permute-start.1 = (f32[6,128,1,128]{3,2,1,0:T(1,128)S(1)}, f32[6,128,1,128]{3,2,1,0:T(1,128)S(1)}, u32[]{:S(2)}, u32[]{:S(2)}) collective-permute-start(f32[6,128,1,128]{3,2,1,0:T(1,128)S(1)} %get-tuple-element.34), channel_id=1, source_target_pairs={{1,2},{2,1},{3,4},{4,3},{5,6},{6,5},{7,8},{8,7},{9,10},{10,9},{11,... | collective-permute-start | bytes 1179656 | tf_op jit(solution)/shard_map/ppermute | solution.py:515
  83.0 1.9 %collective-permute-start.2 = (f32[1,128]{1,0:T(1,128)S(1)}, f32[1,128]{1,0:T(1,128)S(1)}, u32[]{:S(2)}, u32[]{:S(2)}) collective-permute-start(f32[1,128]{1,0:T(1,128)S(1)} %get-tuple-element.49.mine), channel_id=1, source_target_pairs={{0,1},{1,0},{2,3},{3,2},{4,5},{5,4},{6,7},{7,6},{8,9},{9,8},{10,11... | collective-permute-start | bytes 1544 | tf_op jit(solution)/shard_map/ppermute | solution.py:533

commit v7 on v6

--- a/solution.py
+++ b/solution.py
@@ -156,10 +156,19 @@
             self.copy(i, group).wait()
 
 
-def moments_kernel(info, forcing, membership, land, gather, scatter, row_lanes, row_subs, ends,
+def position(membership):
+    rows, total_rows = 2 * 8, membership.shape[0] * TILE
+    index = lax.axis_index(GY)
+    start = index * rows
+    after = jnp.where(start + rows < total_rows, lax.div(start + rows, TILE), -1)
+    before = jnp.where(start > 0, lax.div(start - 1, TILE), -1)
+    return lax.div(lax.rem(start, TILE), 8), (lax.div(start, TILE), after, before)
+
+
+def moments_kernel(forcing, membership, land, gather, scatter, row_lanes, row_subs, ends,
                    sums_o, codes_o, gather_o, scatter_o, lanes_o, patterns_o, field, codes, member_in, land_in, sems, small):
     chunks = forcing.shape[1]
-    block = info[0]
+    block, tile_rows = position(membership)
     pairs = [(membership, member_in), (land, land_in), (gather, gather_o), (row_lanes.at[pl.ds(block, 2)], lanes_o),
              (scatter, scatter_o), (row_subs.at[pl.ds(block, 2)], patterns_o.at[0:2]), (ends.at[lax.div(block, 2)], patterns_o.at[2])]
     copies = [pltpu.make_async_copy(x, y, small.at[i]) for i, (x, y) in enumerate(pairs)]
@@ -170,15 +179,15 @@
     for copy in copies:
         copy.wait()
     for k in range(3):
-        row = pl.ds(jnp.maximum(info[2 + k], 0), 1)
-        dry = (land_in[row] == 1) | (info[2 + k] < 0)
+        row = pl.ds(jnp.maximum(tile_rows[k], 0), 1)
+        dry = (land_in[row] == 1) | (tile_rows[k] < 0)
         codes_o[k : k + 1] = jnp.where(dry, TILE, member_in[row]).astype(F32)
     expand(codes_o, codes)
     tile = moments(field, codes, gather_o, lanes_o, loads)
     sums_o[...] = jnp.broadcast_to(tile[None], sums_o.shape)
 
 
-def faces_kernel(info, codes_small, forcing, east, north, storage, east_o, north_h, center_h, mate_o, other_o,
+def faces_kernel(codes_small, forcing, east, north, storage, east_o, north_h, center_h, mate_o, other_o,
                  north_o, center_o, codes, f_in, e_in, n_in, s_in, sems, out_sems):
     chunks = forcing.shape[1]
     loads = Loads([(east, e_in), (north, n_in), (storage, s_in), (forcing, f_in)], sems, chunks)
@@ -186,7 +195,7 @@
     saves = Loads([(north_o, north_h), (center_o, center_h)], out_sems, chunks)
     expand(codes_small, codes)
     lane, sub = iota((8, 128), 1), iota((8, 128), 0)
-    odd = info[1] == 1
+    odd = lax.rem(lax.axis_index(GY), 2) == 1
 
     def rolled(x):
         return pltpu.roll(x, 1, 1)
@@ -305,7 +314,7 @@
         return [sum(self.patterns[r][p] * x[p] for p in range(ORDER)) for r, x in enumerate((own, own, end))]
 
 
-def second_kernel(info, parts, forcing, north_h, center_h, mate, other, inverse, codes_small, gather, scatter, lanes, patterns, east,
+def second_kernel(parts, forcing, north_h, center_h, mate, other, inverse, codes_small, gather, scatter, lanes, patterns, east,
                   field, north, center, z_pad, image_o, sums_o, kept_o, jacobi_o, end_f, end_n,
                   codes, end_e, end_c, columns, sems):
     chunks = forcing.shape[1]
@@ -320,7 +329,7 @@
     column_tables(coef, codes, scatter, columns)
     spread = Spread(columns, patterns)
     sub = iota((8, 128), 0)
-    after = jnp.logical_xor(sub < 4, info[1] == 1)
+    after = jnp.logical_xor(sub < 4, lax.rem(lax.axis_index(GY), 2) == 1)
 
     def chunk(c, total):
         added = spread.at(c)
@@ -448,14 +457,6 @@
 def body(forcing, east, north, storage, coarse_inverse, membership, land):
     rows, width = forcing.shape
     chunks = width // 128
-    tile_rows = membership.shape[0]
-    total_rows = tile_rows * TILE
-    index = lax.axis_index(GY)
-    start = index * rows
-    info = jnp.stack([
-        start % TILE // 8, index % 2, start // TILE,
-        jnp.where(start + rows < total_rows, (start + rows) // TILE, -1), jnp.where(start > 0, (start - 1) // TILE, -1),
-    ])
     inverse = jnp.transpose(coarse_inverse, (1, 2, 0))
 
     def blocked(x):
@@ -468,7 +469,7 @@
     inner, outer = lax.axis_size(GY[1]) * lax.axis_size(GY[2]), lax.axis_size(GY[0])
 
     def call(kernel, outs, *args, scratch=()):
-        places, kept_in = {"S": pltpu.SMEM, "H": pltpu.HBM}, {"V": pltpu.VMEM, "H": pltpu.HBM}
+        places, kept_in = {"H": pltpu.HBM}, {"V": pltpu.VMEM, "H": pltpu.HBM}
         kinds, values = [], []
         for kind, items in args:
             for x in items:
@@ -501,14 +502,14 @@
         moments_kernel,
         [("", (inner, 8, 128), F32), ("V", (8, membership.shape[1]), F32), ("V", (64, 256), BF16), ("V", (128, 128), BF16),
          ("V", (2, 32, 128), F32), ("V", (3, ORDER, 8, 128), F32)],
-        ("S", [info]), ("H", [forcing, membership, land, *[jnp.asarray(x) for x in tables()]]),
+        ("H", [forcing, membership, land, *[jnp.asarray(x) for x in tables()]]),
         scratch=(own_v, codes_v, pltpu.VMEM(membership.shape, I32), pltpu.VMEM(land.shape, I32), dma(1, HALVES), dma(7)),
     )
     parts = everywhere(sums)
     east, north, center, mate, other = call(
         faces_kernel,
         [("V", (2, chunks + 1, 8, 128), F32)] + [("H", own_shape, F32)] * 2 + [("V", halo, F32)] * 2,
-        ("S", [info]), ("V", [codes]), ("H", [forcing, east, north, storage]),
+        ("V", [codes]), ("H", [forcing, east, north, storage]),
         scratch=(own_v, own_v, codes_v) + (own_v,) * 4 + (dma(4, GROUPS), dma(2, GROUPS)),
     )
     mate = lax.ppermute(mate, GY, mates)
@@ -517,7 +518,7 @@
         second_kernel,
         [("V", own_shape, F32)] * 3 + [("V", pad_shape, F32), ("V", all_shape, F32), ("V", (inner, 16, 128), F32), ("V", (16, 128), F32),
          ("V", all_shape, F32), ("V", end_shape, F32), ("V", end_shape, F32)],
-        ("S", [info]), ("V", [parts]), ("H", [forcing, north, center]),
+        ("V", [parts]), ("H", [forcing, north, center]),
         ("V", [mate, other, inverse, codes, gather, scatter, lanes, patterns, east]),
         scratch=(codes_v, pltpu.VMEM((chunks + 1, 8, 128), F32), pltpu.VMEM(end_shape, F32), columns, dma(3, GROUPS)),
     )

time: 103 us -> 101 us (0.981)
  Pallas kernels: 17.7 us -> 16.5 us
    pallas_call x8, Pallas kernels: 17.7 us -> 16.5 us  [call(): pl.pallas_call(kernel, out_shape=[kept_in[k](s, d) if k in kept_in else j...]
where the time goes in v7:
time: 101 us
  blocking collectives  59.2 us (59%)
  starting transfers between devices  23.6 us (23%)
  Pallas kernels  16.5 us (16%)
    all_to_all x2, blocking collectives, everywhere(): near = lax.all_to_all(copies, GY[1:], 0, 0)  24.4 us
    ppermute x1, starting transfers between devices, body(): mate = lax.ppermute(mate, GY, mates)  20.5 us
    all_to_all x2, blocking collectives, everywhere(): return lax.all_to_all(copies, GY[0], 0, 0)  19.3 us
    pallas_call x8, Pallas kernels, call(): pl.pallas_call(kernel, out_shape=[kept_in[k](s, d) if k in kept_in else j...  16.5 us
    all_to_all x1, blocking collectives, body(): parts = lax.all_to_all(sums, GY[:2], 0, 0)  15.5 us
  transfers between devices with their start and end apart: 3, of which 1 were waited for; matrix products, arithmetic and copies ran while one was open for 0% of the time, Pallas kernels for 0%

profile of v7, /device:TPU:513, one launch (start us, length us, event | category | flops | bytes accessed | tf_op | source)
XLA Modules:
  0.0 100.8 jit_solution(4248404727664763037)
XLA Ops:
  0.6 2.7 %shard_map.131 = (f32[16,8,128]{2,1,0:T(8,128)S(1)}, f32[8,256]{1,0:T(8,128)S(1)}, bf16[64,256]{1,0:T(8,128)(2,1)S(1)}, bf16[128,128]{1,0:T(8,128)(2,1)S(1)}, f3...) custom-call(f32[2,128,8,128]{3,2,1,0:T(8,128)} %bitcast.21, s32[32,256]{1,0:T(8,128)} %membership.1, ...), custom_call_target="tpu_custom_call" | custom-call | tf_op jit(solution)/shard_map/pallas_call | solution.py:479
  3.3 0.0 copy-start
  3.3 3.7 %shard_map.133 = (f32[2,129,8,128]{3,2,1,0:T(8,128)S(1)}, f32[2,128,8,128]{3,2,1,0:T(8,128)}, f32[2,128,8,128]{3,2,1,0:T(8,128)}, f32[6,128,1,128]{3,2,1,0:T(1,128)S(1)}, f32[6,128,1,128]{3,2,1,0:T(1,128)S(1)}) custom-call(f32[8,256]{1,0:T(8,128)S(1)} %get-tuple-element.30.codes_small, f32[2,128,8,128]{3,2,1,0:T(8,128)} %bitcast.22, ...), custom_call_target="tpu_custom_call" | custom-call | tf_op jit(solution)/shard_map/pallas_call | solution.py:479
  7.1 20.5 %collective-permute-start = (f32[6,128,1,128]{3,2,1,0:T(1,128)S(1)}, f32[6,128,1,128]{3,2,1,0:T(1,128)S(1)}, u32[]{:S(2)}, u32[]{:S(2)}) collective-permute-start(f32[6,128,1,128]{3,2,1,0:T(1,128)S(1)} %get-tuple-element.33), channel_id=1, source_target_pairs={{0,1},{1,0},{2,3},{3,2},{4,5},{5,4},{6,7},{7,6},{8,9},{9,8},{10,11... | collective-permute-start | bytes 1179656 | tf_op jit(solution)/shard_map/ppermute | solution.py:515
  27.6 1.9 %collective-permute-start.1 = (f32[6,128,1,128]{3,2,1,0:T(1,128)S(1)}, f32[6,128,1,128]{3,2,1,0:T(1,128)S(1)}, u32[]{:S(2)}, u32[]{:S(2)}) collective-permute-start(f32[6,128,1,128]{3,2,1,0:T(1,128)S(1)} %get-tuple-element.34), channel_id=1, source_target_pairs={{1,2},{2,1},{3,4},{4,3},{5,6},{6,5},{7,8},{8,7},{9,10},{10,9},{11,... | collective-permute-start | bytes 1179656 | tf_op jit(solution)/shard_map/ppermute | solution.py:516
  29.5 10.9 %all_to_all.25.parts = f32[16,8,128]{2,1,0:T(8,128)S(1)} all-to-all(f32[16,8,128]{2,1,0:T(8,128)S(1)} %get-tuple-element.29), channel_id=1, replica_groups=mesh['ens'=2,'gy_0'=8,'gy_1'=8,'gy_2'=2] {'gy_1','gy_2'}, dimensions={0} | all-to-all | bytes 131072 | tf_op jit(solution)/shard_map/all_to_all | solution.py:489
  40.5 9.3 %all_to_all.26.parts = f32[8,8,128]{2,1,0:T(8,128)S(1)} all-to-all(f32[8,8,128]{2,1,0:T(8,128)S(1)} %shard_map.132), channel_id=1, replica_groups=mesh['ens'=2,'gy_0'=8,'gy_1'=8,'gy_2'=2] {'gy_0'}, dimensions={0} | all-to-all | bytes 65536 | tf_op jit(solution)/shard_map/all_to_all | solution.py:491
  49.8 0.0 collective-permute-done.mate
  49.8 0.0 collective-permute-done.1.other
  49.8 0.0 copy-done
  49.8 5.3 %shard_map.134 = (f32[2,128,8,128]{3,2,1,0:T(8,128)S(1)}, f32[2,128,8,128]{3,2,1,0:T(8,128)S(1)}, f32[2,128,8,128]{3,2,1,0:T(8,128)S(1)}, f32[3,130,8,128]{3,2,1...) custom-call(f32[8,8,128]{2,1,0:T(8,128)S(1)} %all_to_all.26.parts, ...), custom_call_target="tpu_custom_call" | custom-call | tf_op jit(solution)/shard_map/pallas_call | solution.py:479
  55.1 13.5 %all_to_all.27.parts = f32[16,16,128]{2,1,0:T(8,128)S(1)} all-to-all(f32[16,16,128]{2,1,0:T(8,128)S(1)} %get-tuple-element.40), channel_id=1, replica_groups=mesh['ens'=2,'gy_0'=8,'gy_1'=8,'gy_2'=2] {'gy_1','gy_2'}, dimensions={0} | all-to-all | bytes 262144 | tf_op jit(solution)/shard_map/all_to_all | solution.py:489
  68.6 10.0 %all_to_all.28.parts = f32[8,16,128]{2,1,0:T(8,128)S(1)} all-to-all(f32[8,16,128]{2,1,0:T(8,128)S(1)} %shard_map.135), channel_id=1, replica_groups=mesh['ens'=2,'gy_0'=8,'gy_1'=8,'gy_2'=2] {'gy_0'}, dimensions={0} | all-to-all | bytes 131072 | tf_op jit(solution)/shard_map/all_to_all | solution.py:491
  78.6 3.0 %shard_map.136 = (f32[3,130,8,128]{3,2,1,0:T(8,128)S(1)}, f32[2,128,8,128]{3,2,1,0:T(8,128)S(1)}, f32[1,128]{1,0:T(1,128)S(1)}, f32[8,128]{1,0:T(8,128)S(1)}) custom-call(f32[8,16,128]{2,1,0:T(8,128)S(1)} %all_to_all.28.parts, f32[16,128]{1,0:T(8,128)S(1)} %get-tuple-element.41.kept, f32[16,16,64]{2,1,0:T(8,128)S(1)} %bitcast.20, ...), custom_call_target="tpu_custom_call" | custom-call | tf_op jit(solution)/shard_map/pallas_call | solution.py:479
  81.6 1.1 %collective-permute-start.2 = (f32[1,128]{1,0:T(1,128)S(1)}, f32[1,128]{1,0:T(1,128)S(1)}, u32[]{:S(2)}, u32[]{:S(2)}) collective-permute-start(f32[1,128]{1,0:T(1,128)S(1)} %get-tuple-element.49.mine), channel_id=1, source_target_pairs={{0,1},{1,0},{2,3},{3,2},{4,5},{5,4},{6,7},{7,6},{8,9},{9,8},{10,11... | collective-permute-start | bytes 1544 | tf_op jit(solution)/shard_map/ppermute | solution.py:534
  82.7 0.8 collective-permute-done.2.mates
  83.5 15.5 %all_to_all.29.parts = f32[64,1,128]{2,1,0:T(1,128)S(1)} all-to-all(f32[64,1,128]{2,1,0:T(1,128)S(1)} %shard_map.137), channel_id=1, replica_groups=mesh['ens'=2,'gy_0'=8,'gy_1'=8,'gy_2'=2] {'gy_0','gy_1'}, dimensions={0} | all-to-all | bytes 65536 | tf_op jit(solution)/shard_map/all_to_all | solution.py:536
  99.0 1.7 %shard_map.138 = (f32[2,128,8,128]{3,2,1,0:T(8,128)}, f32[2,128,8,128]{3,2,1,0:T(8,128)}) custom-call(f32[64,1,128]{2,1,0:T(1,128)S(1)} %all_to_all.29.parts, f32[8,128]{1,0:T(8,128)S(1)} %get-tuple-element.50.scalars, f32[2,128,8,128]{3,2,1,0:T(8,128)S(1)} %get-tuple-element.42.forcing, f32[3,130,8,128]{3,2,1,0:T(8,128)S(1)} %get-tuple-element.51.z_first, ...), custom_call_target="tpu_custom_call" | custom-call | tf_op jit(solution)/shard_map/pallas_call | solution.py:479
  (3 shorter events, 0.1 us)
Async XLA Ops:
  3.3 46.5 %copy-start = (f32[64,16,16]{0,2,1:T(8,128)S(1)}, f32[64,16,16]{0,2,1:T(8,128)}, u32[]{:S(2)}) copy-start(f32[64,16,16]{0,2,1:T(8,128)} %param.16) | copy-start | bytes 196612
  7.1 42.7 %collective-permute-start = (f32[6,128,1,128]{3,2,1,0:T(1,128)S(1)}, f32[6,128,1,128]{3,2,1,0:T(1,128)S(1)}, u32[]{:S(2)}, u32[]{:S(2)}) collective-permute-start(f32[6,128,1,128]{3,2,1,0:T(1,128)S(1)} %get-tuple-element.33), channel_id=1, source_target_pairs={{0,1},{1,0},{2,3},{3,2},{4,5},{5,4},{6,7},{7,6},{8,9},{9,8},{10,11... | collective-permute-start | bytes 1179656 | tf_op jit(solution)/shard_map/ppermute | solution.py:515
  27.6 22.2 %collective-permute-start.1 = (f32[6,128,1,128]{3,2,1,0:T(1,128)S(1)}, f32[6,128,1,128]{3,2,1,0:T(1,128)S(1)}, u32[]{:S(2)}, u32[]{:S(2)}) collective-permute-start(f32[6,128,1,128]{3,2,1,0:T(1,128)S(1)} %get-tuple-element.34), channel_id=1, source_target_pairs={{1,2},{2,1},{3,4},{4,3},{5,6},{6,5},{7,8},{8,7},{9,10},{10,9},{11,... | collective-permute-start | bytes 1179656 | tf_op jit(solution)/shard_map/ppermute | solution.py:516
  81.6 1.9 %collective-permute-start.2 = (f32[1,128]{1,0:T(1,128)S(1)}, f32[1,128]{1,0:T(1,128)S(1)}, u32[]{:S(2)}, u32[]{:S(2)}) collective-permute-start(f32[1,128]{1,0:T(1,128)S(1)} %get-tuple-element.49.mine), channel_id=1, source_target_pairs={{0,1},{1,0},{2,3},{3,2},{4,5},{5,4},{6,7},{7,6},{8,9},{9,8},{10,11... | collective-permute-start | bytes 1544 | tf_op jit(solution)/shard_map/ppermute | solution.py:534

commit v8 on v7

--- a/solution.py
+++ b/solution.py
@@ -18,6 +18,7 @@
 BLOCK = 32
 GROUPS = 4
 HALVES = 2
+EIGHTHS = 8
 VMEM_LIMIT = 24 * 2**20
 
 
@@ -130,6 +131,16 @@
     out[...] = jnp.broadcast_to(jnp.sum(parts[...], axis=0)[None], out.shape)
 
 
+def two_sums(left, right):
+    left, right = [x + pltpu.roll(x, TILE, 1) for x in (left, right)]
+    return jnp.sum(jnp.where(iota((8, 128), 1) < TILE, left, right), axis=0, keepdims=True)
+
+
+def sums_of(row):
+    left = iota(row.shape, 1) < TILE
+    return [jnp.sum(jnp.where(x, row, 0.0), axis=1, keepdims=True) for x in (left, jnp.logical_not(left))]
+
+
 def scalar_rows(values):
     tile = jnp.zeros((8, 128), F32)
     for k, value in enumerate(values):
@@ -176,7 +187,7 @@
         copy.start()
     loads = Loads([(forcing, field)], sems, chunks, HALVES)
     loads.start()
-    for copy in copies:
+    for copy in copies[:4]:
         copy.wait()
     for k in range(3):
         row = pl.ds(jnp.maximum(tile_rows[k], 0), 1)
@@ -185,6 +196,8 @@
     expand(codes_o, codes)
     tile = moments(field, codes, gather_o, lanes_o, loads)
     sums_o[...] = jnp.broadcast_to(tile[None], sums_o.shape)
+    for copy in copies[4:]:
+        copy.wait()
 
 
 def faces_kernel(codes_small, forcing, east, north, storage, east_o, north_h, center_h, mate_o, other_o,
@@ -269,7 +282,7 @@
     chunks = z_pad.shape[1] - 2
     z_pad[:, 0] = z_pad[:, chunks]
     z_pad[:, chunks + 1] = z_pad[:, 1]
-    n = PIECE
+    n = PIECE if blocks == 3 else 2 * PIECE
     sub, lane = iota((n, 8, 128), 1), iota((n, 8, 128), 2)
 
     def step(k, total):
@@ -318,7 +331,7 @@
                   field, north, center, z_pad, image_o, sums_o, kept_o, jacobi_o, end_f, end_n,
                   codes, end_e, end_c, columns, sems):
     chunks = forcing.shape[1]
-    loads = Loads([(forcing, field), (north_h, north), (center_h, center)], sems, chunks)
+    loads = Loads([(forcing, field), (north_h, north), (center_h, center)], sems, chunks, EIGHTHS)
     loads.start()
     expand(codes_small, codes)
     tile = jnp.sum(parts[...], axis=0)
@@ -358,35 +371,36 @@
             z_pad[r, c + 1] = smooth[r] + added[r]
         return total + (field[0, c] * smooth[0] + field[1, c] * smooth[1])
 
-    size = chunks // GROUPS // ROWS
+    rows_a_step = chunks // EIGHTHS
 
     def step(k, total):
-        @pl.when(lax.rem(k, size) == 0)
-        def _():
-            loads.wait(lax.div(k, size))
-
-        for j in range(ROWS):
-            total = chunk(k * ROWS + j, total)
+        loads.wait(k)
+        for j in range(rows_a_step):
+            total = chunk(k * rows_a_step + j, total)
         return total
 
-    smooth_total = lax.fori_loop(0, chunks // ROWS, step, jnp.zeros((8, 128), F32))
+    smooth_total = lax.fori_loop(0, EIGHTHS, step, jnp.zeros((8, 128), F32))
     end_e[0] = end_e[chunks]
     faces = (chooser(east.at[0], east.at[1], end_e), chooser(north.at[0], north.at[1], end_n),
              chooser(center.at[0], center.at[1], end_c))
     image_total = apply_operator(z_pad, faces, 3, image_o)
     tile = moments(image_o, codes, gather, lanes)
-    scalars = scalar_rows([jnp.sum(smooth_total, axis=0, keepdims=True), jnp.sum(image_total, axis=0, keepdims=True)])
-    sums_o[...] = jnp.broadcast_to(jnp.concatenate([tile, scalars], axis=0)[None], sums_o.shape)
+    for k in range(9):
+        row = tile[k : k + 1] if k < 8 else two_sums(smooth_total, image_total)
+        sums_o[:, k] = jnp.broadcast_to(row[None], (sums_o.shape[0], 1, 128))
 
 
 def third_kernel(parts, kept, inverse, forcing, image, codes_small, scatter, patterns, east, north, center,
-                 jacobi, end_f, end_n, z_pad, image_o, sums_o, scalars_o, codes, columns):
+                 jacobi, end_f, end_n, z_pad, image_o, sums_o, scalars_o, codes, columns, tile):
     chunks = forcing.shape[1]
     expand(codes_small, codes)
-    tile = jnp.sum(parts[...], axis=0)
-    energy = jnp.sum(tile[8:9], axis=1, keepdims=True) + kept[8:9, 0:1]
-    alpha = energy / jnp.sum(tile[9:10], axis=1, keepdims=True)
-    sums = unpack(kept[0:8] - alpha * tile[0:8])
+    rows = jnp.sum(parts[...], axis=0)
+    for k in range(8):
+        tile[k : k + 1] = rows[k]
+    energy, image_energy = sums_of(rows[8])
+    energy = energy + kept[8:9, 0:1]
+    alpha = energy / image_energy
+    sums = unpack(kept[0:8] - alpha * tile[...])
     coef = coarse_solve(inverse, sums)
     scalars_o[...] = scalar_rows([alpha, energy, total_of(sums * coef)])
     column_tables(coef, codes, scatter, columns)
@@ -412,9 +426,7 @@
     smooth_total = lax.fori_loop(0, chunks // ROWS, step, jnp.zeros((8, 128), F32))
     faces = (chooser(east.at[0], east.at[1]), chooser(north.at[0], north.at[1], end_n), chooser(center.at[0], center.at[1]))
     image_total = apply_operator(z_pad, faces, 2, image_o)
-    smooth_row, image_row = [x + pltpu.roll(x, TILE, 1) for x in (smooth_total, image_total)]
-    packed = jnp.where(iota((8, 128), 1) < TILE, smooth_row, image_row)
-    sums_o[...] = jnp.sum(packed, axis=0, keepdims=True)
+    sums_o[...] = two_sums(smooth_total, image_total)
 
 
 def pair_kernel(mine, mates, out):
@@ -425,12 +437,11 @@
                 solution_v, residual_v, out_sems):
     chunks = forcing.shape[1]
     saves = Loads([(solution_v, solution_o), (residual_v, residual_o)], out_sems, chunks)
-    row = jnp.sum(parts[...], axis=0)
-    left = iota(row.shape, 1) < TILE
+    energy_next, image_energy = sums_of(jnp.sum(parts[...], axis=0))
     alpha, energy = scalars[0:1, 0:1], scalars[1:2, 0:1]
-    energy_next = jnp.sum(jnp.where(left, row, 0.0), axis=1, keepdims=True) + scalars[2:3, 0:1]
+    energy_next = energy_next + scalars[2:3, 0:1]
     beta = energy_next / energy
-    alpha_next = energy_next / (jnp.sum(jnp.where(left, 0.0, row), axis=1, keepdims=True) - beta * energy_next / alpha)
+    alpha_next = energy_next / (image_energy - beta * energy_next / alpha)
     alpha, beta, alpha_next = [x.reshape(1, 1, 1) for x in (alpha, beta, alpha_next)]
     per_group = chunks // GROUPS // PIECE
 
@@ -516,11 +527,11 @@
     other = lax.ppermute(other, GY, others)
     field, north, center, z_first, image_first, sums, kept, jacobi, end_f, end_n = call(
         second_kernel,
-        [("V", own_shape, F32)] * 3 + [("V", pad_shape, F32), ("V", all_shape, F32), ("V", (inner, 16, 128), F32), ("V", (16, 128), F32),
+        [("V", own_shape, F32)] * 3 + [("V", pad_shape, F32), ("V", all_shape, F32), ("V", (inner, 9, 1, 128), F32), ("V", (16, 128), F32),
          ("V", all_shape, F32), ("V", end_shape, F32), ("V", end_shape, F32)],
         ("V", [parts]), ("H", [forcing, north, center]),
         ("V", [mate, other, inverse, codes, gather, scatter, lanes, patterns, east]),
-        scratch=(codes_v, pltpu.VMEM((chunks + 1, 8, 128), F32), pltpu.VMEM(end_shape, F32), columns, dma(3, GROUPS)),
+        scratch=(codes_v, pltpu.VMEM((chunks + 1, 8, 128), F32), pltpu.VMEM(end_shape, F32), columns, dma(3, EIGHTHS)),
     )
     parts = everywhere(sums)
     z_second, image_second, sums, scalars = call(
@@ -528,7 +539,7 @@
         [("V", pad_shape, F32), ("V", own_shape, F32), ("V", (1, 128), F32), ("V", (8, 128), F32)],
         ("V", [parts]),
         ("V", [kept, inverse, field, image_first, codes, scatter, patterns, east, north, center, jacobi, end_f, end_n]),
-        scratch=(codes_v, columns),
+        scratch=(codes_v, columns, pltpu.VMEM((8, 128), F32)),
     )
     chips = lax.axis_size(GY[:2])
     swapped = lax.ppermute(sums, GY[2], [(0, 1), (1, 0)])

time: 101 us -> 100 us (0.990)
  blocking collectives: 59.2 us -> 57.6 us
where the time goes in v8:
time: 100 us; the launch traced here: 99.7 us
  blocking collectives  57.6 us (58%)
  starting transfers between devices  23.8 us (24%)
  Pallas kernels  16.8 us (17%)
    all_to_all x2, blocking collectives, everywhere(): near = lax.all_to_all(copies, GY[1:], 0, 0)  23.4 us
    ppermute x1, starting transfers between devices, body(): mate = lax.ppermute(mate, GY, mates)  20.5 us
    all_to_all x2, blocking collectives, everywhere(): return lax.all_to_all(copies, GY[0], 0, 0)  18.6 us
    pallas_call x8, Pallas kernels, call(): pl.pallas_call(kernel, out_shape=[kept_in[k](s, d) if k in kept_in else j...  16.8 us
    all_to_all x1, blocking collectives, body(): parts = lax.all_to_all(sums, GY[:2], 0, 0)  15.5 us
  transfers between devices with their start and end apart: 3, of which 1 were waited for; matrix products, arithmetic and copies ran while one was open for 0% of the time, Pallas kernels for 0%

profile of v8, /device:TPU:513, one launch (start us, length us, event | category | flops | bytes accessed | tf_op | source)
XLA Modules:
  0.0 99.7 jit_solution(801168095956129016)
XLA Ops:
  0.6 2.7 %shard_map.131 = (f32[16,8,128]{2,1,0:T(8,128)S(1)}, f32[8,256]{1,0:T(8,128)S(1)}, bf16[64,256]{1,0:T(8,128)(2,1)S(1)}, bf16[128,128]{1,0:T(8,128)(2,1)S(1)}, f3...) custom-call(f32[2,128,8,128]{3,2,1,0:T(8,128)} %bitcast.21, s32[32,256]{1,0:T(8,128)} %membership.1, ...), custom_call_target="tpu_custom_call" | custom-call | tf_op jit(solution)/shard_map/pallas_call | solution.py:490
  3.3 0.0 copy-start
  3.3 3.7 %shard_map.133 = (f32[2,129,8,128]{3,2,1,0:T(8,128)S(1)}, f32[2,128,8,128]{3,2,1,0:T(8,128)}, f32[2,128,8,128]{3,2,1,0:T(8,128)}, f32[6,128,1,128]{3,2,1,0:T(1,128)S(1)}, f32[6,128,1,128]{3,2,1,0:T(1,128)S(1)}) custom-call(f32[8,256]{1,0:T(8,128)S(1)} %get-tuple-element.30.codes_small, f32[2,128,8,128]{3,2,1,0:T(8,128)} %bitcast.22, ...), custom_call_target="tpu_custom_call" | custom-call | tf_op jit(solution)/shard_map/pallas_call | solution.py:490
  7.0 20.5 %collective-permute-start = (f32[6,128,1,128]{3,2,1,0:T(1,128)S(1)}, f32[6,128,1,128]{3,2,1,0:T(1,128)S(1)}, u32[]{:S(2)}, u32[]{:S(2)}) collective-permute-start(f32[6,128,1,128]{3,2,1,0:T(1,128)S(1)} %get-tuple-element.33), channel_id=1, source_target_pairs={{0,1},{1,0},{2,3},{3,2},{4,5},{5,4},{6,7},{7,6},{8,9},{9,8},{10,11... | collective-permute-start | bytes 1179656 | tf_op jit(solution)/shard_map/ppermute | solution.py:526
  27.6 1.9 %collective-permute-start.1 = (f32[6,128,1,128]{3,2,1,0:T(1,128)S(1)}, f32[6,128,1,128]{3,2,1,0:T(1,128)S(1)}, u32[]{:S(2)}, u32[]{:S(2)}) collective-permute-start(f32[6,128,1,128]{3,2,1,0:T(1,128)S(1)} %get-tuple-element.34), channel_id=1, source_target_pairs={{1,2},{2,1},{3,4},{4,3},{5,6},{6,5},{7,8},{8,7},{9,10},{10,9},{11,... | collective-permute-start | bytes 1179656 | tf_op jit(solution)/shard_map/ppermute | solution.py:527
  29.5 10.9 %all_to_all.25.parts = f32[16,8,128]{2,1,0:T(8,128)S(1)} all-to-all(f32[16,8,128]{2,1,0:T(8,128)S(1)} %get-tuple-element.29), channel_id=1, replica_groups=mesh['ens'=2,'gy_0'=8,'gy_1'=8,'gy_2'=2] {'gy_1','gy_2'}, dimensions={0} | all-to-all | bytes 131072 | tf_op jit(solution)/shard_map/all_to_all | solution.py:500
  40.4 9.3 %all_to_all.26.parts = f32[8,8,128]{2,1,0:T(8,128)S(1)} all-to-all(f32[8,8,128]{2,1,0:T(8,128)S(1)} %shard_map.132), channel_id=1, replica_groups=mesh['ens'=2,'gy_0'=8,'gy_1'=8,'gy_2'=2] {'gy_0'}, dimensions={0} | all-to-all | bytes 65536 | tf_op jit(solution)/shard_map/all_to_all | solution.py:502
  49.7 0.0 collective-permute-done.mate
  49.7 0.0 collective-permute-done.1.other
  49.8 0.0 copy-done
  49.8 5.6 %shard_map.134 = (f32[2,128,8,128]{3,2,1,0:T(8,128)S(1)}, f32[2,128,8,128]{3,2,1,0:T(8,128)S(1)}, f32[2,128,8,128]{3,2,1,0:T(8,128)S(1)}, f32[3,130,8,128]{3,2,1...) custom-call(f32[8,8,128]{2,1,0:T(8,128)S(1)} %all_to_all.26.parts, ...), custom_call_target="tpu_custom_call" | custom-call | tf_op jit(solution)/shard_map/pallas_call | solution.py:490
  55.4 12.5 %all_to_all.27.parts = f32[16,9,1,128]{3,2,1,0:T(1,128)S(1)} all-to-all(f32[16,9,1,128]{3,2,1,0:T(1,128)S(1)} %get-tuple-element.40), channel_id=1, replica_groups=mesh['ens'=2,'gy_0'=8,'gy_1'=8,'gy_2'=2] {'gy_1','gy_2'}, dimensions={0} | all-to-all | bytes 147456 | tf_op jit(solution)/shard_map/all_to_all | solution.py:500
  67.9 0.1 shard_map.135
  67.9 9.3 %all_to_all.28.parts = f32[8,9,1,128]{3,2,1,0:T(1,128)S(1)} all-to-all(f32[8,9,1,128]{3,2,1,0:T(1,128)S(1)} %shard_map.135), channel_id=1, replica_groups=mesh['ens'=2,'gy_0'=8,'gy_1'=8,'gy_2'=2] {'gy_0'}, dimensions={0} | all-to-all | bytes 73728 | tf_op jit(solution)/shard_map/all_to_all | solution.py:502
  77.3 3.0 %shard_map.136 = (f32[3,130,8,128]{3,2,1,0:T(8,128)S(1)}, f32[2,128,8,128]{3,2,1,0:T(8,128)S(1)}, f32[1,128]{1,0:T(1,128)S(1)}, f32[8,128]{1,0:T(8,128)S(1)}) custom-call(f32[8,9,1,128]{3,2,1,0:T(1,128)S(1)} %all_to_all.28.parts, f32[16,128]{1,0:T(8,128)S(1)} %get-tuple-element.41.kept, f32[16,16,64]{2,1,0:T(8,128)S(1)} %bitcast.20, ...), custom_call_target="tpu_custom_call" | custom-call | tf_op jit(solution)/shard_map/pallas_call | solution.py:490
  80.2 1.4 %collective-permute-start.2 = (f32[1,128]{1,0:T(1,128)S(1)}, f32[1,128]{1,0:T(1,128)S(1)}, u32[]{:S(2)}, u32[]{:S(2)}) collective-permute-start(f32[1,128]{1,0:T(1,128)S(1)} %get-tuple-element.49.mine), channel_id=1, source_target_pairs={{0,1},{1,0},{2,3},{3,2},{4,5},{5,4},{6,7},{7,6},{8,9},{9,8},{10,11... | collective-permute-start | bytes 1544 | tf_op jit(solution)/shard_map/ppermute | solution.py:545
  81.6 0.8 collective-permute-done.2.mates
  82.4 15.5 %all_to_all.29.parts = f32[64,1,128]{2,1,0:T(1,128)S(1)} all-to-all(f32[64,1,128]{2,1,0:T(1,128)S(1)} %shard_map.137), channel_id=1, replica_groups=mesh['ens'=2,'gy_0'=8,'gy_1'=8,'gy_2'=2] {'gy_0','gy_1'}, dimensions={0} | all-to-all | bytes 65536 | tf_op jit(solution)/shard_map/all_to_all | solution.py:547
  98.0 1.8 %shard_map.138 = (f32[2,128,8,128]{3,2,1,0:T(8,128)}, f32[2,128,8,128]{3,2,1,0:T(8,128)}) custom-call(f32[64,1,128]{2,1,0:T(1,128)S(1)} %all_to_all.29.parts, f32[8,128]{1,0:T(8,128)S(1)} %get-tuple-element.50.scalars, f32[2,128,8,128]{3,2,1,0:T(8,128)S(1)} %get-tuple-element.42.forcing, f32[3,130,8,128]{3,2,1,0:T(8,128)S(1)} %get-tuple-element.51.z_first, ...), custom_call_target="tpu_custom_call" | custom-call | tf_op jit(solution)/shard_map/pallas_call | solution.py:490
  (2 shorter events, 0.0 us)
Async XLA Ops:
  3.3 46.5 %copy-start = (f32[64,16,16]{0,2,1:T(8,128)S(1)}, f32[64,16,16]{0,2,1:T(8,128)}, u32[]{:S(2)}) copy-start(f32[64,16,16]{0,2,1:T(8,128)} %param.16) | copy-start | bytes 196612
  7.0 42.7 %collective-permute-start = (f32[6,128,1,128]{3,2,1,0:T(1,128)S(1)}, f32[6,128,1,128]{3,2,1,0:T(1,128)S(1)}, u32[]{:S(2)}, u32[]{:S(2)}) collective-permute-start(f32[6,128,1,128]{3,2,1,0:T(1,128)S(1)} %get-tuple-element.33), channel_id=1, source_target_pairs={{0,1},{1,0},{2,3},{3,2},{4,5},{5,4},{6,7},{7,6},{8,9},{9,8},{10,11... | collective-permute-start | bytes 1179656 | tf_op jit(solution)/shard_map/ppermute | solution.py:526
  27.6 22.2 %collective-permute-start.1 = (f32[6,128,1,128]{3,2,1,0:T(1,128)S(1)}, f32[6,128,1,128]{3,2,1,0:T(1,128)S(1)}, u32[]{:S(2)}, u32[]{:S(2)}) collective-permute-start(f32[6,128,1,128]{3,2,1,0:T(1,128)S(1)} %get-tuple-element.34), channel_id=1, source_target_pairs={{1,2},{2,1},{3,4},{4,3},{5,6},{6,5},{7,8},{8,7},{9,10},{10,9},{11,... | collective-permute-start | bytes 1179656 | tf_op jit(solution)/shard_map/ppermute | solution.py:527
  80.2 2.2 %collective-permute-start.2 = (f32[1,128]{1,0:T(1,128)S(1)}, f32[1,128]{1,0:T(1,128)S(1)}, u32[]{:S(2)}, u32[]{:S(2)}) collective-permute-start(f32[1,128]{1,0:T(1,128)S(1)} %get-tuple-element.49.mine), channel_id=1, source_target_pairs={{0,1},{1,0},{2,3},{3,2},{4,5},{5,4},{6,7},{7,6},{8,9},{9,8},{10,11... | collective-permute-start | bytes 1544 | tf_op jit(solution)/shard_map/ppermute | solution.py:545

commit v9 on v8

--- a/solution.py
+++ b/solution.py
@@ -15,10 +15,9 @@
 F32, BF16, I32 = jnp.float32, jnp.bfloat16, jnp.int32
 ROWS = 32
 PIECE = 32
-BLOCK = 32
+BLOCK = 64
 GROUPS = 4
 HALVES = 2
-EIGHTHS = 8
 VMEM_LIMIT = 24 * 2**20
 
 
@@ -187,7 +186,7 @@
         copy.start()
     loads = Loads([(forcing, field)], sems, chunks, HALVES)
     loads.start()
-    for copy in copies[:4]:
+    for copy in copies:
         copy.wait()
     for k in range(3):
         row = pl.ds(jnp.maximum(tile_rows[k], 0), 1)
@@ -196,8 +195,6 @@
     expand(codes_o, codes)
     tile = moments(field, codes, gather_o, lanes_o, loads)
     sums_o[...] = jnp.broadcast_to(tile[None], sums_o.shape)
-    for copy in copies[4:]:
-        copy.wait()
 
 
 def faces_kernel(codes_small, forcing, east, north, storage, east_o, north_h, center_h, mate_o, other_o,
@@ -282,7 +279,7 @@
     chunks = z_pad.shape[1] - 2
     z_pad[:, 0] = z_pad[:, chunks]
     z_pad[:, chunks + 1] = z_pad[:, 1]
-    n = PIECE if blocks == 3 else 2 * PIECE
+    n = PIECE
     sub, lane = iota((n, 8, 128), 1), iota((n, 8, 128), 2)
 
     def step(k, total):
@@ -331,7 +328,7 @@
                   field, north, center, z_pad, image_o, sums_o, kept_o, jacobi_o, end_f, end_n,
                   codes, end_e, end_c, columns, sems):
     chunks = forcing.shape[1]
-    loads = Loads([(forcing, field), (north_h, north), (center_h, center)], sems, chunks, EIGHTHS)
+    loads = Loads([(forcing, field), (north_h, north), (center_h, center)], sems, chunks)
     loads.start()
     expand(codes_small, codes)
     tile = jnp.sum(parts[...], axis=0)
@@ -371,15 +368,18 @@
             z_pad[r, c + 1] = smooth[r] + added[r]
         return total + (field[0, c] * smooth[0] + field[1, c] * smooth[1])
 
-    rows_a_step = chunks // EIGHTHS
+    size = chunks // GROUPS // ROWS
 
     def step(k, total):
-        loads.wait(k)
-        for j in range(rows_a_step):
-            total = chunk(k * rows_a_step + j, total)
+        @pl.when(lax.rem(k, size) == 0)
+        def _():
+            loads.wait(lax.div(k, size))
+
+        for j in range(ROWS):
+            total = chunk(k * ROWS + j, total)
         return total
 
-    smooth_total = lax.fori_loop(0, EIGHTHS, step, jnp.zeros((8, 128), F32))
+    smooth_total = lax.fori_loop(0, chunks // ROWS, step, jnp.zeros((8, 128), F32))
     end_e[0] = end_e[chunks]
     faces = (chooser(east.at[0], east.at[1], end_e), chooser(north.at[0], north.at[1], end_n),
              chooser(center.at[0], center.at[1], end_c))
@@ -531,7 +531,7 @@
          ("V", all_shape, F32), ("V", end_shape, F32), ("V", end_shape, F32)],
         ("V", [parts]), ("H", [forcing, north, center]),
         ("V", [mate, other, inverse, codes, gather, scatter, lanes, patterns, east]),
-        scratch=(codes_v, pltpu.VMEM((chunks + 1, 8, 128), F32), pltpu.VMEM(end_shape, F32), columns, dma(3, EIGHTHS)),
+        scratch=(codes_v, pltpu.VMEM((chunks + 1, 8, 128), F32), pltpu.VMEM(end_shape, F32), columns, dma(3, GROUPS)),
     )
     parts = everywhere(sums)
     z_second, image_second, sums, scalars = call(

time: 100 us -> 99.6 us (level)
  no operation moved by 1% of the time
where the time goes in v9:
time: 99.6 us; the launch traced here: 99.3 us
  blocking collectives  57.6 us (58%)
  starting transfers between devices  23.8 us (24%)
  Pallas kernels  16.3 us (16%)
    all_to_all x2, blocking collectives, everywhere(): near = lax.all_to_all(copies, GY[1:], 0, 0)  23.4 us
    ppermute x1, starting transfers between devices, body(): mate = lax.ppermute(mate, GY, mates)  20.5 us
    all_to_all x2, blocking collectives, everywhere(): return lax.all_to_all(copies, GY[0], 0, 0)  18.6 us
    pallas_call x8, Pallas kernels, call(): pl.pallas_call(kernel, out_shape=[kept_in[k](s, d) if k in kept_in else j...  16.3 us
    all_to_all x1, blocking collectives, body(): parts = lax.all_to_all(sums, GY[:2], 0, 0)  15.5 us
  transfers between devices with their start and end apart: 3, of which 1 were waited for; matrix products, arithmetic and copies ran while one was open for 0% of the time, Pallas kernels for 0%

profile of v9, /device:TPU:513, one launch (start us, length us, event | category | flops | bytes accessed | tf_op | source)
XLA Modules:
  0.0 99.3 jit_solution(10762141567000951438)
XLA Ops:
  0.6 2.5 %shard_map.131 = (f32[16,8,128]{2,1,0:T(8,128)S(1)}, f32[8,256]{1,0:T(8,128)S(1)}, bf16[64,256]{1,0:T(8,128)(2,1)S(1)}, bf16[128,128]{1,0:T(8,128)(2,1)S(1)}, f3...) custom-call(f32[2,128,8,128]{3,2,1,0:T(8,128)} %bitcast.21, s32[32,256]{1,0:T(8,128)} %membership.1, ...), custom_call_target="tpu_custom_call" | custom-call | tf_op jit(solution)/shard_map/pallas_call | solution.py:490
  3.1 0.0 copy-start
  3.1 3.7 %shard_map.133 = (f32[2,129,8,128]{3,2,1,0:T(8,128)S(1)}, f32[2,128,8,128]{3,2,1,0:T(8,128)}, f32[2,128,8,128]{3,2,1,0:T(8,128)}, f32[6,128,1,128]{3,2,1,0:T(1,128)S(1)}, f32[6,128,1,128]{3,2,1,0:T(1,128)S(1)}) custom-call(f32[8,256]{1,0:T(8,128)S(1)} %get-tuple-element.30.codes_small, f32[2,128,8,128]{3,2,1,0:T(8,128)} %bitcast.22, ...), custom_call_target="tpu_custom_call" | custom-call | tf_op jit(solution)/shard_map/pallas_call | solution.py:490
  6.9 20.5 %collective-permute-start = (f32[6,128,1,128]{3,2,1,0:T(1,128)S(1)}, f32[6,128,1,128]{3,2,1,0:T(1,128)S(1)}, u32[]{:S(2)}, u32[]{:S(2)}) collective-permute-start(f32[6,128,1,128]{3,2,1,0:T(1,128)S(1)} %get-tuple-element.33), channel_id=1, source_target_pairs={{0,1},{1,0},{2,3},{3,2},{4,5},{5,4},{6,7},{7,6},{8,9},{9,8},{10,11... | collective-permute-start | bytes 1179656 | tf_op jit(solution)/shard_map/ppermute | solution.py:526
  27.4 1.9 %collective-permute-start.1 = (f32[6,128,1,128]{3,2,1,0:T(1,128)S(1)}, f32[6,128,1,128]{3,2,1,0:T(1,128)S(1)}, u32[]{:S(2)}, u32[]{:S(2)}) collective-permute-start(f32[6,128,1,128]{3,2,1,0:T(1,128)S(1)} %get-tuple-element.34), channel_id=1, source_target_pairs={{1,2},{2,1},{3,4},{4,3},{5,6},{6,5},{7,8},{8,7},{9,10},{10,9},{11,... | collective-permute-start | bytes 1179656 | tf_op jit(solution)/shard_map/ppermute | solution.py:527
  29.3 10.9 %all_to_all.25.parts = f32[16,8,128]{2,1,0:T(8,128)S(1)} all-to-all(f32[16,8,128]{2,1,0:T(8,128)S(1)} %get-tuple-element.29), channel_id=1, replica_groups=mesh['ens'=2,'gy_0'=8,'gy_1'=8,'gy_2'=2] {'gy_1','gy_2'}, dimensions={0} | all-to-all | bytes 131072 | tf_op jit(solution)/shard_map/all_to_all | solution.py:500
  40.3 9.3 %all_to_all.26.parts = f32[8,8,128]{2,1,0:T(8,128)S(1)} all-to-all(f32[8,8,128]{2,1,0:T(8,128)S(1)} %shard_map.132), channel_id=1, replica_groups=mesh['ens'=2,'gy_0'=8,'gy_1'=8,'gy_2'=2] {'gy_0'}, dimensions={0} | all-to-all | bytes 65536 | tf_op jit(solution)/shard_map/all_to_all | solution.py:502
  49.6 0.0 collective-permute-done.mate
  49.6 0.0 collective-permute-done.1.other
  49.6 0.0 copy-done
  49.6 5.2 %shard_map.134 = (f32[2,128,8,128]{3,2,1,0:T(8,128)S(1)}, f32[2,128,8,128]{3,2,1,0:T(8,128)S(1)}, f32[2,128,8,128]{3,2,1,0:T(8,128)S(1)}, f32[3,130,8,128]{3,2,1...) custom-call(f32[8,8,128]{2,1,0:T(8,128)S(1)} %all_to_all.26.parts, ...), custom_call_target="tpu_custom_call" | custom-call | tf_op jit(solution)/shard_map/pallas_call | solution.py:490
  54.8 12.5 %all_to_all.27.parts = f32[16,9,1,128]{3,2,1,0:T(1,128)S(1)} all-to-all(f32[16,9,1,128]{3,2,1,0:T(1,128)S(1)} %get-tuple-element.40), channel_id=1, replica_groups=mesh['ens'=2,'gy_0'=8,'gy_1'=8,'gy_2'=2] {'gy_1','gy_2'}, dimensions={0} | all-to-all | bytes 147456 | tf_op jit(solution)/shard_map/all_to_all | solution.py:500
  67.4 0.1 shard_map.135
  67.4 9.3 %all_to_all.28.parts = f32[8,9,1,128]{3,2,1,0:T(1,128)S(1)} all-to-all(f32[8,9,1,128]{3,2,1,0:T(1,128)S(1)} %shard_map.135), channel_id=1, replica_groups=mesh['ens'=2,'gy_0'=8,'gy_1'=8,'gy_2'=2] {'gy_0'}, dimensions={0} | all-to-all | bytes 73728 | tf_op jit(solution)/shard_map/all_to_all | solution.py:502
  76.7 3.0 %shard_map.136 = (f32[3,130,8,128]{3,2,1,0:T(8,128)S(1)}, f32[2,128,8,128]{3,2,1,0:T(8,128)S(1)}, f32[1,128]{1,0:T(1,128)S(1)}, f32[8,128]{1,0:T(8,128)S(1)}) custom-call(f32[8,9,1,128]{3,2,1,0:T(1,128)S(1)} %all_to_all.28.parts, f32[16,128]{1,0:T(8,128)S(1)} %get-tuple-element.41.kept, f32[16,16,64]{2,1,0:T(8,128)S(1)} %bitcast.20, ...), custom_call_target="tpu_custom_call" | custom-call | tf_op jit(solution)/shard_map/pallas_call | solution.py:490
  79.7 1.4 %collective-permute-start.2 = (f32[1,128]{1,0:T(1,128)S(1)}, f32[1,128]{1,0:T(1,128)S(1)}, u32[]{:S(2)}, u32[]{:S(2)}) collective-permute-start(f32[1,128]{1,0:T(1,128)S(1)} %get-tuple-element.49.mine), channel_id=1, source_target_pairs={{0,1},{1,0},{2,3},{3,2},{4,5},{5,4},{6,7},{7,6},{8,9},{9,8},{10,11... | collective-permute-start | bytes 1544 | tf_op jit(solution)/shard_map/ppermute | solution.py:545
  81.1 0.8 collective-permute-done.2.mates
  81.9 15.5 %all_to_all.29.parts = f32[64,1,128]{2,1,0:T(1,128)S(1)} all-to-all(f32[64,1,128]{2,1,0:T(1,128)S(1)} %shard_map.137), channel_id=1, replica_groups=mesh['ens'=2,'gy_0'=8,'gy_1'=8,'gy_2'=2] {'gy_0','gy_1'}, dimensions={0} | all-to-all | bytes 65536 | tf_op jit(solution)/shard_map/all_to_all | solution.py:547
  97.5 1.8 %shard_map.138 = (f32[2,128,8,128]{3,2,1,0:T(8,128)}, f32[2,128,8,128]{3,2,1,0:T(8,128)}) custom-call(f32[64,1,128]{2,1,0:T(1,128)S(1)} %all_to_all.29.parts, f32[8,128]{1,0:T(8,128)S(1)} %get-tuple-element.50.scalars, f32[2,128,8,128]{3,2,1,0:T(8,128)S(1)} %get-tuple-element.42.forcing, f32[3,130,8,128]{3,2,1,0:T(8,128)S(1)} %get-tuple-element.51.z_first, ...), custom_call_target="tpu_custom_call" | custom-call | tf_op jit(solution)/shard_map/pallas_call | solution.py:490
  (2 shorter events, 0.0 us)
Async XLA Ops:
  3.1 46.5 %copy-start = (f32[64,16,16]{0,2,1:T(8,128)S(1)}, f32[64,16,16]{0,2,1:T(8,128)}, u32[]{:S(2)}) copy-start(f32[64,16,16]{0,2,1:T(8,128)} %param.16) | copy-start | bytes 196612
  6.9 42.7 %collective-permute-start = (f32[6,128,1,128]{3,2,1,0:T(1,128)S(1)}, f32[6,128,1,128]{3,2,1,0:T(1,128)S(1)}, u32[]{:S(2)}, u32[]{:S(2)}) collective-permute-start(f32[6,128,1,128]{3,2,1,0:T(1,128)S(1)} %get-tuple-element.33), channel_id=1, source_target_pairs={{0,1},{1,0},{2,3},{3,2},{4,5},{5,4},{6,7},{7,6},{8,9},{9,8},{10,11... | collective-permute-start | bytes 1179656 | tf_op jit(solution)/shard_map/ppermute | solution.py:526
  27.4 22.2 %collective-permute-start.1 = (f32[6,128,1,128]{3,2,1,0:T(1,128)S(1)}, f32[6,128,1,128]{3,2,1,0:T(1,128)S(1)}, u32[]{:S(2)}, u32[]{:S(2)}) collective-permute-start(f32[6,128,1,128]{3,2,1,0:T(1,128)S(1)} %get-tuple-element.34), channel_id=1, source_target_pairs={{1,2},{2,1},{3,4},{4,3},{5,6},{6,5},{7,8},{8,7},{9,10},{10,9},{11,... | collective-permute-start | bytes 1179656 | tf_op jit(solution)/shard_map/ppermute | solution.py:527
  79.7 2.2 %collective-permute-start.2 = (f32[1,128]{1,0:T(1,128)S(1)}, f32[1,128]{1,0:T(1,128)S(1)}, u32[]{:S(2)}, u32[]{:S(2)}) collective-permute-start(f32[1,128]{1,0:T(1,128)S(1)} %get-tuple-element.49.mine), channel_id=1, source_target_pairs={{0,1},{1,0},{2,3},{3,2},{4,5},{5,4},{6,7},{7,6},{8,9},{9,8},{10,11... | collective-permute-start | bytes 1544 | tf_op jit(solution)/shard_map/ppermute | solution.py:545
